TPU v7x, 512 devices: a whole 4x8x8 slice. The times are simulated.
512 devices in a mesh: gx: 8 (over z_hi, core), gyz: 64 (over y, x, z_lo).
Axes of the slice: x: 4, y: 8, z: 8 (z_hi: 4, z_lo: 2; z = z_hi * 2 + z_lo), core: 2. Of those that a mesh axis runs over, the one named last changes fastest.
Arguments:
- bands: bfloat16 [64, 320, 40, 512], P('gx', 'gyz'), may hold values from -16 to 16
- potential: float32 [64, 320, 40], P('gx', 'gyz'), may hold values from 0.5 to 4
- eigenvectors: bfloat16 [512, 512], P('gyz'), may hold values from -0.25 to 0.25
Outputs:
- correlation: float32 [512, 512], P('gyz')
- hamiltonian: float32 [512, 512], P('gyz')
- rotated: bfloat16 [64, 320, 40, 512], P('gx', 'gyz')
All inputs are finite; a program needn't handle non-finite values.
Results may differ from a plain program's by a relative error of at most 0.0012.
Values may be sent and summed in bfloat16 or wider, within the bound.
No kernel may reach another device: no remote copies, remote signals or barrier semaphores. Data moves between devices by JAX's collectives and lax.ppermute only.
A program may use at most 64 MiB of HBM per device.

v0:
```python
import jax
import jax.numpy as jnp
from jax import lax
from jax.sharding import PartitionSpec as P


def extended(x, sides, width):
    edges = {}
    for axis, dim in sides:
        count, length = (lax.axis_size(axis), x.shape[dim])
        up = [(i, (i + 1) % count) for i in range(count - 1)]
        last = lax.slice_in_dim(x, length - width, length, axis=dim)
        leading = lax.slice_in_dim(x, 0, width, axis=dim)
        edges[dim] = (
            lax.ppermute(last, axis, up),
            lax.ppermute(leading, axis, [(b, a) for a, b in up]),
        )
    done = []
    for _, dim in sides:
        low, high = edges[dim]
        around = [(width, width) if d in done else (0, 0) for d in range(x.ndim)]
        x = jnp.concatenate([jnp.pad(low, around), x, jnp.pad(high, around)], axis=dim)
        done.append(dim)
    return x


def split_up(x, dim, count):
    before, after = (x.shape[:dim], x.shape[dim + 1 :])
    return jnp.moveaxis(x.reshape(*before, count, -1, *after), dim, 0)


def sent_and_summed(x, axis, dim):
    parts = split_up(x, dim, lax.axis_size(axis))
    arrived = lax.all_to_all(parts, axis, split_axis=0, concat_axis=0, tiled=True)
    return arrived.astype(jnp.float32).sum(axis=0)


def from_everyone(x, axis):
    count = lax.axis_size(axis)
    return lax.all_to_all(jnp.broadcast_to(x[None], (count, *x.shape)), axis, 0, 0, tiled=True)


def over_copies(x, axis):
    return from_everyone(x, axis).sum(axis=0)


def laid_out(parts, dim):
    parts = jnp.moveaxis(parts, 0, dim)
    shape = parts.shape
    return parts.reshape(*shape[:dim], shape[dim] * shape[dim + 1], *shape[dim + 2 :])


def gathered_copies(x, axis, dim):
    return laid_out(from_everyone(x, axis), dim)


def stencil(padded, potential):
    centre = padded[1:-1, 1:-1, 1:-1].astype(jnp.float32)
    neighbours = padded[2:, 1:-1, 1:-1].astype(jnp.float32) + padded[:-2, 1:-1, 1:-1].astype(
        jnp.float32
    )
    neighbours = (
        neighbours
        + padded[1:-1, 2:, 1:-1].astype(jnp.float32)
        + padded[1:-1, :-2, 1:-1].astype(jnp.float32)
    )
    neighbours = (
        neighbours
        + padded[1:-1, 1:-1, 2:].astype(jnp.float32)
        + padded[1:-1, 1:-1, :-2].astype(jnp.float32)
    )
    return ((3.0 + potential[..., None]) * centre - 0.5 * neighbours).astype(jnp.bfloat16)


def on_device(bands, potential, eigenvectors):
    halo_bands = extended(bands, (("gx", 0), ("gyz", 1)), 1)
    padded = jnp.pad(halo_bands, ((0, 0), (0, 0), (1, 1), (0, 0)))
    hamil_bands = stencil(padded, potential)
    band_count = bands.shape[3]
    cell_count = bands.shape[0] * bands.shape[1] * bands.shape[2]
    flat_bands = bands.reshape(cell_count, band_count)
    combined = jnp.concatenate((flat_bands, hamil_bands.reshape(cell_count, band_count)), axis=1)
    inv_volume = 1.0 / (cell_count * lax.axis_size("gyz"))
    product = lax.dot_general(
        flat_bands, combined, (((0,), (0,)), ((), ())), preferred_element_type=jnp.float32
    )
    row_terms = sent_and_summed((product * inv_volume).astype(jnp.bfloat16), "gyz", 0)
    gram_block = over_copies(row_terms, "gx")
    coefficients = gathered_copies(eigenvectors, "gyz", 0)
    rotated = jnp.dot(flat_bands, coefficients, preferred_element_type=jnp.float32)
    return (
        gram_block[:, :band_count],
        gram_block[:, band_count:],
        rotated.astype(jnp.bfloat16).reshape(bands.shape),
    )


def solution(mesh):
    in_specs = (P("gx", "gyz", None, None), P("gx", "gyz", None), P("gyz", None))
    out_specs = (P("gyz", None), P("gyz", None), P("gx", "gyz", None, None))
    return jax.shard_map(
        on_device, mesh=mesh, in_specs=in_specs, out_specs=out_specs, check_vma=False
    )
```

profile of v0, /device:TPU:2, one launch (start us, length us, event | category | flops | bytes accessed | tf_op | source)
XLA Modules:
  0.0 123.1 jit_solution(2703483198082108912)
XLA Ops:
  0.6 0.0 copy-start
  0.7 1.2 fusion.18
  1.8 1.8 %collective-permute-start.1 = (bf16[1,5,40,512]{3,2,1,0:T(8,128)(2,1)S(1)}, bf16[1,5,40,512]{3,2,1,0:T(8,128)(2,1)S(1)}, u32[]{:S(2)}, u32[]{:S(2)}) collective-permute-start(bf16[1,5,40,512]{3,2,1,0:T(8,128)(2,1)S(1)} %get-tuple-element.6), channel_id=1, source_target_pairs={{0,64},{64,128},{128,192},{192,256},{256,320},{320,384},{384,448},... | collective-permute-start | bytes 614408 | tf_op jit(solution)/shard_map/ppermute | solution.py:15
  3.6 1.3 %collective-permute-start = (bf16[1,5,40,512]{3,2,1,0:T(8,128)(2,1)S(1)}, bf16[1,5,40,512]{3,2,1,0:T(8,128)(2,1)S(1)}, u32[]{:S(2)}, u32[]{:S(2)}) collective-permute-start(bf16[1,5,40,512]{3,2,1,0:T(8,128)(2,1)S(1)} %get-tuple-element.5), channel_id=1, source_target_pairs={{64,0},{128,64},{192,128},{256,192},{320,256},{384,320},{448,384},... | collective-permute-start | bytes 614408 | tf_op jit(solution)/shard_map/ppermute | solution.py:16
  4.9 1.1 fusion.17
  6.0 4.3 %collective-permute-start.2 = (bf16[8,1,40,512]{3,2,1,0:T(8,128)(2,1)S(1)}, bf16[8,1,40,512]{3,2,1,0:T(8,128)(2,1)S(1)}, u32[]{:S(2)}, u32[]{:S(2)}) collective-permute-start(bf16[8,1,40,512]{3,2,1,0:T(8,128)(2,1)S(1)} %get-tuple-element.4), channel_id=1, source_target_pairs={{1,0},{2,1},{3,2},{4,3},{5,4},{6,5},{7,6},{8,7},{9,8},{10,9},{11,1... | collective-permute-start | bytes 983048 | tf_op jit(solution)/shard_map/ppermute | solution.py:16
  10.3 1.9 %collective-permute-start.3 = (bf16[8,1,40,512]{3,2,1,0:T(8,128)(2,1)S(1)}, bf16[8,1,40,512]{3,2,1,0:T(8,128)(2,1)S(1)}, u32[]{:S(2)}, u32[]{:S(2)}) collective-permute-start(bf16[8,1,40,512]{3,2,1,0:T(8,128)(2,1)S(1)} %get-tuple-element.3), channel_id=1, source_target_pairs={{0,1},{1,2},{2,3},{3,4},{4,5},{5,6},{6,7},{7,8},{8,9},{9,10},{10,1... | collective-permute-start | bytes 983048 | tf_op jit(solution)/shard_map/ppermute | solution.py:15
  12.3 0.1 constant_dynamic-update-slice_fusion.1
  12.5 5.7 %collective-permute-done.2 = bf16[8,1,40,512]{3,2,1,0:T(8,128)(2,1)S(1)} collective-permute-done((bf16[8,1,40,512]{3,2,1,0:T(8,128)(2,1)S(1)}, bf16[8,1,40,512]{3,2,1,0:T(8,128)(2,1)S(1)}, u32[]{:S(2)}, u32[]{:S(2)}) %collective-permute-start.2) | collective-permute-done | bytes 327712 | tf_op jit(solution)/shard_map/ppermute | solution.py:16
  18.2 12.3 %collective-permute-done.3 = bf16[8,1,40,512]{3,2,1,0:T(8,128)(2,1)S(1)} collective-permute-done((bf16[8,1,40,512]{3,2,1,0:T(8,128)(2,1)S(1)}, bf16[8,1,40,512]{3,2,1,0:T(8,128)(2,1)S(1)}, u32[]{:S(2)}, u32[]{:S(2)}) %collective-permute-start.3) | collective-permute-done | bytes 327712 | tf_op jit(solution)/shard_map/ppermute | solution.py:15
  30.6 1.7 %fusion.5 = bf16[10,7,42,512]{3,2,1,0:T(8,128)(2,1)S(1)} fusion(bf16[10,1,40,512]{3,2,1,0:T(8,128)(2,1)S(1)} %pad.11, bf16[10,5,40,512]{3,2,1,0:T(8,128)(2,1)S(1)} %constant_dynamic-update-slice_fusion, bf16[10,1,40,512]{3,2,1,0:T(8,128)(2,1)S(1)} %pad.12), kind=kLoop, calls=%fused_computation.7 | loop fusion | flops 18063360 | bytes 5877760 | tf_op jit(solution)/shard_map/concatenate | solution.py:22
  32.3 3.3 %subtract_convert_fusion = bf16[8,5,40,512]{3,2,1,0:T(8,128)(2,1)S(1)} fusion(bf16[8,5,40,512]{3,2,1,0:T(8,128)(2,1)S(1)} %copy-done, bf16[10,7,42,512]{3,2,1,0:T(8,128)(2,1)S(1)} %fusion.5, bf16[10,5,40,512]{3,2,1,0:T(8,128)(2,1)S(1)} %constant_dynamic-update-slice_fusion, bf16[10,1,40,512]{3,2,1,0:T(8,128)(2,1)S(1)} %pad.12, ...), kind=kLoop, calls=%fused_computation.12 | loop fusion | flops 16384000 | bytes 9836800 | tf_op jit(solution)/shard_map/convert_element_type | solution.py:72
  35.6 2.1 %fusion.12 = bf16[64,8,1024]{2,1,0:T(8,128)(2,1)S(1)} fusion(bf16[1600,512]{1,0:T(8,128)(2,1)S(1)} %bitcast.12, bf16[1600,512]{1,0:T(8,128)(2,1)S(1)} %bitcast.14), kind=kOutput, calls=%fused_computation.20 | convolution fusion | flops 1685323776 | bytes 4325376 | tf_op jit(solution)/shard_map/dot_general | solution.py:84
  37.7 0.0 copy-start.2
  37.7 35.9 %all_to_all.15 = bf16[64,8,1024]{2,1,0:T(8,128)(2,1)S(1)} all-to-all(bf16[64,8,1024]{2,1,0:T(8,128)(2,1)S(1)} %fusion.12), channel_id=1, replica_groups=mesh['gx'=8,'gyz'=64] {'gyz'}, dimensions={0} | all-to-all | bytes 2097152 | tf_op jit(solution)/shard_map/all_to_all | solution.py:34
  73.7 0.8 broadcast_in_dim.5
  74.5 6.8 %all-to-all-start.2 = ((bf16[64,8,512]{2,1,0:T(8,128)(2,1)}), bf16[64,8,512]{2,1,0:T(8,128)(2,1)S(1)}, u32[]{:S(2)}, u32[]{:S(2)}) async-start(bf16[64,8,512]{2,1,0:T(8,128)(2,1)} %broadcast_in_dim.5), calls=%async_computation.2 | async-start | bytes 1048576 | tf_op jit(solution)/shard_map/all_to_all | solution.py:40
  81.3 0.2 convert_reduce_fusion
  81.5 16.2 %all-to-all-done.2 = bf16[64,8,512]{2,1,0:T(8,128)(2,1)S(1)} async-done(((bf16[64,8,512]{2,1,0:T(8,128)(2,1)}), bf16[64,8,512]{2,1,0:T(8,128)(2,1)S(1)}, u32[]{:S(2)}, u32[]{:S(2)}) %all-to-all-start.2) | async-done | bytes 524320 | tf_op jit(solution)/shard_map/all_to_all | solution.py:40
  97.7 0.7 broadcast_in_dim.4
  98.4 11.3 %all-to-all-start.1 = ((f32[8,8,1024]{2,1,0:T(8,128)}), f32[8,8,1024]{2,1,0:T(8,128)S(1)}, u32[]{:S(2)}, u32[]{:S(2)}) async-start(f32[8,8,1024]{2,1,0:T(8,128)} %broadcast_in_dim.4), calls=%async_computation.1 | async-start | bytes 524288 | tf_op jit(solution)/shard_map/all_to_all | solution.py:40
  109.7 2.2 %convolution_convert_fusion = bf16[1600,512]{1,0:T(8,128)(2,1)} fusion(bf16[1600,512]{1,0:T(8,128)(2,1)S(1)} %bitcast.13, bf16[64,8,512]{2,1,0:T(8,128)(2,1)S(1)} %all-to-all-done.2), kind=kOutput, calls=%fused_computation.13 | convolution fusion | flops 839680000 | bytes 3801088 | tf_op jit(solution)/shard_map/dot_general | solution.py:90
  111.9 10.5 %all-to-all-done.1 = f32[8,8,1024]{2,1,0:T(8,128)S(1)} async-done(((f32[8,8,1024]{2,1,0:T(8,128)}), f32[8,8,1024]{2,1,0:T(8,128)S(1)}, u32[]{:S(2)}, u32[]{:S(2)}) %all-to-all-start.1) | async-done | bytes 262176 | tf_op jit(solution)/shard_map/all_to_all | solution.py:40
  122.5 0.6 fusion.19
  (13 shorter events, 0.1 us)
Async XLA Ops:
  0.6 11.7 %copy-start = (bf16[8,5,40,512]{3,2,1,0:T(8,128)(2,1)S(1)}, bf16[8,5,40,512]{3,2,1,0:T(8,128)(2,1)}, u32[]{:S(2)}) copy-start(bf16[8,5,40,512]{3,2,1,0:T(8,128)(2,1)} %param.3) | copy-start | bytes 4915204
  0.6 11.6 %copy-start.1 = (f32[8,5,40]{2,0,1:T(8,128)S(1)}, f32[8,5,40]{2,0,1:T(8,128)}, u32[]{:S(2)}) copy-start(f32[8,5,40]{2,0,1:T(8,128)} %param.4) | copy-start | bytes 19204
  1.8 10.5 %collective-permute-start.1 = (bf16[1,5,40,512]{3,2,1,0:T(8,128)(2,1)S(1)}, bf16[1,5,40,512]{3,2,1,0:T(8,128)(2,1)S(1)}, u32[]{:S(2)}, u32[]{:S(2)}) collective-permute-start(bf16[1,5,40,512]{3,2,1,0:T(8,128)(2,1)S(1)} %get-tuple-element.6), channel_id=1, source_target_pairs={{0,64},{64,128},{128,192},{192,256},{256,320},{320,384},{384,448},... | collective-permute-start | bytes 614408 | tf_op jit(solution)/shard_map/ppermute | solution.py:15
  3.6 8.9 %collective-permute-start = (bf16[1,5,40,512]{3,2,1,0:T(8,128)(2,1)S(1)}, bf16[1,5,40,512]{3,2,1,0:T(8,128)(2,1)S(1)}, u32[]{:S(2)}, u32[]{:S(2)}) collective-permute-start(bf16[1,5,40,512]{3,2,1,0:T(8,128)(2,1)S(1)} %get-tuple-element.5), channel_id=1, source_target_pairs={{64,0},{128,64},{192,128},{256,192},{320,256},{384,320},{448,384},... | collective-permute-start | bytes 614408 | tf_op jit(solution)/shard_map/ppermute | solution.py:16
  6.0 12.2 %collective-permute-start.2 = (bf16[8,1,40,512]{3,2,1,0:T(8,128)(2,1)S(1)}, bf16[8,1,40,512]{3,2,1,0:T(8,128)(2,1)S(1)}, u32[]{:S(2)}, u32[]{:S(2)}) collective-permute-start(bf16[8,1,40,512]{3,2,1,0:T(8,128)(2,1)S(1)} %get-tuple-element.4), channel_id=1, source_target_pairs={{1,0},{2,1},{3,2},{4,3},{5,4},{6,5},{7,6},{8,7},{9,8},{10,9},{11,1... | collective-permute-start | bytes 983048 | tf_op jit(solution)/shard_map/ppermute | solution.py:16
  10.3 20.2 %collective-permute-start.3 = (bf16[8,1,40,512]{3,2,1,0:T(8,128)(2,1)S(1)}, bf16[8,1,40,512]{3,2,1,0:T(8,128)(2,1)S(1)}, u32[]{:S(2)}, u32[]{:S(2)}) collective-permute-start(bf16[8,1,40,512]{3,2,1,0:T(8,128)(2,1)S(1)} %get-tuple-element.3), channel_id=1, source_target_pairs={{0,1},{1,2},{2,3},{3,4},{4,5},{5,6},{6,7},{7,8},{8,9},{9,10},{10,1... | collective-permute-start | bytes 983048 | tf_op jit(solution)/shard_map/ppermute | solution.py:15
  37.7 35.9 %copy-start.2 = (bf16[8,512]{1,0:T(8,128)(2,1)S(1)}, bf16[8,512]{1,0:T(8,128)(2,1)}, u32[]{:S(2)}) copy-start(bf16[8,512]{1,0:T(8,128)(2,1)} %param.5) | copy-start | bytes 24580
  74.5 23.2 %all-to-all-start.2 = ((bf16[64,8,512]{2,1,0:T(8,128)(2,1)}), bf16[64,8,512]{2,1,0:T(8,128)(2,1)S(1)}, u32[]{:S(2)}, u32[]{:S(2)}) async-start(bf16[64,8,512]{2,1,0:T(8,128)(2,1)} %broadcast_in_dim.5), calls=%async_computation.2 | async-start | bytes 1048576 | tf_op jit(solution)/shard_map/all_to_all | solution.py:40
  98.4 24.0 %all-to-all-start.1 = ((f32[8,8,1024]{2,1,0:T(8,128)}), f32[8,8,1024]{2,1,0:T(8,128)S(1)}, u32[]{:S(2)}, u32[]{:S(2)}) async-start(f32[8,8,1024]{2,1,0:T(8,128)} %broadcast_in_dim.4), calls=%async_computation.1 | async-start | bytes 524288 | tf_op jit(solution)/shard_map/all_to_all | solution.py:40
where the time goes:
time: 124 us; the launch traced here: 123 us
  waiting for transfers between devices  44.8 us (36%)
  blocking collectives  35.9 us (29%)
  starting transfers between devices  27.4 us (22%)
  other arithmetic  5.24 us (4%)
  local copies, waits for them, and re-layouts  4.68 us (4%)
  matrix products  4.29 us (3%)
    all_to_all x1, blocking collectives, sent_and_summed(): lax.all_to_all(parts, axis, split_axis=0, concat_axis=0, tiled=True)  35.9 us
    all_to_all x2, waiting for transfers between devices, from_everyone(): lax.all_to_all(jnp.broadcast_to(x[None], (count, *x.shape)), axis, 0, 0,...  26.7 us
    all_to_all x2, starting transfers between devices, from_everyone(): lax.all_to_all(jnp.broadcast_to(x[None], (count, *x.shape)), axis, 0, 0,...  18.1 us
    ppermute x2, waiting for transfers between devices, extended(): lax.ppermute(last, axis, up)  12.3 us
    ppermute x2, waiting for transfers between devices, extended(): lax.ppermute(leading, axis, [(b, a) for a, b in up])  5.74 us
    ppermute x2, starting transfers between devices, extended(): lax.ppermute(leading, axis, [(b, a) for a, b in up])  5.54 us
    ppermute x2, starting transfers between devices, extended(): lax.ppermute(last, axis, up)  3.7 us
    convert_element_type x1, other arithmetic, stencil(): ((3.0 + potential[..., None]) * centre - 0.5 * neighbours).astype(jnp.bfl...  3.31 us
  transfers between devices with their start and end apart: 6, of which 4 were waited for; matrix products, arithmetic and copies ran while one was open for 3% of the time, Pallas kernels for 0%

commit v1 on v0

v1 whole, which is shorter than its diff:
```python
import functools

import jax
import jax.numpy as jnp
from jax import lax
from jax.experimental import pallas as pl
from jax.experimental.pallas import tpu as pltpu
from jax.sharding import PartitionSpec as P


F32 = jnp.float32
BF16 = jnp.bfloat16


def over_rows(a, b):
    return lax.dot_general(a, b, (((0,), (0,)), ((), ())), preferred_element_type=F32)


def stencil_kernel(bands_ref, pot_ref, out_ref):
    nx, ny, nz, nb = bands_ref.shape
    row = lax.broadcasted_iota(jnp.int32, (nz, nb), 0)

    def plane(x, carry):
        below = jnp.where(x > 0, 0.5, 0.0)
        above = jnp.where(x < nx - 1, 0.5, 0.0)
        pot = jnp.transpose(pot_ref[x])
        tiles = [bands_ref[x, y].astype(F32) for y in range(ny)]
        for y in range(ny):
            centre = tiles[y]
            total = jnp.where(row > 0, pltpu.roll(centre, 1, 0), 0.0)
            total += jnp.where(row < nz - 1, pltpu.roll(centre, nz - 1, 0), 0.0)
            if y > 0:
                total += tiles[y - 1]
            if y < ny - 1:
                total += tiles[y + 1]
            low = bands_ref[jnp.maximum(x - 1, 0), y].astype(F32)
            high = bands_ref[jnp.minimum(x + 1, nx - 1), y].astype(F32)
            value = (3.0 + pot[:, y : y + 1]) * centre - 0.5 * total
            value -= below * low + above * high
            out_ref[x, y] = value.astype(BF16)
        return carry

    lax.fori_loop(0, nx, plane, 0)


def local_stencil(bands, potential):
    return pl.pallas_call(
        stencil_kernel,
        out_shape=jax.ShapeDtypeStruct(bands.shape, BF16),
        in_specs=[pl.BlockSpec(memory_space=pltpu.VMEM)] * 2,
        out_specs=pl.BlockSpec(memory_space=pltpu.VMEM),
        cost_estimate=pl.CostEstimate(
            flops=12 * bands.size, bytes_accessed=4 * bands.size, transcendentals=0
        ),
        compiler_params=pltpu.CompilerParams(vmem_limit_bytes=12 << 20),
        name="stencil",
    )(bands, potential)


def cross_kernel(scale, local_ref, first_ref, slab_ref, yhalo_ref, xhalo_ref, out_ref):
    nb = local_ref.shape[0]
    first = first_ref[...].reshape(-1, nb)
    slab = slab_ref[...].reshape(-1, nb)
    yhalo = yhalo_ref[...].reshape(-1, nb)
    xhalo = xhalo_ref[...].reshape(-1, nb)
    cross = over_rows(first, yhalo) + over_rows(slab, xhalo)
    cross += over_rows(yhalo, first) + over_rows(xhalo, slab)
    out_ref[...] = (scale * (local_ref[...] - 0.5 * cross)).astype(BF16)


def add_cross(scale, local, first, slab, yhalo, xhalo):
    nb = local.shape[0]
    rows = first.size // nb + slab.size // nb
    return pl.pallas_call(
        functools.partial(cross_kernel, scale),
        out_shape=jax.ShapeDtypeStruct(local.shape, BF16),
        in_specs=[pl.BlockSpec(memory_space=pltpu.VMEM)] * 5,
        out_specs=pl.BlockSpec(memory_space=pltpu.VMEM),
        cost_estimate=pl.CostEstimate(
            flops=4 * rows * nb * nb, bytes_accessed=6 * nb * nb, transcendentals=0
        ),
        compiler_params=pltpu.CompilerParams(vmem_limit_bytes=12 << 20),
        name="cross",
    )(local, first, slab, yhalo, xhalo)


def x_pairs(gx, gyz):
    pairs = []
    for r in range(gyz):
        for g in range(gx - 1):
            low, high = g * gyz + r, (g + 1) * gyz + r
            pairs.append((low, high) if r % 2 == 0 else (high, low))
    return pairs


def to_rows(x, axis):
    count = lax.axis_size(axis)
    parts = x.reshape(count, x.shape[0] // count, x.shape[1])
    return lax.all_to_all(parts, axis, 0, 0, tiled=True)


def from_everyone(x, axis):
    count = lax.axis_size(axis)
    return lax.all_to_all(jnp.broadcast_to(x[None], (count, *x.shape)), axis, 0, 0, tiled=True)


def projected(bands, potential, eigenvectors):
    nx, ny, nz, nb = bands.shape
    gx, gyz = lax.axis_size("gx"), lax.axis_size("gyz")
    odd = lax.rem(lax.axis_index("gyz"), 2)
    cells = nx * ny * nz
    scale = 1.0 / (cells * gyz)
    flat = bands.reshape(cells, nb)

    sent_slab = jnp.where(odd == 0, nx - 1, 0)
    last = lax.slice_in_dim(bands, ny - 1, ny, axis=1)
    slab = lax.dynamic_slice_in_dim(bands, sent_slab, 1, axis=0)
    yhalo = lax.ppermute(last, "gyz", [(i, i + 1) for i in range(gyz - 1)])
    xhalo = lax.ppermute(slab, ("gx", "gyz"), x_pairs(gx, gyz))

    corr = (over_rows(flat, flat) * scale).astype(BF16)
    corr_parts = to_rows(corr, "gyz")

    hamil_bands = local_stencil(bands, potential)
    local = over_rows(flat, hamil_bands.reshape(cells, nb))
    first = lax.slice_in_dim(bands, 0, 1, axis=1)
    own_slab = lax.dynamic_slice_in_dim(bands, nx - 1 - sent_slab, 1, axis=0)
    hamil = add_cross(scale, local, first, own_slab, yhalo, xhalo)
    hamil_parts = to_rows(hamil, "gyz")

    coefficients = from_everyone(eigenvectors, "gyz").reshape(nb, nb)
    rotated = jnp.dot(flat, coefficients, preferred_element_type=F32).astype(BF16)

    rows = jnp.concatenate(
        (corr_parts.astype(F32).sum(axis=0), hamil_parts.astype(F32).sum(axis=0)), axis=1
    )
    total = from_everyone(rows, "gx").sum(axis=0)
    return total[:, :nb], total[:, nb:], rotated.reshape(bands.shape)


def solution(mesh):
    in_specs = (P("gx", "gyz", None, None), P("gx", "gyz", None), P("gyz", None))
    out_specs = (P("gyz", None), P("gyz", None), P("gx", "gyz", None, None))
    return jax.shard_map(
        projected, mesh=mesh, in_specs=in_specs, out_specs=out_specs, check_vma=False
    )
```

time: 124 us -> 113 us (0.911)
  blocking collectives: 35.9 us -> 28 us
  waiting for transfers between devices: 44.8 us -> 37.2 us
  starting transfers between devices: 27.4 us -> 33.2 us
  other arithmetic: 5.24 us -> 0.23 us
  Pallas kernels: 0 us -> 3.59 us
  matrix products: 4.29 us -> 7.32 us
  local copies, waits for them, and re-layouts: 4.68 us -> 2.27 us
    all_to_all x0 -> x1, starting transfers between devices: none -> 12.6 us  [to_rows(): return lax.all_to_all(parts, axis, 0, 0, tiled=True)]
    ppermute x4 -> x2, waiting for transfers between devices: 18 us -> 7.35 us  [the longest x1 7.35 us: projected(): yhalo = lax.ppermute(last, 'gyz', [(i, i + 1) for i in range(gyz - 1)])]
    all_to_all x1, blocking collectives: 35.9 us -> 28 us  [to_rows(): return lax.all_to_all(parts, axis, 0, 0, tiled=True)]
    ppermute x4 -> x2, starting transfers between devices: 9.24 us -> 4.67 us  [the longest x1 3.37 us: projected(): yhalo = lax.ppermute(last, 'gyz', [(i, i + 1) for i in range(gyz - 1)])]
    pallas_call x0 -> x2, Pallas kernels: none -> 3.59 us  [the longest x1 2.57 us: local_stencil(): pl.pallas_call(stencil_kernel, out_shape=jax.ShapeDtypeStruct(bands.shape...]
    convert_element_type x1 -> x0, other arithmetic: 3.31 us -> none  [stencil(): ((3.0 + potential[..., None]) * centre - 0.5 * neighbours).astype(jnp.bfl...]
    dot_general x2 -> x3, matrix products: 4.29 us -> 7.32 us  [the longest x2 5.15 us: over_rows(): lax.dot_general(a, b, (((0,), (0,)), ((), ())), preferred_element_type=F32)]
    slice x3 -> x2, local copies, waits for them, and re-layouts: 2.92 us -> 0.66 us  [the longest x1 0.61 us: projected(): return (total[:, :nb], total[:, nb:], rotated.reshape(bands.shape))]
  transfers between devices with their start and end apart: 6 -> 5, of which waited for: 4 -> 4; matrix products, arithmetic and copies ran while one was open for 3% -> 3% of each run, Pallas kernels for 0% -> 3%
where the time goes in v1:
time: 113 us
  waiting for transfers between devices  37.2 us (33%)
  starting transfers between devices  33.2 us (29%)
  blocking collectives  28 us (25%)
  matrix products  7.32 us (6%)
  Pallas kernels  3.59 us (3%)
  local copies, waits for them, and re-layouts  2.27 us (2%)
    all_to_all x1, blocking collectives, to_rows(): return lax.all_to_all(parts, axis, 0, 0, tiled=True)  28 us
    all_to_all x2, waiting for transfers between devices, from_everyone(): lax.all_to_all(jnp.broadcast_to(x[None], (count, *x.shape)), axis, 0, 0,...  27.8 us
    all_to_all x2, starting transfers between devices, from_everyone(): lax.all_to_all(jnp.broadcast_to(x[None], (count, *x.shape)), axis, 0, 0,...  15.9 us
    all_to_all x1, starting transfers between devices, to_rows(): return lax.all_to_all(parts, axis, 0, 0, tiled=True)  12.6 us
    ppermute x1, waiting for transfers between devices, projected(): yhalo = lax.ppermute(last, 'gyz', [(i, i + 1) for i in range(gyz - 1)])  7.35 us
    dot_general x2, matrix products, over_rows(): lax.dot_general(a, b, (((0,), (0,)), ((), ())), preferred_element_type=F32)  5.15 us
    ppermute x1, starting transfers between devices, projected(): yhalo = lax.ppermute(last, 'gyz', [(i, i + 1) for i in range(gyz - 1)])  3.37 us
    pallas_call x1, Pallas kernels, local_stencil(): pl.pallas_call(stencil_kernel, out_shape=jax.ShapeDtypeStruct(bands.shape...  2.57 us
  transfers between devices with their start and end apart: 5, of which 4 were waited for; matrix products, arithmetic and copies ran while one was open for 3% of the time, Pallas kernels for 3%

profile of v1, /device:TPU:2, one launch (start us, length us, event | category | flops | bytes accessed | tf_op | source)
XLA Modules:
  0.0 112.6 jit_solution(896895620463253098)
XLA Ops:
  0.6 0.0 copy-start
  0.6 4.0 %fusion.2 = bf16[64,8,512]{2,1,0:T(8,128)(2,1)} fusion(bf16[8,5,40,512]{3,2,1,0:T(8,128)(2,1)} %bands_ref.1), kind=kOutput, calls=%fused_computation.5 | convolution fusion | flops 839385088 | bytes 2162688 | tf_op jit(solution)/shard_map/dot_general | solution.py:16
  4.6 12.6 %all-to-all-start = ((bf16[64,8,512]{2,1,0:T(8,128)(2,1)}), bf16[64,8,512]{2,1,0:T(8,128)(2,1)S(1)}, u32[]{:S(2)}, u32[]{:S(2)}) async-start(bf16[64,8,512]{2,1,0:T(8,128)(2,1)} %fusion.2), calls=%async_computation | async-start | bytes 1048576 | tf_op jit(solution)/shard_map/all_to_all | solution.py:99
  17.2 0.0 copy-done
  17.3 3.4 %collective-permute-start = (bf16[8,1,40,512]{3,2,1,0:T(8,128)(2,1)S(1)}, bf16[8,1,40,512]{3,2,1,0:T(8,128)(2,1)S(1)}, u32[]{:S(2)}, u32[]{:S(2)}) collective-permute-start(bf16[8,1,40,512]{3,2,1,0:T(8,128)(2,1)S(1)} %get-tuple-element.5), channel_id=1, source_target_pairs={{0,1},{1,2},{2,3},{3,4},{4,5},{5,6},{6,7},{7,8},{8,9},{9,10},{10,1... | collective-permute-start | bytes 983048 | tf_op jit(solution)/shard_map/ppermute | solution.py:118
  20.7 1.3 %collective-permute-start.1 = (bf16[1,5,40,512]{3,2,1,0:T(8,128)(2,1)S(1)}, bf16[1,5,40,512]{3,2,1,0:T(8,128)(2,1)S(1)}, u32[]{:S(2)}, u32[]{:S(2)}) collective-permute-start(bf16[1,5,40,512]{3,2,1,0:T(8,128)(2,1)S(1)} %get-tuple-element.3), channel_id=1, source_target_pairs={{0,64},{64,128},{128,192},{192,256},{256,320},{320,384},{384,448},... | collective-permute-start | bytes 614408 | tf_op jit(solution)/shard_map/ppermute | solution.py:119
  22.0 0.0 copy-done.1
  22.0 2.6 %stencil.1 = bf16[8,5,40,512]{3,2,1,0:T(8,128)(2,1)S(1)} custom-call(bf16[8,5,40,512]{3,2,1,0:T(8,128)(2,1)S(1)} %copy-done, f32[8,5,40]{2,1,0:T(8,128)S(1)} %copy.8.pot_ref), custom_call_target="tpu_custom_call" | custom-call | flops 9830400 | bytes 3276800 | tf_op jit(solution)/shard_map/stencil/pallas_call | solution.py:47
  24.6 1.2 %convolution_bitcast_fusion.local_ref = f32[512,512]{1,0:T(8,128)S(1)} fusion(bf16[8,5,40,512]{3,2,1,0:T(8,128)(2,1)S(1)} %stencil.1, bf16[8,5,40,512]{3,2,1,0:T(8,128)(2,1)S(1)} %copy-done), kind=kOutput, calls=%fused_computation.1 | convolution fusion | flops 838860800 | bytes 4325376 | tf_op jit(solution)/shard_map/dot_general | solution.py:16
  25.8 0.0 collective-permute-done.1.xhalo_ref
  25.8 7.3 %collective-permute-done.yhalo_ref = bf16[8,1,40,512]{3,2,1,0:T(8,128)(2,1)S(1)} collective-permute-done((bf16[8,1,40,512]{3,2,1,0:T(8,128)(2,1)S(1)}, bf16[8,1,40,512]{3,2,1,0:T(8,128)(2,1)S(1)}, u32[]{:S(2)}, u32[]{:S(2)}) %collective-permute-start) | collective-permute-done | bytes 327712 | tf_op jit(solution)/shard_map/ppermute | solution.py:118
  33.2 1.0 cross.1
  34.2 2.1 %all-to-all-done = bf16[64,8,512]{2,1,0:T(8,128)(2,1)S(1)} async-done(((bf16[64,8,512]{2,1,0:T(8,128)(2,1)}), bf16[64,8,512]{2,1,0:T(8,128)(2,1)S(1)}, u32[]{:S(2)}, u32[]{:S(2)}) %all-to-all-start) | async-done | bytes 524320 | tf_op jit(solution)/shard_map/all_to_all | solution.py:99
  36.3 28.0 %all_to_all.20 = bf16[64,8,512]{2,1,0:T(8,128)(2,1)S(1)} all-to-all(bf16[64,8,512]{2,1,0:T(8,128)(2,1)S(1)} %bitcast.28), channel_id=1, replica_groups=mesh['gx'=8,'gyz'=64] {'gyz'}, dimensions={0} | all-to-all | bytes 1048576 | tf_op jit(solution)/shard_map/all_to_all | solution.py:99
  64.3 0.8 broadcast_in_dim.5
  65.1 7.9 %all-to-all-start.3 = ((bf16[64,8,512]{2,1,0:T(8,128)(2,1)}), bf16[64,8,512]{2,1,0:T(8,128)(2,1)S(1)}, u32[]{:S(2)}, u32[]{:S(2)}) async-start(bf16[64,8,512]{2,1,0:T(8,128)(2,1)} %broadcast_in_dim.5), calls=%async_computation.3 | async-start | bytes 1048576 | tf_op jit(solution)/shard_map/all_to_all | solution.py:104
  73.0 0.1 convert_reduce_fusion.1
  73.1 0.1 convert_reduce_fusion
  73.2 17.2 %all-to-all-done.3 = bf16[64,8,512]{2,1,0:T(8,128)(2,1)S(1)} async-done(((bf16[64,8,512]{2,1,0:T(8,128)(2,1)}), bf16[64,8,512]{2,1,0:T(8,128)(2,1)S(1)}, u32[]{:S(2)}, u32[]{:S(2)}) %all-to-all-start.3) | async-done | bytes 524320 | tf_op jit(solution)/shard_map/all_to_all | solution.py:104
  90.5 0.7 broadcast_in_dim.4
  91.2 8.0 %all-to-all-start.2 = ((f32[8,8,1024]{2,1,0:T(8,128)}), f32[8,8,1024]{2,1,0:T(8,128)S(1)}, u32[]{:S(2)}, u32[]{:S(2)}) async-start(f32[8,8,1024]{2,1,0:T(8,128)} %broadcast_in_dim.4), calls=%async_computation.2 | async-start | bytes 524288 | tf_op jit(solution)/shard_map/all_to_all | solution.py:104
  99.2 2.2 %convolution_convert_fusion = bf16[1600,512]{1,0:T(8,128)(2,1)} fusion(bf16[1600,512]{1,0:T(8,128)(2,1)S(1)} %bitcast.27, bf16[64,8,512]{2,1,0:T(8,128)(2,1)S(1)} %all-to-all-done.3), kind=kOutput, calls=%fused_computation | convolution fusion | flops 839680000 | bytes 3801088 | tf_op jit(solution)/shard_map/dot_general | solution.py:132
  101.4 10.5 %all-to-all-done.2 = f32[8,8,1024]{2,1,0:T(8,128)S(1)} async-done(((f32[8,8,1024]{2,1,0:T(8,128)}), f32[8,8,1024]{2,1,0:T(8,128)S(1)}, u32[]{:S(2)}, u32[]{:S(2)}) %all-to-all-start.2) | async-done | bytes 262176 | tf_op jit(solution)/shard_map/all_to_all | solution.py:104
  112.0 0.6 fusion.5
  (8 shorter events, 0.1 us)
Async XLA Ops:
  0.6 16.6 %copy-start = (bf16[8,5,40,512]{3,2,1,0:T(8,128)(2,1)S(1)}, bf16[8,5,40,512]{3,2,1,0:T(8,128)(2,1)}, u32[]{:S(2)}) copy-start(bf16[8,5,40,512]{3,2,1,0:T(8,128)(2,1)} %bands_ref.1) | copy-start | bytes 4915204
  4.6 17.4 %copy-start.1 = (f32[8,5,40]{2,0,1:T(8,128)S(1)}, f32[8,5,40]{2,0,1:T(8,128)}, u32[]{:S(2)}) copy-start(f32[8,5,40]{2,0,1:T(8,128)} %param.4) | copy-start | bytes 19204
  4.6 31.7 %all-to-all-start = ((bf16[64,8,512]{2,1,0:T(8,128)(2,1)}), bf16[64,8,512]{2,1,0:T(8,128)(2,1)S(1)}, u32[]{:S(2)}, u32[]{:S(2)}) async-start(bf16[64,8,512]{2,1,0:T(8,128)(2,1)} %fusion.2), calls=%async_computation | async-start | bytes 1048576 | tf_op jit(solution)/shard_map/all_to_all | solution.py:99
  17.3 15.9 %collective-permute-start = (bf16[8,1,40,512]{3,2,1,0:T(8,128)(2,1)S(1)}, bf16[8,1,40,512]{3,2,1,0:T(8,128)(2,1)S(1)}, u32[]{:S(2)}, u32[]{:S(2)}) collective-permute-start(bf16[8,1,40,512]{3,2,1,0:T(8,128)(2,1)S(1)} %get-tuple-element.5), channel_id=1, source_target_pairs={{0,1},{1,2},{2,3},{3,4},{4,5},{5,6},{6,7},{7,8},{8,9},{9,10},{10,1... | collective-permute-start | bytes 983048 | tf_op jit(solution)/shard_map/ppermute | solution.py:118
  20.7 5.1 %collective-permute-start.1 = (bf16[1,5,40,512]{3,2,1,0:T(8,128)(2,1)S(1)}, bf16[1,5,40,512]{3,2,1,0:T(8,128)(2,1)S(1)}, u32[]{:S(2)}, u32[]{:S(2)}) collective-permute-start(bf16[1,5,40,512]{3,2,1,0:T(8,128)(2,1)S(1)} %get-tuple-element.3), channel_id=1, source_target_pairs={{0,64},{64,128},{128,192},{192,256},{256,320},{320,384},{384,448},... | collective-permute-start | bytes 614408 | tf_op jit(solution)/shard_map/ppermute | solution.py:119
  33.2 31.1 %copy-start.2 = (bf16[8,512]{1,0:T(8,128)(2,1)S(1)}, bf16[8,512]{1,0:T(8,128)(2,1)}, u32[]{:S(2)}) copy-start(bf16[8,512]{1,0:T(8,128)(2,1)} %param.5) | copy-start | bytes 24580
  65.1 25.3 %all-to-all-start.3 = ((bf16[64,8,512]{2,1,0:T(8,128)(2,1)}), bf16[64,8,512]{2,1,0:T(8,128)(2,1)S(1)}, u32[]{:S(2)}, u32[]{:S(2)}) async-start(bf16[64,8,512]{2,1,0:T(8,128)(2,1)} %broadcast_in_dim.5), calls=%async_computation.3 | async-start | bytes 1048576 | tf_op jit(solution)/shard_map/all_to_all | solution.py:104
  91.2 20.7 %all-to-all-start.2 = ((f32[8,8,1024]{2,1,0:T(8,128)}), f32[8,8,1024]{2,1,0:T(8,128)S(1)}, u32[]{:S(2)}, u32[]{:S(2)}) async-start(f32[8,8,1024]{2,1,0:T(8,128)} %broadcast_in_dim.4), calls=%async_computation.2 | async-start | bytes 524288 | tf_op jit(solution)/shard_map/all_to_all | solution.py:104

commit v2 on v1

v2 whole, which is shorter than its diff:
```python
import functools

import jax
import jax.numpy as jnp
from jax import lax
from jax.experimental import pallas as pl
from jax.experimental.pallas import tpu as pltpu
from jax.sharding import PartitionSpec as P


F32 = jnp.float32
BF16 = jnp.bfloat16
BOTH = ("gx", "gyz")


def over_rows(a, b):
    return lax.dot_general(a, b, (((0,), (0,)), ((), ())), preferred_element_type=F32)


def half_stencil(core, planes, pots, outs):
    nx, ny, nz, nb = planes[0].shape
    row = lax.broadcasted_iota(jnp.int32, (nz, nb), 0)
    half = jnp.where(core == 1, 0.5, 0.0).astype(F32)

    def tiles_at(ref, x):
        return [ref[x, y].astype(F32) for y in range(ny)]

    def one(ref, pot_ref, out_ref, x, below, weight):
        pot = jnp.transpose(pot_ref[x])
        factor = 0.5 + half * (2.0 + pot)
        tiles = tiles_at(ref, x)
        for y in range(ny):
            total = jnp.where(row > 0, pltpu.roll(tiles[y], 1, 0), 0.0)
            if y > 0:
                total += tiles[y - 1]
            value = factor[:, y : y + 1] * tiles[y] - half * total - weight * below[y]
            out_ref[x, y] = value.astype(BF16)

    low, high = planes
    zero = [jnp.zeros((nz, nb), F32)] * ny
    one(low, pots[0], outs[0], 0, zero, half)
    one(high, pots[1], outs[1], 0, tiles_at(low, nx - 1), half)

    def step(x, carry):
        for ref, pot, out in zip(planes, pots, outs):
            one(ref, pot, out, x, tiles_at(ref, x - 1), half)
        return carry

    lax.fori_loop(1, nx, step, 0)


def gram_kernel(
    scale, place_ref, own_ref, other_ref, pot_ref, other_pot_ref, yown_ref, yother_ref, xhalo_ref,
    out_ref, right_own, right_other,
):
    nx, _, _, nb = own_ref.shape
    core, odd = place_ref[0], place_ref[1]
    half_stencil(
        core, (other_ref, own_ref), (other_pot_ref, pot_ref), (right_other, right_own)
    )

    def rows(value):
        return value.reshape(-1, nb)

    gram = over_rows(rows(own_ref[...]), rows(right_own[...]))
    gram += over_rows(rows(other_ref[...]), rows(right_other[...]))
    cross = over_rows(rows(own_ref[:, 0]), rows(yown_ref[...]))
    cross += over_rows(rows(other_ref[:, 0]), rows(yother_ref[...]))
    slab = jnp.where(odd == 0, other_ref[0], own_ref[nx - 1])
    cross += over_rows(rows(slab), rows(xhalo_ref[...]))
    gram -= 0.5 * cross
    out_ref[...] = (scale * (gram + jnp.transpose(gram))).astype(BF16)


def gram_partial(scale, place, own, other, pot, other_pot, yown, yother, xhalo):
    nb = own.shape[-1]
    rows = 2 * (own.size // nb)
    vmem = pl.BlockSpec(memory_space=pltpu.VMEM)
    return pl.pallas_call(
        functools.partial(gram_kernel, scale),
        out_shape=jax.ShapeDtypeStruct((nb, nb), BF16),
        in_specs=[pl.BlockSpec(memory_space=pltpu.SMEM)] + [vmem] * 7,
        out_specs=vmem,
        scratch_shapes=[pltpu.VMEM(own.shape, BF16)] * 2,
        cost_estimate=pl.CostEstimate(
            flops=2 * rows * nb * nb, bytes_accessed=4 * rows * nb, transcendentals=0
        ),
        compiler_params=pltpu.CompilerParams(vmem_limit_bytes=24 << 20),
        name="gram",
    )(place, own, other, pot, other_pot, yown, yother, xhalo)


def pairs_of(gx, gyz):
    def at(g, r):
        return g * gyz + r

    same, next_core, x = [], [], []
    for chip in range(gx // 2):
        for r in range(gyz - 1):
            same.append((at(2 * chip + 1, r), at(2 * chip + 1, r + 1)))
            next_core.append((at(2 * chip, r), at(2 * chip + 1, r + 1)))
    for chip in range(gx // 2 - 1):
        for r in range(gyz):
            if r % 2 == 0:
                x.append((at(2 * chip + 1, r), at(2 * chip + 3, r)))
            else:
                x.append((at(2 * chip + 2, r), at(2 * chip + 1, r)))
    return same, next_core, x


def to_rows(x, axis):
    count = lax.axis_size(axis)
    parts = x.reshape(count, x.shape[0] // count, x.shape[1])
    return lax.all_to_all(parts, axis, 0, 0, tiled=True)


def from_everyone(x, axis):
    count = lax.axis_size(axis)
    return lax.all_to_all(jnp.broadcast_to(x[None], (count, *x.shape)), axis, 0, 0, tiled=True)


def projected(bands, potential, eigenvectors):
    nx, ny, nz, nb = bands.shape
    gx, gyz = lax.axis_size("gx"), lax.axis_size("gyz")
    core = lax.rem(lax.axis_index("gx"), 2)
    odd = lax.rem(lax.axis_index("gyz"), 2)
    cells = nx * ny * nz
    scale = 1.0 / (cells * gyz)

    same, next_core, x_pairs = pairs_of(gx, gyz)
    partner = [(g, g ^ 1) for g in range(gx)]
    last = lax.slice_in_dim(bands, ny - 1, ny, axis=1)
    slab = lax.dynamic_slice_in_dim(bands, jnp.where(odd == 0, nx - 1, 0), 1, axis=0)
    yother = lax.ppermute(last, BOTH, next_core)
    yown = lax.ppermute(last, BOTH, same)
    xhalo = lax.ppermute(slab, BOTH, x_pairs)
    other = lax.ppermute(bands, "gx", partner)
    other_pot = lax.ppermute(potential, "gx", partner)

    coefficients = from_everyone(eigenvectors, "gyz").reshape(nb, nb)

    place = jnp.stack((core, odd)).astype(jnp.int32)
    gram = gram_partial(
        scale, place, bands, other, potential, other_pot, yown, yother, xhalo
    )
    gram_parts = to_rows(gram, "gyz")
    rotated = jnp.dot(
        bands.reshape(cells, nb), coefficients, preferred_element_type=F32
    ).astype(BF16)

    parts = from_everyone(gram_parts.astype(F32).sum(axis=0), "gx")
    sums = parts.reshape(gx // 2, 2, *parts.shape[1:]).sum(axis=0)
    return sums[0], sums[1], rotated.reshape(bands.shape)


def solution(mesh):
    in_specs = (P("gx", "gyz", None, None), P("gx", "gyz", None), P("gyz", None))
    out_specs = (P("gyz", None), P("gyz", None), P("gx", "gyz", None, None))
    return jax.shard_map(
        projected, mesh=mesh, in_specs=in_specs, out_specs=out_specs, check_vma=False
    )
```

time: 113 us -> 102 us (0.903)
  the two profiles are of different devices: /device:TPU:2 before, /device:TPU:1 now
where the time goes in v2:
time: 102 us
  starting transfers between devices  31.8 us (31%)
  blocking collectives  28.9 us (28%)
  waiting for transfers between devices  25.3 us (25%)
  Pallas kernels  6.51 us (6%)
  local copies, waits for them, and re-layouts  6.23 us (6%)
  matrix products  2.18 us (2%)
    all_to_all x1, blocking collectives, to_rows(): return lax.all_to_all(parts, axis, 0, 0, tiled=True)  28.9 us
    all_to_all x2, waiting for transfers between devices, from_everyone(): lax.all_to_all(jnp.broadcast_to(x[None], (count, *x.shape)), axis, 0, 0,...  23.1 us
    all_to_all x2, starting transfers between devices, from_everyone(): lax.all_to_all(jnp.broadcast_to(x[None], (count, *x.shape)), axis, 0, 0,...  16 us
    ppermute x1, starting transfers between devices, projected(): other = lax.ppermute(bands, 'gx', partner)  8.75 us
    pallas_call x1, Pallas kernels, gram_partial(): pl.pallas_call(functools.partial(gram_kernel, scale), out_shape=jax.Shape...  6.51 us
    ppermute x1, starting transfers between devices, projected(): xhalo = lax.ppermute(slab, BOTH, x_pairs)  3.18 us
    dot_general x1, matrix products, projected(): jnp.dot(bands.reshape(cells, nb), coefficients, preferred_element_type=F32)  2.18 us
    unnamed x7, local copies, waits for them, and re-layouts  2.17 us
  transfers between devices with their start and end apart: 7, of which 4 were waited for; matrix products, arithmetic and copies ran while one was open for 5% of the time, Pallas kernels for 0%

profile of v2, /device:TPU:1, one launch (start us, length us, event | category | flops | bytes accessed | tf_op | source)
XLA Modules:
  0.0 101.9 jit_solution(18382430222488698958)
XLA Ops:
  0.6 8.7 %collective-permute-start = (bf16[8,5,40,512]{3,2,1,0:T(8,128)(2,1)}, bf16[8,5,40,512]{3,2,1,0:T(8,128)(2,1)S(1)}, u32[]{:S(2)}, u32[]{:S(2)}) collective-permute-start(bf16[8,5,40,512]{3,2,1,0:T(8,128)(2,1)} %own_ref.1), channel_id=1, source_target_pairs={{0,64},{64,0},{128,192},{192,128},{256,320},{320,256},{384,448},{4... | collective-permute-start | bytes 4915208 | tf_op jit(solution)/shard_map/ppermute | solution.py:137
  9.4 1.0 slice.9
  10.4 1.3 %collective-permute-start.2 = (bf16[8,1,40,512]{3,2,1,0:T(8,128)(2,1)S(1)}, bf16[8,1,40,512]{3,2,1,0:T(8,128)(2,1)S(1)}, u32[]{:S(2)}, u32[]{:S(2)}) collective-permute-start(bf16[8,1,40,512]{3,2,1,0:T(8,128)(2,1)S(1)} %slice.9), channel_id=1, source_target_pairs={{64,65},{65,66},{66,67},{67,68},{68,69},{69,70},{70,71},{71,72},{7... | collective-permute-start | bytes 983048 | tf_op jit(solution)/shard_map/ppermute | solution.py:135
  11.7 0.7 collective-permute-start.3
  12.4 0.9 constant_dynamic-slice_fusion
  13.4 3.2 %collective-permute-start.4 = (bf16[1,5,40,512]{3,2,1,0:T(8,128)(2,1)S(1)}, bf16[1,5,40,512]{3,2,1,0:T(8,128)(2,1)S(1)}, u32[]{:S(2)}, u32[]{:S(2)}) collective-permute-start(bf16[1,5,40,512]{3,2,1,0:T(8,128)(2,1)S(1)} %constant_dynamic-slice_fusion), channel_id=1, source_target_pairs={{64,192},{129,65},{66,194},{131,67},{68,196},{133,69},{70,198},{13... | collective-permute-start | bytes 614408 | tf_op jit(solution)/shard_map/ppermute | solution.py:136
  16.5 0.7 copy.9.pot_ref
  17.3 1.9 %collective-permute-start.1 = (f32[8,5,40]{2,1,0:T(8,128)S(1)}, f32[8,5,40]{2,1,0:T(8,128)S(1)}, u32[]{:S(2)}, u32[]{:S(2)}) collective-permute-start(f32[8,5,40]{2,1,0:T(8,128)S(1)} %copy.9.pot_ref), channel_id=1, source_target_pairs={{0,64},{64,0},{128,192},{192,128},{256,320},{320,256},{384,448},{4... | collective-permute-start | bytes 19208 | tf_op jit(solution)/shard_map/ppermute | solution.py:138
  19.2 0.1 pad_add_fusion.place_ref
  19.3 1.1 %collective-permute-done.1.other_pot_ref = f32[8,5,40]{2,1,0:T(8,128)S(1)} collective-permute-done((f32[8,5,40]{2,1,0:T(8,128)S(1)}, f32[8,5,40]{2,1,0:T(8,128)S(1)}, u32[]{:S(2)}, u32[]{:S(2)}) %collective-permute-start.1) | collective-permute-done | bytes 6432 | tf_op jit(solution)/shard_map/ppermute | solution.py:138
  20.4 1.0 %collective-permute-done.4.xhalo_ref = bf16[1,5,40,512]{3,2,1,0:T(8,128)(2,1)S(1)} collective-permute-done((bf16[1,5,40,512]{3,2,1,0:T(8,128)(2,1)S(1)}, bf16[1,5,40,512]{3,2,1,0:T(8,128)(2,1)S(1)}, u32[]{:S(2)}, u32[]{:S(2)}) %collective-permute-start.4) | collective-permute-done | bytes 204832 | tf_op jit(solution)/shard_map/ppermute | solution.py:136
  21.4 1.4 %copy-done = bf16[8,5,40,512]{3,2,1,0:T(8,128)(2,1)S(1)} copy-done((bf16[8,5,40,512]{3,2,1,0:T(8,128)(2,1)S(1)}, bf16[8,5,40,512]{3,2,1,0:T(8,128)(2,1)}, u32[]{:S(2)}) %copy-start) | copy-done | bytes 1638424
  22.8 6.5 %gram.1 = bf16[512,512]{1,0:T(8,128)(2,1)S(1)} custom-call(s32[2]{0:T(128)S(1)} %pad_add_fusion.place_ref, bf16[8,5,40,512]{3,2,1,0:T(8,128)(2,1)S(1)} %copy-done, bf16[8,5,40,512]{3,2,1,0:T(8,128)(2,1)S(1)} %collective-permute-done.other_ref, f32[8,5,40]{2,1,0:T(8,128)S(1)} %copy.9.pot_ref, f32[8,5,40]{2,1,0:T(8,128)S(1)} %collective-permute-done.1.other_pot_ref, ...), custom_call_target="tpu_custom_call" | custom-call | flops 1677721600 | bytes 6553600 | tf_op jit(solution)/shard_map/gram/pallas_call | solution.py:79
  29.4 0.0 copy-start.1
  29.4 28.9 %all_to_all.15 = bf16[64,8,512]{2,1,0:T(8,128)(2,1)S(1)} all-to-all(bf16[64,8,512]{2,1,0:T(8,128)(2,1)S(1)} %bitcast.14), channel_id=1, replica_groups=mesh['gx'=8,'gyz'=64] {'gyz'}, dimensions={0} | all-to-all | bytes 1048576 | tf_op jit(solution)/shard_map/all_to_all | solution.py:114
  58.3 0.8 broadcast_in_dim.5
  59.1 5.3 %all-to-all-start.2 = ((bf16[64,8,512]{2,1,0:T(8,128)(2,1)}), bf16[64,8,512]{2,1,0:T(8,128)(2,1)S(1)}, u32[]{:S(2)}, u32[]{:S(2)}) async-start(bf16[64,8,512]{2,1,0:T(8,128)(2,1)} %broadcast_in_dim.5), calls=%async_computation.2 | async-start | bytes 1048576 | tf_op jit(solution)/shard_map/all_to_all | solution.py:119
  64.4 0.1 convert_reduce_fusion
  64.5 17.2 %all-to-all-done.2 = bf16[64,8,512]{2,1,0:T(8,128)(2,1)S(1)} async-done(((bf16[64,8,512]{2,1,0:T(8,128)(2,1)}), bf16[64,8,512]{2,1,0:T(8,128)(2,1)S(1)}, u32[]{:S(2)}, u32[]{:S(2)}) %all-to-all-start.2) | async-done | bytes 524320 | tf_op jit(solution)/shard_map/all_to_all | solution.py:119
  81.7 0.7 broadcast_in_dim.4
  82.4 10.7 %all-to-all-start.1 = ((f32[8,8,512]{2,1,0:T(8,128)}), f32[8,8,512]{2,1,0:T(8,128)S(1)}, u32[]{:S(2)}, u32[]{:S(2)}) async-start(f32[8,8,512]{2,1,0:T(8,128)} %broadcast_in_dim.4), calls=%async_computation.1 | async-start | bytes 262144 | tf_op jit(solution)/shard_map/all_to_all | solution.py:119
  93.1 2.2 %convolution_convert_fusion = bf16[1600,512]{1,0:T(8,128)(2,1)} fusion(bf16[1600,512]{1,0:T(8,128)(2,1)S(1)} %bitcast.15, bf16[64,8,512]{2,1,0:T(8,128)(2,1)S(1)} %all-to-all-done.2), kind=kOutput, calls=%fused_computation | convolution fusion | flops 839680000 | bytes 3801088 | tf_op jit(solution)/shard_map/dot_general | solution.py:147
  95.3 5.9 %all-to-all-done.1 = f32[8,8,512]{2,1,0:T(8,128)S(1)} async-done(((f32[8,8,512]{2,1,0:T(8,128)}), f32[8,8,512]{2,1,0:T(8,128)S(1)}, u32[]{:S(2)}, u32[]{:S(2)}) %all-to-all-start.1) | async-done | bytes 131104 | tf_op jit(solution)/shard_map/all_to_all | solution.py:119
  101.3 0.6 slice_bitcast_fusion
  (8 shorter events, 0.0 us)
Async XLA Ops:
  0.6 20.8 %collective-permute-start = (bf16[8,5,40,512]{3,2,1,0:T(8,128)(2,1)}, bf16[8,5,40,512]{3,2,1,0:T(8,128)(2,1)S(1)}, u32[]{:S(2)}, u32[]{:S(2)}) collective-permute-start(bf16[8,5,40,512]{3,2,1,0:T(8,128)(2,1)} %own_ref.1), channel_id=1, source_target_pairs={{0,64},{64,0},{128,192},{192,128},{256,320},{320,256},{384,448},{4... | collective-permute-start | bytes 4915208 | tf_op jit(solution)/shard_map/ppermute | solution.py:137
  10.4 11.0 %collective-permute-start.2 = (bf16[8,1,40,512]{3,2,1,0:T(8,128)(2,1)S(1)}, bf16[8,1,40,512]{3,2,1,0:T(8,128)(2,1)S(1)}, u32[]{:S(2)}, u32[]{:S(2)}) collective-permute-start(bf16[8,1,40,512]{3,2,1,0:T(8,128)(2,1)S(1)} %slice.9), channel_id=1, source_target_pairs={{64,65},{65,66},{66,67},{67,68},{68,69},{69,70},{70,71},{71,72},{7... | collective-permute-start | bytes 983048 | tf_op jit(solution)/shard_map/ppermute | solution.py:135
  11.7 9.7 %collective-permute-start.3 = (bf16[8,1,40,512]{3,2,1,0:T(8,128)(2,1)S(1)}, bf16[8,1,40,512]{3,2,1,0:T(8,128)(2,1)S(1)}, u32[]{:S(2)}, u32[]{:S(2)}) collective-permute-start(bf16[8,1,40,512]{3,2,1,0:T(8,128)(2,1)S(1)} %slice.9), channel_id=1, source_target_pairs={{0,65},{1,66},{2,67},{3,68},{4,69},{5,70},{6,71},{7,72},{8,73},{9,... | collective-permute-start | bytes 983048 | tf_op jit(solution)/shard_map/ppermute | solution.py:134
  13.4 8.0 %collective-permute-start.4 = (bf16[1,5,40,512]{3,2,1,0:T(8,128)(2,1)S(1)}, bf16[1,5,40,512]{3,2,1,0:T(8,128)(2,1)S(1)}, u32[]{:S(2)}, u32[]{:S(2)}) collective-permute-start(bf16[1,5,40,512]{3,2,1,0:T(8,128)(2,1)S(1)} %constant_dynamic-slice_fusion), channel_id=1, source_target_pairs={{64,192},{129,65},{66,194},{131,67},{68,196},{133,69},{70,198},{13... | collective-permute-start | bytes 614408 | tf_op jit(solution)/shard_map/ppermute | solution.py:136
  17.3 3.1 %collective-permute-start.1 = (f32[8,5,40]{2,1,0:T(8,128)S(1)}, f32[8,5,40]{2,1,0:T(8,128)S(1)}, u32[]{:S(2)}, u32[]{:S(2)}) collective-permute-start(f32[8,5,40]{2,1,0:T(8,128)S(1)} %copy.9.pot_ref), channel_id=1, source_target_pairs={{0,64},{64,0},{128,192},{192,128},{256,320},{320,256},{384,448},{4... | collective-permute-start | bytes 19208 | tf_op jit(solution)/shard_map/ppermute | solution.py:138
  21.4 1.4 %copy-start = (bf16[8,5,40,512]{3,2,1,0:T(8,128)(2,1)S(1)}, bf16[8,5,40,512]{3,2,1,0:T(8,128)(2,1)}, u32[]{:S(2)}) copy-start(bf16[8,5,40,512]{3,2,1,0:T(8,128)(2,1)} %own_ref.1) | copy-start | bytes 4915204
  22.8 35.5 %copy-start.2 = (bf16[8,512]{1,0:T(8,128)(2,1)S(1)}, bf16[8,512]{1,0:T(8,128)(2,1)}, u32[]{:S(2)}) copy-start(bf16[8,512]{1,0:T(8,128)(2,1)} %param.5) | copy-start | bytes 24580
  29.4 63.8 %copy-start.1 = (bf16[8,5,40,512]{3,2,1,0:T(8,128)(2,1)S(1)}, bf16[8,5,40,512]{3,2,1,0:T(8,128)(2,1)}, u32[]{:S(2)}) copy-start(bf16[8,5,40,512]{3,2,1,0:T(8,128)(2,1)} %own_ref.1) | copy-start | bytes 4915204
  59.1 22.6 %all-to-all-start.2 = ((bf16[64,8,512]{2,1,0:T(8,128)(2,1)}), bf16[64,8,512]{2,1,0:T(8,128)(2,1)S(1)}, u32[]{:S(2)}, u32[]{:S(2)}) async-start(bf16[64,8,512]{2,1,0:T(8,128)(2,1)} %broadcast_in_dim.5), calls=%async_computation.2 | async-start | bytes 1048576 | tf_op jit(solution)/shard_map/all_to_all | solution.py:119
  82.4 18.8 %all-to-all-start.1 = ((f32[8,8,512]{2,1,0:T(8,128)}), f32[8,8,512]{2,1,0:T(8,128)S(1)}, u32[]{:S(2)}, u32[]{:S(2)}) async-start(f32[8,8,512]{2,1,0:T(8,128)} %broadcast_in_dim.4), calls=%async_computation.1 | async-start | bytes 262144 | tf_op jit(solution)/shard_map/all_to_all | solution.py:119

commit v3 on v2

v3 whole, which is shorter than its diff:
```python
import functools

import jax
import jax.numpy as jnp
from jax import lax
from jax.experimental import pallas as pl
from jax.experimental.pallas import tpu as pltpu
from jax.sharding import PartitionSpec as P


F32 = jnp.float32
BF16 = jnp.bfloat16
BOTH = ("gx", "gyz")
PIECES = 3

VMEM = pl.BlockSpec(memory_space=pltpu.VMEM)
SMEM = pl.BlockSpec(memory_space=pltpu.SMEM)


def over_rows(a, b):
    return lax.dot_general(a, b, (((0,), (0,)), ((), ())), preferred_element_type=F32)


def call(kernel, out_shape, in_specs, args, scratch=(), flops=0):
    many = isinstance(out_shape, tuple)
    moved = sum(a.size * a.dtype.itemsize for a in args)
    return pl.pallas_call(
        kernel,
        out_shape=out_shape,
        in_specs=in_specs,
        out_specs=(VMEM,) * len(out_shape) if many else VMEM,
        scratch_shapes=list(scratch),
        cost_estimate=pl.CostEstimate(flops=flops, bytes_accessed=moved, transcendentals=0),
        compiler_params=pltpu.CompilerParams(vmem_limit_bytes=20 << 20),
    )(*args)


def prepare_kernel(place_ref, bands_ref, pot_ref, held_ref, last_ref, slab_ref, sems):
    nx, ny, nz, _ = bands_ref.shape
    sent = jnp.where(place_ref[1] == 0, nx - 1, 0)
    copies = (
        pltpu.make_async_copy(bands_ref.at[:, ny - 1], last_ref, sems.at[0]),
        pltpu.make_async_copy(bands_ref.at[sent], slab_ref, sems.at[1]),
        pltpu.make_async_copy(bands_ref, held_ref.at[pl.ds(0, nx)], sems.at[2]),
    )
    for copy in copies:
        copy.start()
    rest = pot_ref[...].reshape(nx * ny, nz)
    for piece in range(PIECES):
        part = rest.astype(BF16)
        held_ref[nx, piece, 0 : nx * ny, 0:nz] = part
        rest = rest - part.astype(F32)
    for copy in copies:
        copy.wait()


def prepare(place, bands, pot):
    nx, ny, nz, nb = bands.shape
    assert ny >= PIECES and nx * ny <= nz <= nb
    shapes = ((nx + 1, ny, nz, nb), (nx, nz, nb), (ny, nz, nb))
    return call(
        prepare_kernel,
        tuple(jax.ShapeDtypeStruct(s, BF16) for s in shapes),
        [SMEM, pl.BlockSpec(memory_space=pltpu.HBM), VMEM],
        (place, bands, pot),
        scratch=[pltpu.SemaphoreType.DMA((3,))],
    )


def half_stencil(core, planes, pots, outs):
    nx, ny, nz, nb = outs[0].shape
    row = lax.broadcasted_iota(jnp.int32, (nz, nb), 0)
    half = jnp.where(core == 1, 0.5, 0.0).astype(F32)

    def tiles_at(ref, x):
        return [ref[x, y].astype(F32) for y in range(ny)]

    def one(ref, pot_ref, out_ref, x, below):
        pot = jnp.transpose(pot_ref[:, pl.ds(x, 1), :].reshape(ny, nz))
        factor = 0.5 + half * (2.0 + pot)
        tiles = tiles_at(ref, x)
        for y in range(ny):
            total = jnp.where(row > 0, pltpu.roll(tiles[y], 1, 0), 0.0)
            if y > 0:
                total += tiles[y - 1]
            if below is not None:
                total += below[y]
            out_ref[x, y] = (factor[:, y : y + 1] * tiles[y] - half * total).astype(BF16)

    low, high = planes
    one(low, pots[0], outs[0], 0, None)
    one(high, pots[1], outs[1], 0, tiles_at(low, nx - 1))

    def step(x, carry):
        for ref, pot, out in zip(planes, pots, outs):
            one(ref, pot, out, x, tiles_at(ref, x - 1))
        return carry

    lax.fori_loop(1, nx, step, 0)


def local_kernel(place_ref, own_ref, other_ref, pot_ref, gram_ref, other_pot, right_own, right_other):
    nx, ny, nz, nb = right_own.shape
    pieces = [other_ref[nx, p, 0 : nx * ny, 0:nz].astype(F32) for p in range(PIECES)]
    other_pot[...] = ((pieces[2] + pieces[1]) + pieces[0]).reshape(ny, nx, nz)
    half_stencil(
        place_ref[0], (other_ref, own_ref), (other_pot, pot_ref), (right_other, right_own)
    )

    def rows(ref):
        return ref[0:nx].reshape(-1, nb)

    gram_ref[...] = over_rows(rows(own_ref), rows(right_own)) + over_rows(
        rows(other_ref), rows(right_other)
    )


def local_gram(place, own, other, pot, shape):
    nx, ny, nz, nb = shape
    return call(
        local_kernel,
        jax.ShapeDtypeStruct((nb, nb), F32),
        [SMEM, VMEM, VMEM, VMEM],
        (place, own, other, pot),
        scratch=[pltpu.VMEM(pot.shape, F32)] + [pltpu.VMEM(shape, BF16)] * 2,
        flops=4 * nx * ny * nz * nb * nb,
    )


def cross_kernel(
    scale, place_ref, gram_ref, own_ref, other_ref, yown_ref, yother_ref, xhalo_ref, coef_ref, out_ref
):
    _, _, nb = xhalo_ref.shape
    nx = yown_ref.shape[0]
    groups, depth = out_ref.shape[0], coef_ref.shape[0]

    def rows(value):
        return value.reshape(-1, nb)

    cross = over_rows(rows(own_ref[0:nx, 0]), rows(yown_ref[...]))
    cross += over_rows(rows(other_ref[0:nx, 0]), rows(yother_ref[...]))
    slab = jnp.where(place_ref[1] == 0, other_ref[0], own_ref[nx - 1])
    cross += over_rows(rows(slab), rows(xhalo_ref[...]))
    gram = gram_ref[...] - 0.5 * cross
    total = (scale * (gram + jnp.transpose(gram))).astype(BF16)
    total = total.reshape(nb // (groups * depth), groups, depth, nb)
    for d in range(groups):
        out_ref[d, 0 : nb // groups] = rows(total[:, d])
        out_ref[d, nb // groups :] = coef_ref[...]


def add_cross(scale, groups, place, gram, own, other, yown, yother, xhalo, coef):
    nb = gram.shape[0]
    depth = coef.shape[0]
    halo_rows = (yown.size + yother.size + xhalo.size) // nb
    return call(
        functools.partial(cross_kernel, scale),
        jax.ShapeDtypeStruct((groups, nb // groups + depth, nb), BF16),
        [SMEM] + [VMEM] * 7,
        (place, gram, own, other, yown, yother, xhalo, coef),
        flops=2 * halo_rows * nb * nb,
    )


def middle_kernel(place_ref, in_ref, out_ref):
    sources, height, nb = in_ref.shape
    targets, _, _ = out_ref.shape
    depth = (height * targets - nb * targets // sources) // targets
    width = nb // 2
    total = in_ref[0, 0 : height - depth].astype(F32)
    for s in range(1, sources):
        total += in_ref[s, 0 : height - depth].astype(F32)
    total = total.astype(BF16).reshape(targets, depth, nb)
    upper = sources // 2
    for s in range(sources):
        coef = in_ref[s, height - depth :]
        coef = jnp.where(place_ref[0] == 0, coef[:, :width], coef[:, width:])
        first = depth + (s % upper) * depth
        lane = (s // upper) * width
        for t in range(targets):
            out_ref[t, first : first + depth, lane : lane + width] = coef
    for t in range(targets):
        out_ref[t, 0:depth] = total[t]


def middle(place, arrived, targets):
    sources, height, nb = arrived.shape
    depth = height - nb // sources
    return call(
        middle_kernel,
        jax.ShapeDtypeStruct((targets, depth + sources * depth // 2, nb), BF16),
        [SMEM, VMEM],
        (place, arrived),
    )


def last_kernel(in_ref, rows_ref, coef_ref):
    sources, height, nb = in_ref.shape
    copies, depth, _ = rows_ref.shape
    total = in_ref[0, 0:depth].astype(F32)
    for s in range(1, sources):
        total += in_ref[s, 0:depth].astype(F32)
    for c in range(copies):
        rows_ref[c] = total
    plane = 2 * (height - depth)
    for s in range(sources):
        for part in range(2):
            start = s * plane + part * (plane // 2)
            coef_ref[start : start + plane // 2] = in_ref[
                s, depth:, part * (nb // 2) : (part + 1) * (nb // 2)
            ]


def finish(arrived, copies, depth):
    _, _, nb = arrived.shape
    return call(
        last_kernel,
        (
            jax.ShapeDtypeStruct((copies, depth, nb), F32),
            jax.ShapeDtypeStruct((nb, nb // 2), BF16),
        ),
        [VMEM],
        (arrived,),
    )


def pairs_of(gx, gyz):
    def at(g, r):
        return g * gyz + r

    same, next_core, x = [], [], []
    for chip in range(gx // 2):
        for r in range(gyz - 1):
            same.append((at(2 * chip + 1, r), at(2 * chip + 1, r + 1)))
            next_core.append((at(2 * chip, r), at(2 * chip + 1, r + 1)))
    for chip in range(gx // 2 - 1):
        for r in range(gyz):
            if r % 2 == 0:
                x.append((at(2 * chip + 1, r), at(2 * chip + 3, r)))
            else:
                x.append((at(2 * chip + 2, r), at(2 * chip + 1, r)))
    return same, next_core, x


def exchanged(x, axis, groups=None):
    return lax.all_to_all(x, axis, 0, 0, tiled=True, axis_index_groups=groups)


def projected(bands, potential, eigenvectors):
    nx, ny, nz, nb = bands.shape
    gx, gyz = lax.axis_size("gx"), lax.axis_size("gyz")
    depth = eigenvectors.shape[0]
    inner = 8
    outer = gyz // inner
    core = lax.rem(lax.axis_index("gx"), 2)
    odd = lax.rem(lax.axis_index("gyz"), 2)
    cells = nx * ny * nz
    scale = 1.0 / (cells * gyz)
    place = jnp.stack((core, odd)).astype(jnp.int32)
    pot = jnp.transpose(potential, (1, 0, 2))

    own, last, slab = prepare(place, bands, pot)
    same, next_core, x_pairs = pairs_of(gx, gyz)
    partner = [(g, g ^ 1) for g in range(gx)]
    yother = lax.ppermute(last, BOTH, next_core)
    yown = lax.ppermute(last, BOTH, same)
    xhalo = lax.ppermute(slab, BOTH, x_pairs)
    other = lax.ppermute(own, "gx", partner)

    gram = local_gram(place, own, other, pot, bands.shape)
    sent = add_cross(
        scale, inner, place, gram, own, other, yown, yother, xhalo, eigenvectors
    )
    arrived = exchanged(sent, "gyz", [[o * inner + i for i in range(inner)] for o in range(outer)])
    sent = middle(place, arrived, outer)
    arrived = exchanged(sent, "gyz", [[o * inner + i for o in range(outer)] for i in range(inner)])
    rows, coef = finish(arrived, gx, depth)
    coef_other = lax.ppermute(coef, "gx", partner)
    parts = exchanged(rows, "gx")
    sums = parts.reshape(gx // 2, 2, *parts.shape[1:]).sum(axis=0)

    left = jnp.where(core == 0, coef, coef_other)
    right = jnp.where(core == 0, coef_other, coef)
    rotated = jnp.dot(
        bands.reshape(cells, nb),
        jnp.concatenate((left, right), axis=1),
        preferred_element_type=F32,
    ).astype(BF16)
    return sums[0], sums[1], rotated.reshape(bands.shape)


def solution(mesh):
    in_specs = (P("gx", "gyz", None, None), P("gx", "gyz", None), P("gyz", None))
    out_specs = (P("gyz", None), P("gyz", None), P("gx", "gyz", None, None))
    return jax.shard_map(
        projected, mesh=mesh, in_specs=in_specs, out_specs=out_specs, check_vma=False
    )
```

time: 102 us -> 84.1 us (0.82)
  waiting for transfers between devices: 25.3 us -> 6.19 us
  local copies, waits for them, and re-layouts: 6.23 us -> 2.78 us
  Pallas kernels: 6.51 us -> 9.46 us
  blocking collectives: 28.9 us -> 31.6 us
  starting transfers between devices: 31.8 us -> 30.5 us
    all_to_all x2 -> x1, waiting for transfers between devices: 23.1 us -> 6.18 us  [exchanged(): return lax.all_to_all(x, axis, 0, 0, tiled=True, axis_index_groups=groups)]
    pallas_call x1 -> x5, Pallas kernels: 6.51 us -> 9.46 us  [call(): pl.pallas_call(kernel, out_shape=out_shape, in_specs=in_specs, out_specs=...]
    all_to_all x1 -> x2, blocking collectives: 28.9 us -> 31.6 us  [exchanged(): return lax.all_to_all(x, axis, 0, 0, tiled=True, axis_index_groups=groups)]
    all_to_all x2 -> x1, starting transfers between devices: 16 us -> 14.1 us  [exchanged(): return lax.all_to_all(x, axis, 0, 0, tiled=True, axis_index_groups=groups)]
    broadcast_in_dim x2 -> x0, local copies, waits for them, and re-layouts: 1.49 us -> none  [from_everyone(): jnp.broadcast_to(x[None], (count, *x.shape))]
    ppermute x2, waiting for transfers between devices: 1.09 us -> 0.01 us  [the longest x1 0.01 us: projected(): other = lax.ppermute(own, 'gx', partner)]
    ppermute x1, waiting for transfers between devices: 1.02 us -> 0.01 us  [projected(): xhalo = lax.ppermute(slab, BOTH, x_pairs)]
    unnamed x7 -> x8, local copies, waits for them, and re-layouts: 2.17 us -> 2.17 us
  transfers between devices with their start and end apart: 7 -> 6, of which waited for: 4 -> 1; matrix products, arithmetic and copies ran while one was open for 5% -> 1% of each run, Pallas kernels for 0% -> 7%
where the time goes in v3:
time: 84.1 us; the launch traced here: 83.6 us
  blocking collectives  31.6 us (38%)
  starting transfers between devices  30.5 us (36%)
  Pallas kernels  9.46 us (11%)
  waiting for transfers between devices  6.19 us (7%)
  local copies, waits for them, and re-layouts  2.78 us (3%)
  matrix products  2.18 us (3%)
    all_to_all x2, blocking collectives, exchanged(): return lax.all_to_all(x, axis, 0, 0, tiled=True, axis_index_groups=groups)  31.6 us
    all_to_all x1, starting transfers between devices, exchanged(): return lax.all_to_all(x, axis, 0, 0, tiled=True, axis_index_groups=groups)  14.1 us
    pallas_call x5, Pallas kernels, call(): pl.pallas_call(kernel, out_shape=out_shape, in_specs=in_specs, out_specs=...  9.46 us
    ppermute x1, starting transfers between devices, projected(): other = lax.ppermute(own, 'gx', partner)  8.75 us
    all_to_all x1, waiting for transfers between devices, exchanged(): return lax.all_to_all(x, axis, 0, 0, tiled=True, axis_index_groups=groups)  6.18 us
    ppermute x1, starting transfers between devices, projected(): xhalo = lax.ppermute(slab, BOTH, x_pairs)  3.79 us
    dot_general x1, matrix products, projected(): jnp.dot(bands.reshape(cells, nb), jnp.concatenate((left, right), axis=1),...  2.18 us
    unnamed x8, local copies, waits for them, and re-layouts  2.17 us
  transfers between devices with their start and end apart: 6, of which 1 were waited for; matrix products, arithmetic and copies ran while one was open for 1% of the time, Pallas kernels for 7%

profile of v3, /device:TPU:1, one launch (start us, length us, event | category | flops | bytes accessed | tf_op | source)
XLA Modules:
  0.0 83.6 jit_solution(1542122610138192751)
XLA Ops:
  0.6 0.1 pad_add_fusion.place_ref
  0.7 1.4 %copy-done = bf16[8,5,40,512]{3,2,1,0:T(8,128)(2,1)S(1)} copy-done((bf16[8,5,40,512]{3,2,1,0:T(8,128)(2,1)S(1)}, bf16[8,5,40,512]{3,2,1,0:T(8,128)(2,1)}, u32[]{:S(2)}) %copy-start) | copy-done | bytes 1638424
  2.1 0.7 copy-done.2
  2.9 1.1 %shard_map.58 = (bf16[9,5,40,512]{3,2,1,0:T(8,128)(2,1)S(1)}, bf16[8,40,512]{2,1,0:T(8,128)(2,1)S(1)}, bf16[5,40,512]{2,1,0:T(8,128)(2,1)S(1)}) custom-call(s32[2]{0:T(128)S(1)} %pad_add_fusion.place_ref, bf16[8,5,40,512]{3,2,1,0:T(8,128)(2,1)S(1)} %copy-done, f32[5,8,40]{2,1,0:T(8,128)S(1)} %bitcast.14), custom_call_target="tpu_custom_call" | custom-call | bytes 1644808 | tf_op jit(solution)/shard_map/pallas_call | solution.py:27
  3.9 8.7 %collective-permute-start = (bf16[9,5,40,512]{3,2,1,0:T(8,128)(2,1)S(1)}, bf16[9,5,40,512]{3,2,1,0:T(8,128)(2,1)S(1)}, u32[]{:S(2)}, u32[]{:S(2)}) collective-permute-start(bf16[9,5,40,512]{3,2,1,0:T(8,128)(2,1)S(1)} %get-tuple-element.8.own_ref), channel_id=1, source_target_pairs={{0,64},{64,0},{128,192},{192,128},{256,320},{320,256},{384,448},{4... | collective-permute-start | bytes 5529608 | tf_op jit(solution)/shard_map/ppermute | solution.py:268
  12.7 0.7 collective-permute-start.2
  13.4 1.3 %collective-permute-start.1 = (bf16[8,40,512]{2,1,0:T(8,128)(2,1)S(1)}, bf16[8,40,512]{2,1,0:T(8,128)(2,1)S(1)}, u32[]{:S(2)}, u32[]{:S(2)}) collective-permute-start(bf16[8,40,512]{2,1,0:T(8,128)(2,1)S(1)} %get-tuple-element.9), channel_id=1, source_target_pairs={{64,65},{65,66},{66,67},{67,68},{68,69},{69,70},{70,71},{71,72},{7... | collective-permute-start | bytes 983048 | tf_op jit(solution)/shard_map/ppermute | solution.py:266
  14.7 0.0 copy-start.3
  14.7 3.8 %collective-permute-start.3 = (bf16[5,40,512]{2,1,0:T(8,128)(2,1)S(1)}, bf16[5,40,512]{2,1,0:T(8,128)(2,1)S(1)}, u32[]{:S(2)}, u32[]{:S(2)}) collective-permute-start(bf16[5,40,512]{2,1,0:T(8,128)(2,1)S(1)} %get-tuple-element.10), channel_id=1, source_target_pairs={{64,192},{129,65},{66,194},{131,67},{68,196},{133,69},{70,198},{13... | collective-permute-start | bytes 614408 | tf_op jit(solution)/shard_map/ppermute | solution.py:267
  18.5 0.0 collective-permute-done.other_ref
  18.5 5.4 %shard_map.59.gram_ref = f32[512,512]{1,0:T(8,128)S(1)} custom-call(s32[2]{0:T(128)S(1)} %pad_add_fusion.place_ref, bf16[9,5,40,512]{3,2,1,0:T(8,128)(2,1)S(1)} %get-tuple-element.8.own_ref, bf16[9,5,40,512]{3,2,1,0:T(8,128)(2,1)S(1)} %collective-permute-done.other_ref, f32[5,8,40]{2,1,0:T(8,128)S(1)} %bitcast.15), custom_call_target="tpu_custom_call" | custom-call | flops 1677721600 | bytes 3692808 | tf_op jit(solution)/shard_map/pallas_call | solution.py:27
  24.0 0.0 collective-permute-done.3.xhalo_ref
  24.0 0.0 collective-permute-done.2.yother_ref
  24.0 0.0 collective-permute-done.1.yown_ref
  24.0 1.6 %shard_map.60 = bf16[8,72,512]{2,1,0:T(8,128)(2,1)S(1)} custom-call(s32[2]{0:T(128)S(1)} %pad_add_fusion.place_ref, f32[512,512]{1,0:T(8,128)S(1)} %shard_map.59.gram_ref, bf16[9,5,40,512]{3,2,1,0:T(8,128)(2,1)S(1)} %get-tuple-element.8.own_ref, bf16[9,5,40,512]{3,2,1,0:T(8,128)(2,1)S(1)} %collective-permute-done.other_ref, ...), custom_call_target="tpu_custom_call" | custom-call | flops 440401920 | bytes 5603336 | tf_op jit(solution)/shard_map/pallas_call | solution.py:27
  25.7 13.5 %all_to_all.15.in_ref = bf16[8,72,512]{2,1,0:T(8,128)(2,1)S(1)} all-to-all(bf16[8,72,512]{2,1,0:T(8,128)(2,1)S(1)} %shard_map.60), channel_id=1, replica_groups={{0,1,2,3,4,5,6,7},{8,9,10,11,12,13,14,15},{16,17,18,19,20,21,22,23},{24..., dimensions={0} | all-to-all | bytes 1179648 | tf_op jit(solution)/shard_map/all_to_all | solution.py:246
  39.2 0.6 shard_map.61
  39.8 18.1 %all_to_all.16.in_ref = bf16[8,40,512]{2,1,0:T(8,128)(2,1)S(1)} all-to-all(bf16[8,40,512]{2,1,0:T(8,128)(2,1)S(1)} %shard_map.61), channel_id=1, replica_groups={{0,8,16,24,32,40,48,56},{1,9,17,25,33,41,49,57},{2,10,18,26,34,42,50,58..., dimensions={0} | all-to-all | bytes 655360 | tf_op jit(solution)/shard_map/all_to_all | solution.py:246
  57.9 0.7 shard_map.62
  58.6 14.1 %all-to-all-start.2 = ((f32[8,8,512]{2,1,0:T(8,128)}), f32[8,8,512]{2,1,0:T(8,128)S(1)}, u32[]{:S(2)}, u32[]{:S(2)}) async-start(f32[8,8,512]{2,1,0:T(8,128)} %get-tuple-element.11), calls=%async_computation.2 | async-start | bytes 262144 | tf_op jit(solution)/shard_map/all_to_all | solution.py:246
  72.7 1.9 %collective-permute-start.4 = (bf16[512,256]{1,0:T(8,128)(2,1)S(1)}, bf16[512,256]{1,0:T(8,128)(2,1)S(1)}, u32[]{:S(2)}, u32[]{:S(2)}) collective-permute-start(bf16[512,256]{1,0:T(8,128)(2,1)S(1)} %get-tuple-element.12), channel_id=1, source_target_pairs={{0,64},{64,0},{128,192},{192,128},{256,320},{320,256},{384,448},{4... | collective-permute-start | bytes 786440 | tf_op jit(solution)/shard_map/ppermute | solution.py:278
  74.6 6.2 %all-to-all-done.2 = f32[8,8,512]{2,1,0:T(8,128)S(1)} async-done(((f32[8,8,512]{2,1,0:T(8,128)}), f32[8,8,512]{2,1,0:T(8,128)S(1)}, u32[]{:S(2)}, u32[]{:S(2)}) %all-to-all-start.2) | async-done | bytes 131104 | tf_op jit(solution)/shard_map/all_to_all | solution.py:246
  80.8 0.6 slice_bitcast_fusion
  81.4 2.2 %convolution_convert_fusion = bf16[512,1600]{0,1:T(8,128)(2,1)} fusion(bf16[1600,512]{1,0:T(8,128)(2,1)S(1)} %bitcast.13, bf16[512,256]{1,0:T(8,128)(2,1)S(1)} %get-tuple-element.14, bf16[512,256]{1,0:T(8,128)(2,1)S(1)} %get-tuple-element.13), kind=kOutput, calls=%fused_computation | convolution fusion | flops 840728576 | bytes 3801088 | tf_op jit(solution)/shard_map/dot_general | solution.py:284
  (8 shorter events, 0.1 us)
Async XLA Ops:
  0.7 1.4 %copy-start = (bf16[8,5,40,512]{3,2,1,0:T(8,128)(2,1)S(1)}, bf16[8,5,40,512]{3,2,1,0:T(8,128)(2,1)}, u32[]{:S(2)}) copy-start(bf16[8,5,40,512]{3,2,1,0:T(8,128)(2,1)} %bands_ref.1) | copy-start | bytes 4915204
  2.1 0.7 copy-start.2
  3.9 14.6 %collective-permute-start = (bf16[9,5,40,512]{3,2,1,0:T(8,128)(2,1)S(1)}, bf16[9,5,40,512]{3,2,1,0:T(8,128)(2,1)S(1)}, u32[]{:S(2)}, u32[]{:S(2)}) collective-permute-start(bf16[9,5,40,512]{3,2,1,0:T(8,128)(2,1)S(1)} %get-tuple-element.8.own_ref), channel_id=1, source_target_pairs={{0,64},{64,0},{128,192},{192,128},{256,320},{320,256},{384,448},{4... | collective-permute-start | bytes 5529608 | tf_op jit(solution)/shard_map/ppermute | solution.py:268
  12.7 11.3 %collective-permute-start.2 = (bf16[8,40,512]{2,1,0:T(8,128)(2,1)S(1)}, bf16[8,40,512]{2,1,0:T(8,128)(2,1)S(1)}, u32[]{:S(2)}, u32[]{:S(2)}) collective-permute-start(bf16[8,40,512]{2,1,0:T(8,128)(2,1)S(1)} %get-tuple-element.9), channel_id=1, source_target_pairs={{0,65},{1,66},{2,67},{3,68},{4,69},{5,70},{6,71},{7,72},{8,73},{9,... | collective-permute-start | bytes 983048 | tf_op jit(solution)/shard_map/ppermute | solution.py:265
  13.4 10.6 %collective-permute-start.1 = (bf16[8,40,512]{2,1,0:T(8,128)(2,1)S(1)}, bf16[8,40,512]{2,1,0:T(8,128)(2,1)S(1)}, u32[]{:S(2)}, u32[]{:S(2)}) collective-permute-start(bf16[8,40,512]{2,1,0:T(8,128)(2,1)S(1)} %get-tuple-element.9), channel_id=1, source_target_pairs={{64,65},{65,66},{66,67},{67,68},{68,69},{69,70},{70,71},{71,72},{7... | collective-permute-start | bytes 983048 | tf_op jit(solution)/shard_map/ppermute | solution.py:266
  14.7 9.3 %copy-start.3 = (bf16[8,512]{1,0:T(8,128)(2,1)S(1)}, bf16[8,512]{1,0:T(8,128)(2,1)}, u32[]{:S(2)}) copy-start(bf16[8,512]{1,0:T(8,128)(2,1)} %coef_ref.1) | copy-start | bytes 24580
  14.7 9.3 %collective-permute-start.3 = (bf16[5,40,512]{2,1,0:T(8,128)(2,1)S(1)}, bf16[5,40,512]{2,1,0:T(8,128)(2,1)S(1)}, u32[]{:S(2)}, u32[]{:S(2)}) collective-permute-start(bf16[5,40,512]{2,1,0:T(8,128)(2,1)S(1)} %get-tuple-element.10), channel_id=1, source_target_pairs={{64,192},{129,65},{66,194},{131,67},{68,196},{133,69},{70,198},{13... | collective-permute-start | bytes 614408 | tf_op jit(solution)/shard_map/ppermute | solution.py:267
  39.2 42.2 %copy-start.1 = (bf16[8,5,40,512]{3,2,1,0:T(8,128)(2,1)S(1)}, bf16[8,5,40,512]{3,2,1,0:T(8,128)(2,1)}, u32[]{:S(2)}) copy-start(bf16[8,5,40,512]{3,2,1,0:T(8,128)(2,1)} %bands_ref.1) | copy-start | bytes 4915204
  58.6 22.2 %all-to-all-start.2 = ((f32[8,8,512]{2,1,0:T(8,128)}), f32[8,8,512]{2,1,0:T(8,128)S(1)}, u32[]{:S(2)}, u32[]{:S(2)}) async-start(f32[8,8,512]{2,1,0:T(8,128)} %get-tuple-element.11), calls=%async_computation.2 | async-start | bytes 262144 | tf_op jit(solution)/shard_map/all_to_all | solution.py:246
  72.7 8.7 %collective-permute-start.4 = (bf16[512,256]{1,0:T(8,128)(2,1)S(1)}, bf16[512,256]{1,0:T(8,128)(2,1)S(1)}, u32[]{:S(2)}, u32[]{:S(2)}) collective-permute-start(bf16[512,256]{1,0:T(8,128)(2,1)S(1)} %get-tuple-element.12), channel_id=1, source_target_pairs={{0,64},{64,0},{128,192},{192,128},{256,320},{320,256},{384,448},{4... | collective-permute-start | bytes 786440 | tf_op jit(solution)/shard_map/ppermute | solution.py:278

commit v4 on v3

v4 whole, which is shorter than its diff:
```python
import functools

import jax
import jax.numpy as jnp
from jax import lax
from jax.experimental import pallas as pl
from jax.experimental.pallas import tpu as pltpu
from jax.sharding import PartitionSpec as P


F32 = jnp.float32
BF16 = jnp.bfloat16
BOTH = ("gx", "gyz")
PIECES = 3

VMEM = pl.BlockSpec(memory_space=pltpu.VMEM)
SMEM = pl.BlockSpec(memory_space=pltpu.SMEM)


def over_rows(a, b):
    return lax.dot_general(a, b, (((0,), (0,)), ((), ())), preferred_element_type=F32)


def call(kernel, out_shape, in_specs, args, scratch=(), flops=0):
    many = isinstance(out_shape, tuple)
    moved = sum(a.size * a.dtype.itemsize for a in args)
    return pl.pallas_call(
        kernel,
        out_shape=out_shape,
        in_specs=in_specs,
        out_specs=(VMEM,) * len(out_shape) if many else VMEM,
        scratch_shapes=list(scratch),
        cost_estimate=pl.CostEstimate(flops=flops, bytes_accessed=moved, transcendentals=0),
        compiler_params=pltpu.CompilerParams(vmem_limit_bytes=20 << 20),
    )(*args)


def half_kernel(place_ref, bands_ref, pot_ref, *refs):
    nx, ny, nz, nb = bands_ref.shape
    right_ref, gram_ref = refs[-1], refs[-2]
    row = lax.broadcasted_iota(jnp.int32, (nz, nb), 0)
    half = jnp.where(place_ref[0] == 1, 0.5, 0.0).astype(F32)

    def slab(x, below):
        pot = jnp.transpose(pot_ref[:, pl.ds(x, 1), :].reshape(ny, nz))
        factor = 0.5 + half * (2.0 + pot)
        tiles = [bands_ref[x, y].astype(F32) for y in range(ny)]
        for y in range(ny):
            total = jnp.where(row > 0, pltpu.roll(tiles[y], 1, 0), 0.0)
            if y > 0:
                total += tiles[y - 1]
            if below is not None:
                total += below[y]
            right_ref[x, y] = (factor[:, y : y + 1] * tiles[y] - half * total).astype(BF16)
        return tiles

    lax.fori_loop(1, nx, lambda x, below: slab(x, below), slab(0, None))
    gram = over_rows(bands_ref[...].reshape(-1, nb), right_ref[...].reshape(-1, nb))
    if len(refs) > 2:
        gram += refs[0][...]
    gram_ref[...] = gram


def half_gram(place, bands, pot, given=()):
    nb = bands.shape[-1]
    return call(
        half_kernel,
        jax.ShapeDtypeStruct((nb, nb), F32),
        [SMEM] + [VMEM] * (2 + len(given)),
        (place, bands, pot, *given),
        scratch=[pltpu.VMEM(bands.shape, BF16)],
        flops=2 * bands.size * nb,
    )


def cross_kernel(
    scale, place_ref, gram_ref, own_ref, other_ref, yown_ref, yother_ref, xhalo_ref, coef_ref, out_ref
):
    _, _, nb = xhalo_ref.shape
    nx = yown_ref.shape[0]
    groups, depth = out_ref.shape[0], coef_ref.shape[0]

    def rows(value):
        return value.reshape(-1, nb)

    cross = over_rows(rows(own_ref[0:nx, 0]), rows(yown_ref[...]))
    cross += over_rows(rows(other_ref[0:nx, 0]), rows(yother_ref[...]))
    slab = jnp.where(place_ref[1] == 0, other_ref[0], own_ref[nx - 1])
    cross += over_rows(rows(slab), rows(xhalo_ref[...]))
    inside = over_rows(rows(own_ref[0]), rows(other_ref[nx - 1]))
    gram = gram_ref[...] - 0.5 * (cross + jnp.where(place_ref[0] == 1, inside, 0.0))
    total = (scale * (gram + jnp.transpose(gram))).astype(BF16)
    total = total.reshape(nb // (groups * depth), groups, depth, nb)
    for d in range(groups):
        out_ref[d, 0 : nb // groups] = rows(total[:, d])
        out_ref[d, nb // groups :] = coef_ref[...]


def add_cross(scale, groups, place, gram, own, other, yown, yother, xhalo, coef):
    nb = gram.shape[0]
    depth = coef.shape[0]
    halo_rows = (yown.size + yother.size + xhalo.size) // nb
    return call(
        functools.partial(cross_kernel, scale),
        jax.ShapeDtypeStruct((groups, nb // groups + depth, nb), BF16),
        [SMEM] + [VMEM] * 7,
        (place, gram, own, other, yown, yother, xhalo, coef),
        flops=2 * halo_rows * nb * nb,
    )


def middle_kernel(place_ref, in_ref, out_ref):
    core, chip = place_ref[0], place_ref[2]
    sources, height, nb = in_ref.shape
    rows = nb // sources
    depth = height - rows
    targets = rows // depth
    copies = out_ref.shape[0] // targets
    width = nb // 2
    total = in_ref[0, 0:rows].astype(F32)
    for s in range(1, sources):
        total += in_ref[s, 0:rows].astype(F32)
    total = total.astype(BF16).reshape(targets, depth, nb)
    share = sources // copies
    coef = [in_ref[share * chip + i, rows:] for i in range(share)]
    coef = jnp.concatenate(
        [jnp.where(core == 0, c[:, :width], c[:, width:]) for c in coef], axis=1
    )
    for t in range(targets):
        for c in range(copies):
            out_ref[t * copies + c, 0:depth] = total[t]
            out_ref[t * copies + c, depth:] = coef


def middle(place, arrived, targets, copies):
    sources, height, nb = arrived.shape
    depth = height - nb // sources
    assert sources == 2 * copies and targets * depth == nb // sources
    return call(
        middle_kernel,
        jax.ShapeDtypeStruct((targets * copies, 2 * depth, nb), BF16),
        [SMEM, VMEM],
        (place, arrived),
    )


def finish_kernel(in_ref, rows_ref, sent_ref):
    sources, height, nb = in_ref.shape
    depth, width = height // 2, nb // 2
    total = in_ref[0, 0:depth].astype(F32)
    for s in range(1, sources):
        total += in_ref[s, 0:depth].astype(F32)
    rows_ref[...] = total
    for s in range(sources):
        for part in range(2):
            start = (2 * s + part) * depth
            sent_ref[start : start + depth] = in_ref[
                s, depth:, part * width : (part + 1) * width
            ]
    for piece in range(PIECES):
        value = total.astype(BF16)
        total = total - value.astype(F32)
        for part in range(2):
            start = nb + (2 * piece + part) * depth
            sent_ref[start : start + depth] = value[:, part * width : (part + 1) * width]


def finish(arrived):
    _, height, nb = arrived.shape
    depth = height // 2
    return call(
        finish_kernel,
        (
            jax.ShapeDtypeStruct((depth, nb), F32),
            jax.ShapeDtypeStruct((nb + 2 * PIECES * depth, nb // 2), BF16),
        ),
        [VMEM],
        (arrived,),
    )


def rotate_kernel(place_ref, bands_ref, rows_ref, mine_ref, theirs_ref, corr_ref, hamil_ref, out_ref):
    core = place_ref[0]
    depth, nb = rows_ref.shape
    width = nb // 2
    block = out_ref.shape[0]
    step = pl.program_id(0)
    left = jnp.where(core == 0, mine_ref[0:nb], theirs_ref[0:nb])
    right = jnp.where(core == 0, theirs_ref[0:nb], mine_ref[0:nb])
    some = bands_ref[pl.ds(pl.multiple_of(step * block, block), block)]
    out_ref[:, :width] = jnp.dot(some, left, preferred_element_type=F32).astype(BF16)
    out_ref[:, width:] = jnp.dot(some, right, preferred_element_type=F32).astype(BF16)

    @pl.when(step == 0)
    def _():
        halves = []
        for part in range(2):
            starts = [nb + (2 * piece + part) * depth for piece in range(PIECES)]
            parts = [theirs_ref[s : s + depth].astype(F32) for s in starts]
            halves.append((parts[2] + parts[1]) + parts[0])
        theirs = jnp.concatenate(halves, axis=1)
        mine = rows_ref[...]
        corr_ref[...] = jnp.where(core == 0, mine, theirs)
        hamil_ref[...] = jnp.where(core == 0, theirs, mine)


def rotate(place, flat, rows, mine, theirs):
    cells, nb = flat.shape
    depth = rows.shape[0]
    steps = 5
    block = cells // steps
    small = pl.BlockSpec((depth, nb), lambda i: (0, 0))
    return pl.pallas_call(
        rotate_kernel,
        grid=(steps,),
        out_shape=(
            jax.ShapeDtypeStruct((depth, nb), F32),
            jax.ShapeDtypeStruct((depth, nb), F32),
            jax.ShapeDtypeStruct((cells, nb), BF16),
        ),
        in_specs=[SMEM] + [VMEM] * 4,
        out_specs=(small, small, pl.BlockSpec((block, nb), lambda i: (i, 0))),
        cost_estimate=pl.CostEstimate(
            flops=2 * cells * nb * nb, bytes_accessed=4 * cells * nb, transcendentals=0
        ),
        compiler_params=pltpu.CompilerParams(vmem_limit_bytes=20 << 20),
        name="rotate",
    )(place, flat, rows, mine, theirs)


def pairs_of(gx, gyz):
    def at(g, r):
        return g * gyz + r

    same, next_core, x = [], [], []
    for chip in range(gx // 2):
        for r in range(gyz - 1):
            same.append((at(2 * chip + 1, r), at(2 * chip + 1, r + 1)))
            next_core.append((at(2 * chip, r), at(2 * chip + 1, r + 1)))
    for chip in range(gx // 2 - 1):
        for r in range(gyz):
            if r % 2 == 0:
                x.append((at(2 * chip + 1, r), at(2 * chip + 3, r)))
            else:
                x.append((at(2 * chip + 2, r), at(2 * chip + 1, r)))
    return same, next_core, x


def exchanged(x, axis, groups=None):
    return lax.all_to_all(x, axis, 0, 0, tiled=True, axis_index_groups=groups)


def projected(bands, potential, eigenvectors):
    nx, ny, nz, nb = bands.shape
    gx, gyz = lax.axis_size("gx"), lax.axis_size("gyz")
    inner = 8
    outer = gyz // inner
    core = lax.rem(lax.axis_index("gx"), 2)
    odd = lax.rem(lax.axis_index("gyz"), 2)
    cells = nx * ny * nz
    scale = 1.0 / (cells * gyz)
    chip = lax.axis_index("gx") // 2
    place = jnp.stack((core, odd, chip)).astype(jnp.int32)
    pot = jnp.transpose(potential, (1, 0, 2))

    same, next_core, x_pairs = pairs_of(gx, gyz)
    partner = [(g, g ^ 1) for g in range(gx)]
    last = bands[:, ny - 1]
    slab = lax.dynamic_index_in_dim(bands, jnp.where(odd == 0, nx - 1, 0), 0, keepdims=False)
    yother = lax.ppermute(last, BOTH, next_core)
    yown = lax.ppermute(last, BOTH, same)
    xhalo = lax.ppermute(slab, BOTH, x_pairs)
    other = lax.ppermute(bands, "gx", partner)
    other_pot = lax.ppermute(pot, "gx", partner)

    gram = half_gram(place, bands, pot)
    gram = half_gram(place, other, other_pot, (gram,))
    sent = add_cross(
        scale, inner, place, gram, bands, other, yown, yother, xhalo, eigenvectors
    )
    groups = [[o * inner + i for i in range(inner)] for o in range(outer)]
    arrived = exchanged(sent, "gyz", groups)
    sent = middle(place, arrived, outer, gx // 2)
    groups = [
        [(2 * c + k) * gyz + o * inner + i for o in range(outer) for c in range(gx // 2)]
        for i in range(inner)
        for k in range(2)
    ]
    arrived = exchanged(sent, BOTH, groups)
    rows, mine = finish(arrived)
    theirs = lax.ppermute(mine, "gx", partner)
    corr, hamil, rotated = rotate(place, bands.reshape(cells, nb), rows, mine, theirs)
    return corr, hamil, rotated.reshape(bands.shape)


def solution(mesh):
    in_specs = (P("gx", "gyz", None, None), P("gx", "gyz", None), P("gyz", None))
    out_specs = (P("gyz", None), P("gyz", None), P("gx", "gyz", None, None))
    return jax.shard_map(
        projected, mesh=mesh, in_specs=in_specs, out_specs=out_specs, check_vma=False
    )
```

time: 84.1 us -> 87 us (1.034)
  the two profiles are of different devices: /device:TPU:1 before, /device:TPU:9 now
where the time goes in v4:
time: 87 us; the launch traced here: 86.6 us
  blocking collectives  45.9 us (53%)
  starting transfers between devices  21 us (24%)
  Pallas kernels  13.4 us (15%)
  local copies, waits for them, and re-layouts  4.12 us (5%)
  waiting for transfers between devices  1.19 us (1%)
    all_to_all x2, blocking collectives, exchanged(): return lax.all_to_all(x, axis, 0, 0, tiled=True, axis_index_groups=groups)  45.9 us
    pallas_call x5, Pallas kernels, call(): pl.pallas_call(kernel, out_shape=out_shape, in_specs=in_specs, out_specs=...  9.66 us
    ppermute x1, starting transfers between devices, projected(): xhalo = lax.ppermute(slab, BOTH, x_pairs)  5.82 us
    ppermute x1, starting transfers between devices, projected(): theirs = lax.ppermute(mine, 'gx', partner)  4.1 us
    ppermute x1, starting transfers between devices, projected(): yown = lax.ppermute(last, BOTH, same)  4 us
    pallas_call x1, Pallas kernels, rotate(): pl.pallas_call(rotate_kernel, grid=(steps,), out_shape=(jax.ShapeDtypeStr...  3.77 us
    ppermute x1, starting transfers between devices, projected(): other_pot = lax.ppermute(pot, 'gx', partner)  3.24 us
    ppermute x1, starting transfers between devices, projected(): other = lax.ppermute(bands, 'gx', partner)  2.59 us
  transfers between devices with their start and end apart: 6, of which 1 were waited for; matrix products, arithmetic and copies ran while one was open for 2% of the time, Pallas kernels for 8%

profile of v4, /device:TPU:9, one launch (start us, length us, event | category | flops | bytes accessed | tf_op | source)
XLA Modules:
  0.0 86.6 jit_solution(12518993352000124021)
XLA Ops:
  0.6 2.6 %collective-permute-start = (bf16[8,5,40,512]{3,2,1,0:T(8,128)(2,1)}, bf16[8,5,40,512]{3,2,1,0:T(8,128)(2,1)S(1)}, u32[]{:S(2)}, u32[]{:S(2)}) collective-permute-start(bf16[8,5,40,512]{3,2,1,0:T(8,128)(2,1)} %own_ref.1), channel_id=1, source_target_pairs={{0,64},{64,0},{128,192},{192,128},{256,320},{320,256},{384,448},{4... | collective-permute-start | bytes 4915208 | tf_op jit(solution)/shard_map/ppermute | solution.py:273
  3.2 1.0 %slice_bitcast_fusion = bf16[8,40,512]{2,1,0:T(8,128)(2,1)S(1)} fusion(bf16[8,5,40,512]{3,2,1,0:T(8,128)(2,1)} %own_ref.1), kind=kLoop, calls=%fused_computation | loop fusion | bytes 655360 | tf_op jit(solution)/shard_map/squeeze | solution.py:268
  4.2 4.0 %collective-permute-start.2 = (bf16[8,40,512]{2,1,0:T(8,128)(2,1)S(1)}, bf16[8,40,512]{2,1,0:T(8,128)(2,1)S(1)}, u32[]{:S(2)}, u32[]{:S(2)}) collective-permute-start(bf16[8,40,512]{2,1,0:T(8,128)(2,1)S(1)} %slice_bitcast_fusion), channel_id=1, source_target_pairs={{64,65},{65,66},{66,67},{67,68},{68,69},{69,70},{70,71},{71,72},{7... | collective-permute-start | bytes 983048 | tf_op jit(solution)/shard_map/ppermute | solution.py:271
  8.2 1.3 %collective-permute-start.3 = (bf16[8,40,512]{2,1,0:T(8,128)(2,1)S(1)}, bf16[8,40,512]{2,1,0:T(8,128)(2,1)S(1)}, u32[]{:S(2)}, u32[]{:S(2)}) collective-permute-start(bf16[8,40,512]{2,1,0:T(8,128)(2,1)S(1)} %slice_bitcast_fusion), channel_id=1, source_target_pairs={{0,65},{1,66},{2,67},{3,68},{4,69},{5,70},{6,71},{7,72},{8,73},{9,... | collective-permute-start | bytes 983048 | tf_op jit(solution)/shard_map/ppermute | solution.py:270
  9.5 3.2 %collective-permute-start.1 = (f32[5,8,40]{2,1,0:T(8,128)}, f32[5,8,40]{2,1,0:T(8,128)S(1)}, u32[]{:S(2)}, u32[]{:S(2)}) collective-permute-start(f32[5,8,40]{2,1,0:T(8,128)} %bitcast.13), channel_id=1, source_target_pairs={{0,64},{64,0},{128,192},{192,128},{256,320},{320,256},{384,448},{4... | collective-permute-start | bytes 19208 | tf_op jit(solution)/shard_map/ppermute | solution.py:274
  12.8 0.9 %dynamic-slice_bitcast_fusion = bf16[5,40,512]{2,1,0:T(8,128)(2,1)S(1)} fusion(bf16[8,5,40,512]{3,2,1,0:T(8,128)(2,1)} %own_ref.1, s32[]{:T(128)S(6)} %select_n.12), kind=kLoop, calls=%fused_computation.1 | loop fusion | bytes 409604 | tf_op jit(solution)/shard_map/jit(dynamic_index_in_dim)/squeeze | solution.py:269
  13.7 5.8 %collective-permute-start.4 = (bf16[5,40,512]{2,1,0:T(8,128)(2,1)S(1)}, bf16[5,40,512]{2,1,0:T(8,128)(2,1)S(1)}, u32[]{:S(2)}, u32[]{:S(2)}) collective-permute-start(bf16[5,40,512]{2,1,0:T(8,128)(2,1)S(1)} %dynamic-slice_bitcast_fusion), channel_id=1, source_target_pairs={{64,192},{129,65},{66,194},{131,67},{68,196},{133,69},{70,198},{13... | collective-permute-start | bytes 614408 | tf_op jit(solution)/shard_map/ppermute | solution.py:272
  19.6 0.1 pad_add_fusion.place_ref
  19.7 1.4 %copy-done = bf16[8,5,40,512]{3,2,1,0:T(8,128)(2,1)S(1)} copy-done((bf16[8,5,40,512]{3,2,1,0:T(8,128)(2,1)S(1)}, bf16[8,5,40,512]{3,2,1,0:T(8,128)(2,1)}, u32[]{:S(2)}) %copy-start) | copy-done | bytes 1638424
  21.1 0.7 copy-done.3
  21.8 3.6 %shard_map.58.refs_0_ = f32[512,512]{1,0:T(8,128)S(1)} custom-call(s32[3]{0:T(128)S(1)} %pad_add_fusion.place_ref, bf16[8,5,40,512]{3,2,1,0:T(8,128)(2,1)S(1)} %copy-done, f32[5,8,40]{2,1,0:T(8,128)S(1)} %bitcast.14), custom_call_target="tpu_custom_call" | custom-call | flops 838860800 | bytes 1644812 | tf_op jit(solution)/shard_map/pallas_call | solution.py:27
  25.4 0.0 copy-start.1
  25.4 0.0 copy-start.2
  25.4 0.0 collective-permute-done.1.pot_ref
  25.5 0.0 collective-permute-done.bands_ref.other_ref
  25.5 3.6 %shard_map.59.gram_ref = f32[512,512]{1,0:T(8,128)S(1)} custom-call(s32[3]{0:T(128)S(1)} %pad_add_fusion.place_ref, bf16[8,5,40,512]{3,2,1,0:T(8,128)(2,1)S(1)} %collective-permute-done.bands_ref.other_ref, f32[5,8,40]{2,1,0:T(8,128)S(1)} %collective-permute-done.1.pot_ref, f32[512,512]{1,0:T(8,128)S(1)} %shard_map.58.refs_0_), custom_call_target="tpu_custom_call" | custom-call | flops 838860800 | bytes 2693388 | tf_op jit(solution)/shard_map/pallas_call | solution.py:27
  29.1 1.8 %shard_map.60 = bf16[8,72,512]{2,1,0:T(8,128)(2,1)S(1)} custom-call(s32[3]{0:T(128)S(1)} %pad_add_fusion.place_ref, f32[512,512]{1,0:T(8,128)S(1)} %shard_map.59.gram_ref, bf16[8,5,40,512]{3,2,1,0:T(8,128)(2,1)S(1)} %copy-done.1, bf16[8,5,40,512]{3,2,1,0:T(8,128)(2,1)S(1)} %collective-permute-done.bands_ref.other_ref, ...), custom_call_target="tpu_custom_call" | custom-call | flops 440401920 | bytes 5193740 | tf_op jit(solution)/shard_map/pallas_call | solution.py:27
  30.9 12.1 %all_to_all.10.in_ref = bf16[8,72,512]{2,1,0:T(8,128)(2,1)S(1)} all-to-all(bf16[8,72,512]{2,1,0:T(8,128)(2,1)S(1)} %shard_map.60), channel_id=1, replica_groups={{0,1,2,3,4,5,6,7},{8,9,10,11,12,13,14,15},{16,17,18,19,20,21,22,23},{24..., dimensions={0} | all-to-all | bytes 1179648 | tf_op jit(solution)/shard_map/all_to_all | solution.py:250
  43.0 0.6 shard_map.61
  43.7 33.8 %all_to_all.11.in_ref = bf16[32,16,512]{2,1,0:T(8,128)(2,1)S(1)} all-to-all(bf16[32,16,512]{2,1,0:T(8,128)(2,1)S(1)} %shard_map.61), channel_id=1, replica_groups={{0,128,256,384,8,136,264,392,16,144,272,400,24,152,280,408,32,160,288,4..., dimensions={0} | all-to-all | bytes 1048576 | tf_op jit(solution)/shard_map/all_to_all | solution.py:250
  77.4 0.1 shard_map.62
  77.5 4.1 %collective-permute-start.5 = (bf16[560,256]{1,0:T(8,128)(2,1)S(1)}, bf16[560,256]{1,0:T(8,128)(2,1)S(1)}, u32[]{:S(2)}, u32[]{:S(2)}) collective-permute-start(bf16[560,256]{1,0:T(8,128)(2,1)S(1)} %get-tuple-element.9.mine_ref), channel_id=1, source_target_pairs={{0,64},{64,0},{128,192},{192,128},{256,320},{320,256},{384,448},{4... | collective-permute-start | bytes 860168 | tf_op jit(solution)/shard_map/ppermute | solution.py:291
  81.6 1.2 %collective-permute-done.5.theirs_ref = bf16[560,256]{1,0:T(8,128)(2,1)S(1)} collective-permute-done((bf16[560,256]{1,0:T(8,128)(2,1)S(1)}, bf16[560,256]{1,0:T(8,128)(2,1)S(1)}, u32[]{:S(2)}, u32[]{:S(2)}) %collective-permute-start.5) | collective-permute-done | bytes 286752 | tf_op jit(solution)/shard_map/ppermute | solution.py:291
  82.8 3.8 %rotate.1 = (f32[8,512]{1,0:T(8,128)}, f32[8,512]{1,0:T(8,128)}, bf16[1600,512]{1,0:T(8,128)(2,1)}) custom-call(s32[3]{0:T(128)S(1)} %pad_add_fusion.place_ref, bf16[1600,512]{1,0:T(8,128)(2,1)S(1)} %bitcast.12, f32[8,512]{1,0:T(8,128)S(1)} %get-tuple-element.8.rows_ref, bf16[560,256]{1,0:T(8,128)(2,1)S(1)} %get-tuple-element.9.mine_ref, ...), custom_call_target="tpu_custom_call" | custom-call | flops 838860800 | bytes 3276800 | tf_op jit(solution)/shard_map/rotate/pallas_call | solution.py:213
  (7 shorter events, 0.0 us)
Async XLA Ops:
  0.6 24.8 %collective-permute-start = (bf16[8,5,40,512]{3,2,1,0:T(8,128)(2,1)}, bf16[8,5,40,512]{3,2,1,0:T(8,128)(2,1)S(1)}, u32[]{:S(2)}, u32[]{:S(2)}) collective-permute-start(bf16[8,5,40,512]{3,2,1,0:T(8,128)(2,1)} %own_ref.1), channel_id=1, source_target_pairs={{0,64},{64,0},{128,192},{192,128},{256,320},{320,256},{384,448},{4... | collective-permute-start | bytes 4915208 | tf_op jit(solution)/shard_map/ppermute | solution.py:273
  4.2 24.8 %collective-permute-start.2 = (bf16[8,40,512]{2,1,0:T(8,128)(2,1)S(1)}, bf16[8,40,512]{2,1,0:T(8,128)(2,1)S(1)}, u32[]{:S(2)}, u32[]{:S(2)}) collective-permute-start(bf16[8,40,512]{2,1,0:T(8,128)(2,1)S(1)} %slice_bitcast_fusion), channel_id=1, source_target_pairs={{64,65},{65,66},{66,67},{67,68},{68,69},{69,70},{70,71},{71,72},{7... | collective-permute-start | bytes 983048 | tf_op jit(solution)/shard_map/ppermute | solution.py:271
  8.2 20.8 %collective-permute-start.3 = (bf16[8,40,512]{2,1,0:T(8,128)(2,1)S(1)}, bf16[8,40,512]{2,1,0:T(8,128)(2,1)S(1)}, u32[]{:S(2)}, u32[]{:S(2)}) collective-permute-start(bf16[8,40,512]{2,1,0:T(8,128)(2,1)S(1)} %slice_bitcast_fusion), channel_id=1, source_target_pairs={{0,65},{1,66},{2,67},{3,68},{4,69},{5,70},{6,71},{7,72},{8,73},{9,... | collective-permute-start | bytes 983048 | tf_op jit(solution)/shard_map/ppermute | solution.py:270
  9.5 15.9 %collective-permute-start.1 = (f32[5,8,40]{2,1,0:T(8,128)}, f32[5,8,40]{2,1,0:T(8,128)S(1)}, u32[]{:S(2)}, u32[]{:S(2)}) collective-permute-start(f32[5,8,40]{2,1,0:T(8,128)} %bitcast.13), channel_id=1, source_target_pairs={{0,64},{64,0},{128,192},{192,128},{256,320},{320,256},{384,448},{4... | collective-permute-start | bytes 19208 | tf_op jit(solution)/shard_map/ppermute | solution.py:274
  13.7 15.3 %collective-permute-start.4 = (bf16[5,40,512]{2,1,0:T(8,128)(2,1)S(1)}, bf16[5,40,512]{2,1,0:T(8,128)(2,1)S(1)}, u32[]{:S(2)}, u32[]{:S(2)}) collective-permute-start(bf16[5,40,512]{2,1,0:T(8,128)(2,1)S(1)} %dynamic-slice_bitcast_fusion), channel_id=1, source_target_pairs={{64,192},{129,65},{66,194},{131,67},{68,196},{133,69},{70,198},{13... | collective-permute-start | bytes 614408 | tf_op jit(solution)/shard_map/ppermute | solution.py:272
  19.7 1.4 %copy-start = (bf16[8,5,40,512]{3,2,1,0:T(8,128)(2,1)S(1)}, bf16[8,5,40,512]{3,2,1,0:T(8,128)(2,1)}, u32[]{:S(2)}) copy-start(bf16[8,5,40,512]{3,2,1,0:T(8,128)(2,1)} %own_ref.1) | copy-start | bytes 4915204
  21.1 0.7 copy-start.3
  25.4 3.7 %copy-start.1 = (bf16[8,5,40,512]{3,2,1,0:T(8,128)(2,1)S(1)}, bf16[8,5,40,512]{3,2,1,0:T(8,128)(2,1)}, u32[]{:S(2)}) copy-start(bf16[8,5,40,512]{3,2,1,0:T(8,128)(2,1)} %own_ref.1) | copy-start | bytes 4915204
  25.4 3.7 %copy-start.2 = (bf16[8,512]{1,0:T(8,128)(2,1)S(1)}, bf16[8,512]{1,0:T(8,128)(2,1)}, u32[]{:S(2)}) copy-start(bf16[8,512]{1,0:T(8,128)(2,1)} %coef_ref.1) | copy-start | bytes 24580
  77.5 5.3 %collective-permute-start.5 = (bf16[560,256]{1,0:T(8,128)(2,1)S(1)}, bf16[560,256]{1,0:T(8,128)(2,1)S(1)}, u32[]{:S(2)}, u32[]{:S(2)}) collective-permute-start(bf16[560,256]{1,0:T(8,128)(2,1)S(1)} %get-tuple-element.9.mine_ref), channel_id=1, source_target_pairs={{0,64},{64,0},{128,192},{192,128},{256,320},{320,256},{384,448},{4... | collective-permute-start | bytes 860168 | tf_op jit(solution)/shard_map/ppermute | solution.py:291

commit v5 on v2

v5 whole, which is shorter than its diff:
```python
import functools

import jax
import jax.numpy as jnp
from jax import lax
from jax.experimental import pallas as pl
from jax.experimental.pallas import tpu as pltpu
from jax.sharding import PartitionSpec as P


F32 = jnp.float32
BF16 = jnp.bfloat16
BOTH = ("gx", "gyz")

VMEM = pl.BlockSpec(memory_space=pltpu.VMEM)
SMEM = pl.BlockSpec(memory_space=pltpu.SMEM)


def over_rows(a, b):
    return lax.dot_general(a, b, (((0,), (0,)), ((), ())), preferred_element_type=F32)


def call(kernel, out_shape, in_specs, args, scratch=(), flops=0):
    many = isinstance(out_shape, tuple)
    moved = sum(a.size * a.dtype.itemsize for a in args)
    return pl.pallas_call(
        kernel,
        out_shape=out_shape,
        in_specs=in_specs,
        out_specs=(VMEM,) * len(out_shape) if many else VMEM,
        scratch_shapes=list(scratch),
        cost_estimate=pl.CostEstimate(flops=flops, bytes_accessed=moved, transcendentals=0),
        compiler_params=pltpu.CompilerParams(vmem_limit_bytes=20 << 20),
    )(*args)


def half_kernel(place_ref, bands_ref, pot_ref, *refs):
    nx, ny, nz, nb = bands_ref.shape
    right_ref, gram_ref = refs[-1], refs[-2]
    row = lax.broadcasted_iota(jnp.int32, (nz, nb), 0)
    half = jnp.where(place_ref[0] == 1, 0.5, 0.0).astype(F32)

    def tiles_at(x):
        return [bands_ref[x, y].astype(F32) for y in range(ny)]

    def slab(x, first):
        pot = jnp.transpose(pot_ref[:, pl.ds(x, 1), :].reshape(ny, nz))
        factor = 0.5 + half * (2.0 + pot)
        tiles = tiles_at(x)
        below = None if first else tiles_at(x - 1)
        for y in range(ny):
            total = jnp.where(row > 0, pltpu.roll(tiles[y], 1, 0), 0.0)
            if y > 0:
                total += tiles[y - 1]
            if not first:
                total += below[y]
            right_ref[x, y] = (factor[:, y : y + 1] * tiles[y] - half * total).astype(BF16)

    def step(x, carry):
        slab(x, False)
        return carry

    slab(0, True)
    lax.fori_loop(1, nx, step, 0)
    gram = over_rows(bands_ref[...].reshape(-1, nb), right_ref[...].reshape(-1, nb))
    if len(refs) > 2:
        gram += refs[0][...]
    gram_ref[...] = gram


def half_gram(place, bands, pot, given=()):
    nb = bands.shape[-1]
    return call(
        half_kernel,
        jax.ShapeDtypeStruct((nb, nb), F32),
        [SMEM] + [VMEM] * (2 + len(given)),
        (place, bands, pot, *given),
        scratch=[pltpu.VMEM(bands.shape, BF16)],
        flops=2 * bands.size * nb,
    )


def cross_kernel(
    scale, place_ref, gram_ref, own_ref, other_ref, yown_ref, yother_ref, xhalo_ref, out_ref
):
    _, _, nb = xhalo_ref.shape
    nx = yown_ref.shape[0]

    def rows(value):
        return value.reshape(-1, nb)

    cross = over_rows(rows(own_ref[:, 0]), rows(yown_ref[...]))
    cross += over_rows(rows(other_ref[:, 0]), rows(yother_ref[...]))
    slab = jnp.where(place_ref[1] == 0, other_ref[0], own_ref[nx - 1])
    cross += over_rows(rows(slab), rows(xhalo_ref[...]))
    inside = over_rows(rows(own_ref[0]), rows(other_ref[nx - 1]))
    gram = gram_ref[...] - 0.5 * (cross + jnp.where(place_ref[0] == 1, inside, 0.0))
    out_ref[...] = (scale * (gram + jnp.transpose(gram))).astype(BF16)


def add_cross(scale, place, gram, own, other, yown, yother, xhalo):
    nb = gram.shape[0]
    halo_rows = (yown.size + yother.size + xhalo.size) // nb
    return call(
        functools.partial(cross_kernel, scale),
        jax.ShapeDtypeStruct((nb, nb), BF16),
        [SMEM] + [VMEM] * 6,
        (place, gram, own, other, yown, yother, xhalo),
        flops=2 * halo_rows * nb * nb,
    )


def finish_kernel(in_ref, rows_ref):
    total = in_ref[0].astype(F32)
    for s in range(1, in_ref.shape[0]):
        total += in_ref[s].astype(F32)
    for c in range(rows_ref.shape[0]):
        rows_ref[c] = total


def finish(arrived, copies):
    _, depth, nb = arrived.shape
    return call(finish_kernel, jax.ShapeDtypeStruct((copies, depth, nb), F32), [VMEM], (arrived,))


def rotate_kernel(place_ref, bands_ref, mine_ref, theirs_ref, out_ref):
    core = place_ref[0]
    width = mine_ref.shape[1]
    block = out_ref.shape[0]
    mine, theirs = mine_ref[...], theirs_ref[...]
    start = pl.multiple_of(pl.program_id(0) * block, block)
    some = bands_ref[pl.ds(start, block)]
    left = jnp.where(core == 0, mine, theirs)
    right = jnp.where(core == 0, theirs, mine)
    out_ref[:, :width] = jnp.dot(some, left, preferred_element_type=F32).astype(BF16)
    out_ref[:, width:] = jnp.dot(some, right, preferred_element_type=F32).astype(BF16)


def rotate(place, flat, mine, theirs):
    cells, nb = flat.shape
    steps = 5
    block = cells // steps
    return pl.pallas_call(
        rotate_kernel,
        grid=(steps,),
        out_shape=jax.ShapeDtypeStruct((cells, nb), BF16),
        in_specs=[SMEM] + [VMEM] * 3,
        out_specs=pl.BlockSpec((block, nb), lambda i: (i, 0)),
        cost_estimate=pl.CostEstimate(
            flops=2 * cells * nb * nb, bytes_accessed=4 * cells * nb, transcendentals=0
        ),
        compiler_params=pltpu.CompilerParams(vmem_limit_bytes=20 << 20),
        name="rotate",
    )(place, flat, mine, theirs)


def pairs_of(gx, gyz):
    def at(g, r):
        return g * gyz + r

    same, next_core, x = [], [], []
    for chip in range(gx // 2):
        for r in range(gyz - 1):
            same.append((at(2 * chip + 1, r), at(2 * chip + 1, r + 1)))
            next_core.append((at(2 * chip, r), at(2 * chip + 1, r + 1)))
    for chip in range(gx // 2 - 1):
        for r in range(gyz):
            if r % 2 == 0:
                x.append((at(2 * chip + 1, r), at(2 * chip + 3, r)))
            else:
                x.append((at(2 * chip + 2, r), at(2 * chip + 1, r)))
    return same, next_core, x


def exchanged(x, axis):
    return lax.all_to_all(x, axis, 0, 0, tiled=True)


def projected(bands, potential, eigenvectors):
    nx, ny, nz, nb = bands.shape
    gx, gyz = lax.axis_size("gx"), lax.axis_size("gyz")
    depth = eigenvectors.shape[0]
    core = lax.rem(lax.axis_index("gx"), 2)
    odd = lax.rem(lax.axis_index("gyz"), 2)
    cells = nx * ny * nz
    scale = 1.0 / (cells * gyz)
    place = jnp.stack((core, odd)).astype(jnp.int32)
    pot = jnp.transpose(potential, (1, 0, 2))

    half = lax.dynamic_slice_in_dim(eigenvectors, core * (nb // 2), nb // 2, axis=1)
    mine = exchanged(jnp.broadcast_to(half[None], (gyz, *half.shape)), "gyz")
    mine = mine.reshape(nb, nb // 2)

    same, next_core, x_pairs = pairs_of(gx, gyz)
    partner = [(g, g ^ 1) for g in range(gx)]
    last = bands[:, ny - 1]
    slab = lax.dynamic_index_in_dim(bands, jnp.where(odd == 0, nx - 1, 0), 0, keepdims=False)
    yother = lax.ppermute(last, BOTH, next_core)
    yown = lax.ppermute(last, BOTH, same)
    xhalo = lax.ppermute(slab, BOTH, x_pairs)
    other = lax.ppermute(bands, "gx", partner)
    other_pot = lax.ppermute(pot, "gx", partner)

    gram = half_gram(place, bands, pot)
    gram = half_gram(place, other, other_pot, (gram,))
    gram = add_cross(scale, place, gram, bands, other, yown, yother, xhalo)
    arrived = exchanged(gram.reshape(gyz, depth, nb), "gyz")
    rows = finish(arrived, gx)
    parts = exchanged(rows, "gx")
    sums = parts.reshape(gx // 2, 2, depth, nb).sum(axis=0)
    theirs = lax.ppermute(mine, "gx", partner)
    rotated = rotate(place, bands.reshape(cells, nb), mine, theirs)
    return sums[0], sums[1], rotated.reshape(bands.shape)


def solution(mesh):
    in_specs = (P("gx", "gyz", None, None), P("gx", "gyz", None), P("gyz", None))
    out_specs = (P("gyz", None), P("gyz", None), P("gx", "gyz", None, None))
    return jax.shard_map(
        projected, mesh=mesh, in_specs=in_specs, out_specs=out_specs, check_vma=False
    )
```

time: 102 us -> 90.4 us (0.89)
  blocking collectives: 28.9 us -> 0 us
  starting transfers between devices: 31.8 us -> 52.3 us
  waiting for transfers between devices: 25.3 us -> 17.2 us
  Pallas kernels: 6.51 us -> 13.8 us
  matrix products: 2.18 us -> 0 us
    all_to_all x1 -> x0, blocking collectives: 28.9 us -> none  [to_rows(): return lax.all_to_all(parts, axis, 0, 0, tiled=True)]
    all_to_all x2 -> x3, starting transfers between devices: 16 us -> 26.6 us  [exchanged(): return lax.all_to_all(x, axis, 0, 0, tiled=True)]
    pallas_call x1 -> x5, Pallas kernels: 6.51 us -> 13.8 us  [the longest x4 10 us: call(): pl.pallas_call(kernel, out_shape=out_shape, in_specs=in_specs, out_specs=...]
    all_to_all x2 -> x3, waiting for transfers between devices: 23.1 us -> 17.1 us  [exchanged(): return lax.all_to_all(x, axis, 0, 0, tiled=True)]
    ppermute x1 -> x2, starting transfers between devices: 1.91 us -> 5.93 us  [the longest x1 4.01 us: projected(): other_pot = lax.ppermute(pot, 'gx', partner)]
    squeeze x0 -> x2, local copies, waits for them, and re-layouts: none -> 2.67 us  [the longest x1 1.73 us: projected(): last = bands[:, ny - 1]]
    ppermute x1, starting transfers between devices: 3.18 us -> 5.82 us  [projected(): xhalo = lax.ppermute(slab, BOTH, x_pairs)]
    ppermute x1, starting transfers between devices: 1.31 us -> 3.63 us  [projected(): yown = lax.ppermute(last, BOTH, same)]
  transfers between devices with their start and end apart: 7 -> 9, of which waited for: 4 -> 2; matrix products, arithmetic and copies ran while one was open for 5% -> 4% of each run, Pallas kernels for 0% -> 15%
where the time goes in v5:
time: 90.4 us; the launch traced here: 89.7 us
  starting transfers between devices  52.3 us (58%)
  waiting for transfers between devices  17.2 us (19%)
  Pallas kernels  13.8 us (15%)
  local copies, waits for them, and re-layouts  5.54 us (6%)
    all_to_all x3, starting transfers between devices, exchanged(): return lax.all_to_all(x, axis, 0, 0, tiled=True)  26.6 us
    all_to_all x3, waiting for transfers between devices, exchanged(): return lax.all_to_all(x, axis, 0, 0, tiled=True)  17.1 us
    pallas_call x4, Pallas kernels, call(): pl.pallas_call(kernel, out_shape=out_shape, in_specs=in_specs, out_specs=...  10 us
    ppermute x1, starting transfers between devices, projected(): other = lax.ppermute(bands, 'gx', partner)  8.88 us
    ppermute x1, starting transfers between devices, projected(): xhalo = lax.ppermute(slab, BOTH, x_pairs)  5.82 us
    ppermute x1, starting transfers between devices, projected(): other_pot = lax.ppermute(pot, 'gx', partner)  4.01 us
    pallas_call x1, Pallas kernels, rotate(): pl.pallas_call(rotate_kernel, grid=(steps,), out_shape=jax.ShapeDtypeStru...  3.77 us
    ppermute x1, starting transfers between devices, projected(): yown = lax.ppermute(last, BOTH, same)  3.63 us
  transfers between devices with their start and end apart: 9, of which 2 were waited for; matrix products, arithmetic and copies ran while one was open for 4% of the time, Pallas kernels for 15%

profile of v5, /device:TPU:1, one launch (start us, length us, event | category | flops | bytes accessed | tf_op | source)
XLA Modules:
  0.0 89.7 jit_solution(8032882916506712890)
XLA Ops:
  0.6 0.0 copy-start
  0.7 8.9 %collective-permute-start = (bf16[8,5,40,512]{3,2,1,0:T(8,128)(2,1)}, bf16[8,5,40,512]{3,2,1,0:T(8,128)(2,1)S(1)}, u32[]{:S(2)}, u32[]{:S(2)}) collective-permute-start(bf16[8,5,40,512]{3,2,1,0:T(8,128)(2,1)} %own_ref.1), channel_id=1, source_target_pairs={{0,64},{64,0},{128,192},{192,128},{256,320},{320,256},{384,448},{4... | collective-permute-start | bytes 4915208 | tf_op jit(solution)/shard_map/ppermute | solution.py:201
  9.6 0.7 broadcast_in_dim.2
  10.3 6.8 %all-to-all-start.2 = ((bf16[64,8,256]{2,1,0:T(8,128)(2,1)}), bf16[64,8,256]{2,1,0:T(8,128)(2,1)S(1)}, u32[]{:S(2)}, u32[]{:S(2)}) async-start(bf16[64,8,256]{2,1,0:T(8,128)(2,1)} %broadcast_in_dim.2), calls=%async_computation.2 | async-start | bytes 524288 | tf_op jit(solution)/shard_map/all_to_all | solution.py:176
  17.1 1.7 %slice_bitcast_fusion = bf16[8,40,512]{2,1,0:T(8,128)(2,1)} fusion(bf16[8,5,40,512]{3,2,1,0:T(8,128)(2,1)} %own_ref.1), kind=kLoop, calls=%fused_computation | loop fusion | bytes 655360 | tf_op jit(solution)/shard_map/squeeze | solution.py:196
  18.8 3.6 %collective-permute-start.2 = (bf16[8,40,512]{2,1,0:T(8,128)(2,1)}, bf16[8,40,512]{2,1,0:T(8,128)(2,1)}, u32[]{:S(2)}, u32[]{:S(2)}) collective-permute-start(bf16[8,40,512]{2,1,0:T(8,128)(2,1)} %slice_bitcast_fusion), channel_id=1, source_target_pairs={{64,65},{65,66},{66,67},{67,68},{68,69},{69,70},{70,71},{71,72},{7... | collective-permute-start | bytes 983048 | tf_op jit(solution)/shard_map/ppermute | solution.py:199
  22.4 1.4 %collective-permute-start.3 = (bf16[8,40,512]{2,1,0:T(8,128)(2,1)}, bf16[8,40,512]{2,1,0:T(8,128)(2,1)}, u32[]{:S(2)}, u32[]{:S(2)}) collective-permute-start(bf16[8,40,512]{2,1,0:T(8,128)(2,1)} %slice_bitcast_fusion), channel_id=1, source_target_pairs={{0,65},{1,66},{2,67},{3,68},{4,69},{5,70},{6,71},{7,72},{8,73},{9,... | collective-permute-start | bytes 983048 | tf_op jit(solution)/shard_map/ppermute | solution.py:198
  23.8 4.0 %collective-permute-start.1 = (f32[5,8,40]{2,1,0:T(8,128)}, f32[5,8,40]{2,1,0:T(8,128)}, u32[]{:S(2)}, u32[]{:S(2)}) collective-permute-start(f32[5,8,40]{2,1,0:T(8,128)} %bitcast.22), channel_id=1, source_target_pairs={{0,64},{64,0},{128,192},{192,128},{256,320},{320,256},{384,448},{4... | collective-permute-start | bytes 19208 | tf_op jit(solution)/shard_map/ppermute | solution.py:202
  27.8 0.9 %dynamic-slice_bitcast_fusion = bf16[5,40,512]{2,1,0:T(8,128)(2,1)S(1)} fusion(bf16[8,5,40,512]{3,2,1,0:T(8,128)(2,1)} %own_ref.1, s32[]{:T(128)S(6)} %select_n.9), kind=kLoop, calls=%fused_computation.1 | loop fusion | bytes 409604 | tf_op jit(solution)/shard_map/jit(dynamic_index_in_dim)/squeeze | solution.py:197
  28.8 5.8 %collective-permute-start.4 = (bf16[5,40,512]{2,1,0:T(8,128)(2,1)S(1)}, bf16[5,40,512]{2,1,0:T(8,128)(2,1)S(1)}, u32[]{:S(2)}, u32[]{:S(2)}) collective-permute-start(bf16[5,40,512]{2,1,0:T(8,128)(2,1)S(1)} %dynamic-slice_bitcast_fusion), channel_id=1, source_target_pairs={{64,192},{129,65},{66,194},{131,67},{68,196},{133,69},{70,198},{13... | collective-permute-start | bytes 614408 | tf_op jit(solution)/shard_map/ppermute | solution.py:200
  34.6 0.1 pad_add_fusion.place_ref
  34.7 0.7 copy-done.3
  35.4 3.4 %shard_map.58.refs_0_ = f32[512,512]{1,0:T(8,128)S(1)} custom-call(s32[2]{0:T(128)S(1)} %pad_add_fusion.place_ref, bf16[8,5,40,512]{3,2,1,0:T(8,128)(2,1)S(1)} %copy-done.1, f32[5,8,40]{2,1,0:T(8,128)S(1)} %bitcast.23), custom_call_target="tpu_custom_call" | custom-call | flops 838860800 | bytes 1644808 | tf_op jit(solution)/shard_map/pallas_call | solution.py:26
  38.8 3.6 %shard_map.59.gram_ref = f32[512,512]{1,0:T(8,128)S(1)} custom-call(s32[2]{0:T(128)S(1)} %pad_add_fusion.place_ref, bf16[8,5,40,512]{3,2,1,0:T(8,128)(2,1)S(1)} %collective-permute-done.bands_ref.other_ref, f32[5,8,40]{2,1,0:T(8,128)} %collective-permute-done.1.pot_ref, f32[512,512]{1,0:T(8,128)S(1)} %shard_map.58.refs_0_), custom_call_target="tpu_custom_call" | custom-call | flops 838860800 | bytes 2693384 | tf_op jit(solution)/shard_map/pallas_call | solution.py:26
  42.5 2.3 %shard_map.60 = bf16[512,512]{1,0:T(8,128)(2,1)S(1)} custom-call(s32[2]{0:T(128)S(1)} %pad_add_fusion.place_ref, f32[512,512]{1,0:T(8,128)S(1)} %shard_map.59.gram_ref, bf16[8,5,40,512]{3,2,1,0:T(8,128)(2,1)S(1)} %copy-done.1, bf16[8,5,40,512]{3,2,1,0:T(8,128)(2,1)S(1)} %collective-permute-done.bands_ref.other_ref, ...), custom_call_target="tpu_custom_call" | custom-call | flops 440401920 | bytes 5185544 | tf_op jit(solution)/shard_map/pallas_call | solution.py:26
  44.8 0.8 copy-done.2
  45.6 9.6 %all-to-all-start = ((bf16[64,8,512]{2,1,0:T(8,128)(2,1)}), bf16[64,8,512]{2,1,0:T(8,128)(2,1)S(1)}, u32[]{:S(2)}, u32[]{:S(2)}) async-start(bf16[64,8,512]{2,1,0:T(8,128)(2,1)} %bitcast.19), calls=%async_computation | async-start | bytes 1048576 | tf_op jit(solution)/shard_map/all_to_all | solution.py:176
  55.2 1.9 %collective-permute-start.5 = (bf16[512,256]{1,0:T(8,128)(2,1)S(1)}, bf16[512,256]{1,0:T(8,128)(2,1)S(1)}, u32[]{:S(2)}, u32[]{:S(2)}) collective-permute-start(bf16[512,256]{1,0:T(8,128)(2,1)S(1)} %bitcast.20), channel_id=1, source_target_pairs={{0,64},{64,0},{128,192},{192,128},{256,320},{320,256},{384,448},{4... | collective-permute-start | bytes 786440 | tf_op jit(solution)/shard_map/ppermute | solution.py:211
  57.1 12.8 %all-to-all-done.in_ref = bf16[64,8,512]{2,1,0:T(8,128)(2,1)S(1)} async-done(((bf16[64,8,512]{2,1,0:T(8,128)(2,1)}), bf16[64,8,512]{2,1,0:T(8,128)(2,1)S(1)}, u32[]{:S(2)}, u32[]{:S(2)}) %all-to-all-start) | async-done | bytes 524320 | tf_op jit(solution)/shard_map/all_to_all | solution.py:176
  70.0 0.8 shard_map.61
  70.7 10.3 %all-to-all-start.1 = ((f32[8,8,512]{2,1,0:T(8,128)}), f32[8,8,512]{2,1,0:T(8,128)S(1)}, u32[]{:S(2)}, u32[]{:S(2)}) async-start(f32[8,8,512]{2,1,0:T(8,128)} %shard_map.61), calls=%async_computation.1 | async-start | bytes 262144 | tf_op jit(solution)/shard_map/all_to_all | solution.py:176
  81.0 3.8 %rotate.1 = bf16[1600,512]{1,0:T(8,128)(2,1)} custom-call(s32[2]{0:T(128)S(1)} %pad_add_fusion.place_ref, bf16[1600,512]{1,0:T(8,128)(2,1)S(1)} %bitcast.18, bf16[512,256]{1,0:T(8,128)(2,1)S(1)} %bitcast.21, bf16[512,256]{1,0:T(8,128)(2,1)S(1)} %collective-permute-done.5.theirs_ref), custom_call_target="tpu_custom_call" | custom-call | flops 838860800 | bytes 3276800 | tf_op jit(solution)/shard_map/rotate/pallas_call | solution.py:143
  84.7 4.3 %all-to-all-done.1 = f32[8,8,512]{2,1,0:T(8,128)S(1)} async-done(((f32[8,8,512]{2,1,0:T(8,128)}), f32[8,8,512]{2,1,0:T(8,128)S(1)}, u32[]{:S(2)}, u32[]{:S(2)}) %all-to-all-start.1) | async-done | bytes 131104 | tf_op jit(solution)/shard_map/all_to_all | solution.py:176
  89.1 0.6 slice_bitcast_fusion.1
  (14 shorter events, 0.1 us)
Async XLA Ops:
  0.6 8.9 %copy-start = (bf16[8,512]{1,0:T(8,128)(2,1)S(1)}, bf16[8,512]{1,0:T(8,128)(2,1)}, u32[]{:S(2)}) copy-start(bf16[8,512]{1,0:T(8,128)(2,1)} %param.5) | copy-start | bytes 24580
  0.6 34.1 %copy-start.1 = (bf16[8,5,40,512]{3,2,1,0:T(8,128)(2,1)S(1)}, bf16[8,5,40,512]{3,2,1,0:T(8,128)(2,1)}, u32[]{:S(2)}) copy-start(bf16[8,5,40,512]{3,2,1,0:T(8,128)(2,1)} %own_ref.1) | copy-start | bytes 4915204
  0.7 38.2 %collective-permute-start = (bf16[8,5,40,512]{3,2,1,0:T(8,128)(2,1)}, bf16[8,5,40,512]{3,2,1,0:T(8,128)(2,1)S(1)}, u32[]{:S(2)}, u32[]{:S(2)}) collective-permute-start(bf16[8,5,40,512]{3,2,1,0:T(8,128)(2,1)} %own_ref.1), channel_id=1, source_target_pairs={{0,64},{64,0},{128,192},{192,128},{256,320},{320,256},{384,448},{4... | collective-permute-start | bytes 4915208 | tf_op jit(solution)/shard_map/ppermute | solution.py:201
  10.3 35.3 %all-to-all-start.2 = ((bf16[64,8,256]{2,1,0:T(8,128)(2,1)}), bf16[64,8,256]{2,1,0:T(8,128)(2,1)S(1)}, u32[]{:S(2)}, u32[]{:S(2)}) async-start(bf16[64,8,256]{2,1,0:T(8,128)(2,1)} %broadcast_in_dim.2), calls=%async_computation.2 | async-start | bytes 524288 | tf_op jit(solution)/shard_map/all_to_all | solution.py:176
  18.8 23.7 %collective-permute-start.2 = (bf16[8,40,512]{2,1,0:T(8,128)(2,1)}, bf16[8,40,512]{2,1,0:T(8,128)(2,1)}, u32[]{:S(2)}, u32[]{:S(2)}) collective-permute-start(bf16[8,40,512]{2,1,0:T(8,128)(2,1)} %slice_bitcast_fusion), channel_id=1, source_target_pairs={{64,65},{65,66},{66,67},{67,68},{68,69},{69,70},{70,71},{71,72},{7... | collective-permute-start | bytes 983048 | tf_op jit(solution)/shard_map/ppermute | solution.py:199
  22.4 20.0 %collective-permute-start.3 = (bf16[8,40,512]{2,1,0:T(8,128)(2,1)}, bf16[8,40,512]{2,1,0:T(8,128)(2,1)}, u32[]{:S(2)}, u32[]{:S(2)}) collective-permute-start(bf16[8,40,512]{2,1,0:T(8,128)(2,1)} %slice_bitcast_fusion), channel_id=1, source_target_pairs={{0,65},{1,66},{2,67},{3,68},{4,69},{5,70},{6,71},{7,72},{8,73},{9,... | collective-permute-start | bytes 983048 | tf_op jit(solution)/shard_map/ppermute | solution.py:198
  23.8 15.0 %collective-permute-start.1 = (f32[5,8,40]{2,1,0:T(8,128)}, f32[5,8,40]{2,1,0:T(8,128)}, u32[]{:S(2)}, u32[]{:S(2)}) collective-permute-start(f32[5,8,40]{2,1,0:T(8,128)} %bitcast.22), channel_id=1, source_target_pairs={{0,64},{64,0},{128,192},{192,128},{256,320},{320,256},{384,448},{4... | collective-permute-start | bytes 19208 | tf_op jit(solution)/shard_map/ppermute | solution.py:202
  28.8 13.6 %collective-permute-start.4 = (bf16[5,40,512]{2,1,0:T(8,128)(2,1)S(1)}, bf16[5,40,512]{2,1,0:T(8,128)(2,1)S(1)}, u32[]{:S(2)}, u32[]{:S(2)}) collective-permute-start(bf16[5,40,512]{2,1,0:T(8,128)(2,1)S(1)} %dynamic-slice_bitcast_fusion), channel_id=1, source_target_pairs={{64,192},{129,65},{66,194},{131,67},{68,196},{133,69},{70,198},{13... | collective-permute-start | bytes 614408 | tf_op jit(solution)/shard_map/ppermute | solution.py:200
  34.7 0.7 copy-start.3
  44.8 0.8 copy-start.2
  45.6 24.4 %all-to-all-start = ((bf16[64,8,512]{2,1,0:T(8,128)(2,1)}), bf16[64,8,512]{2,1,0:T(8,128)(2,1)S(1)}, u32[]{:S(2)}, u32[]{:S(2)}) async-start(bf16[64,8,512]{2,1,0:T(8,128)(2,1)} %bitcast.19), calls=%async_computation | async-start | bytes 1048576 | tf_op jit(solution)/shard_map/all_to_all | solution.py:176
  55.2 25.8 %collective-permute-start.5 = (bf16[512,256]{1,0:T(8,128)(2,1)S(1)}, bf16[512,256]{1,0:T(8,128)(2,1)S(1)}, u32[]{:S(2)}, u32[]{:S(2)}) collective-permute-start(bf16[512,256]{1,0:T(8,128)(2,1)S(1)} %bitcast.20), channel_id=1, source_target_pairs={{0,64},{64,0},{128,192},{192,128},{256,320},{320,256},{384,448},{4... | collective-permute-start | bytes 786440 | tf_op jit(solution)/shard_map/ppermute | solution.py:211
  70.7 18.4 %all-to-all-start.1 = ((f32[8,8,512]{2,1,0:T(8,128)}), f32[8,8,512]{2,1,0:T(8,128)S(1)}, u32[]{:S(2)}, u32[]{:S(2)}) async-start(f32[8,8,512]{2,1,0:T(8,128)} %shard_map.61), calls=%async_computation.1 | async-start | bytes 262144 | tf_op jit(solution)/shard_map/all_to_all | solution.py:176

commit v6 on v3

--- a/solution.py
+++ b/solution.py
@@ -11,7 +11,6 @@
 F32 = jnp.float32
 BF16 = jnp.bfloat16
 BOTH = ("gx", "gyz")
-PIECES = 3
 
 VMEM = pl.BlockSpec(memory_space=pltpu.VMEM)
 SMEM = pl.BlockSpec(memory_space=pltpu.SMEM)
@@ -31,99 +30,56 @@
         out_specs=(VMEM,) * len(out_shape) if many else VMEM,
         scratch_shapes=list(scratch),
         cost_estimate=pl.CostEstimate(flops=flops, bytes_accessed=moved, transcendentals=0),
-        compiler_params=pltpu.CompilerParams(vmem_limit_bytes=20 << 20),
+        compiler_params=pltpu.CompilerParams(vmem_limit_bytes=10 << 20),
     )(*args)
 
 
-def prepare_kernel(place_ref, bands_ref, pot_ref, held_ref, last_ref, slab_ref, sems):
-    nx, ny, nz, _ = bands_ref.shape
-    sent = jnp.where(place_ref[1] == 0, nx - 1, 0)
-    copies = (
-        pltpu.make_async_copy(bands_ref.at[:, ny - 1], last_ref, sems.at[0]),
-        pltpu.make_async_copy(bands_ref.at[sent], slab_ref, sems.at[1]),
-        pltpu.make_async_copy(bands_ref, held_ref.at[pl.ds(0, nx)], sems.at[2]),
-    )
-    for copy in copies:
-        copy.start()
-    rest = pot_ref[...].reshape(nx * ny, nz)
-    for piece in range(PIECES):
-        part = rest.astype(BF16)
-        held_ref[nx, piece, 0 : nx * ny, 0:nz] = part
-        rest = rest - part.astype(F32)
-    for copy in copies:
-        copy.wait()
-
-
-def prepare(place, bands, pot):
-    nx, ny, nz, nb = bands.shape
-    assert ny >= PIECES and nx * ny <= nz <= nb
-    shapes = ((nx + 1, ny, nz, nb), (nx, nz, nb), (ny, nz, nb))
-    return call(
-        prepare_kernel,
-        tuple(jax.ShapeDtypeStruct(s, BF16) for s in shapes),
-        [SMEM, pl.BlockSpec(memory_space=pltpu.HBM), VMEM],
-        (place, bands, pot),
-        scratch=[pltpu.SemaphoreType.DMA((3,))],
-    )
-
-
-def half_stencil(core, planes, pots, outs):
-    nx, ny, nz, nb = outs[0].shape
+def half_kernel(place_ref, bands_ref, pot_ref, *refs):
+    nx, ny, nz, nb = bands_ref.shape
+    right_ref = refs[-1]
+    given = refs[0][...] if refs[1].shape == (nb, nb) else None
+    gram_ref = refs[1] if given is not None else refs[0]
+    if given is None:
+        refs[1][...] = bands_ref[jnp.where(place_ref[1] == 0, nx - 1, 0)]
     row = lax.broadcasted_iota(jnp.int32, (nz, nb), 0)
-    half = jnp.where(core == 1, 0.5, 0.0).astype(F32)
-
-    def tiles_at(ref, x):
-        return [ref[x, y].astype(F32) for y in range(ny)]
-
-    def one(ref, pot_ref, out_ref, x, below):
+    half = jnp.where(place_ref[0] == 1, 0.5, 0.0).astype(F32)
+
+    def tiles_at(x):
+        return [bands_ref[x, y].astype(F32) for y in range(ny)]
+
+    def slab(x, first):
         pot = jnp.transpose(pot_ref[:, pl.ds(x, 1), :].reshape(ny, nz))
         factor = 0.5 + half * (2.0 + pot)
-        tiles = tiles_at(ref, x)
+        tiles = tiles_at(x)
+        below = None if first else tiles_at(x - 1)
         for y in range(ny):
             total = jnp.where(row > 0, pltpu.roll(tiles[y], 1, 0), 0.0)
             if y > 0:
                 total += tiles[y - 1]
-            if below is not None:
+            if not first:
                 total += below[y]
-            out_ref[x, y] = (factor[:, y : y + 1] * tiles[y] - half * total).astype(BF16)
-
-    low, high = planes
-    one(low, pots[0], outs[0], 0, None)
-    one(high, pots[1], outs[1], 0, tiles_at(low, nx - 1))
+            right_ref[x, y] = (factor[:, y : y + 1] * tiles[y] - half * total).astype(BF16)
 
     def step(x, carry):
-        for ref, pot, out in zip(planes, pots, outs):
-            one(ref, pot, out, x, tiles_at(ref, x - 1))
+        slab(x, False)
         return carry
 
-    lax.fori_loop(1, nx, step, 0)
-
-
-def local_kernel(place_ref, own_ref, other_ref, pot_ref, gram_ref, other_pot, right_own, right_other):
-    nx, ny, nz, nb = right_own.shape
-    pieces = [other_ref[nx, p, 0 : nx * ny, 0:nz].astype(F32) for p in range(PIECES)]
-    other_pot[...] = ((pieces[2] + pieces[1]) + pieces[0]).reshape(ny, nx, nz)
-    half_stencil(
-        place_ref[0], (other_ref, own_ref), (other_pot, pot_ref), (right_other, right_own)
-    )
-
-    def rows(ref):
-        return ref[0:nx].reshape(-1, nb)
-
-    gram_ref[...] = over_rows(rows(own_ref), rows(right_own)) + over_rows(
-        rows(other_ref), rows(right_other)
-    )
-
-
-def local_gram(place, own, other, pot, shape):
-    nx, ny, nz, nb = shape
-    return call(
-        local_kernel,
-        jax.ShapeDtypeStruct((nb, nb), F32),
-        [SMEM, VMEM, VMEM, VMEM],
-        (place, own, other, pot),
-        scratch=[pltpu.VMEM(pot.shape, F32)] + [pltpu.VMEM(shape, BF16)] * 2,
-        flops=4 * nx * ny * nz * nb * nb,
+    slab(0, True)
+    lax.fori_loop(1, nx, step, 0, unroll=True)
+    gram = over_rows(bands_ref[...].reshape(-1, nb), right_ref[...].reshape(-1, nb))
+    gram_ref[...] = gram if given is None else given + gram
+
+
+def half_gram(place, bands, pot, given=()):
+    nb = bands.shape[-1]
+    gram = jax.ShapeDtypeStruct((nb, nb), F32)
+    return call(
+        half_kernel,
+        gram if given else (gram, jax.ShapeDtypeStruct(bands.shape[1:], BF16)),
+        [SMEM] + [VMEM] * (2 + len(given)),
+        (place, bands, pot, *given),
+        scratch=[pltpu.VMEM(bands.shape, BF16)],
+        flops=2 * bands.size * nb,
     )
 
 
@@ -137,11 +93,12 @@
     def rows(value):
         return value.reshape(-1, nb)
 
-    cross = over_rows(rows(own_ref[0:nx, 0]), rows(yown_ref[...]))
-    cross += over_rows(rows(other_ref[0:nx, 0]), rows(yother_ref[...]))
+    cross = over_rows(rows(own_ref[:, 0]), rows(yown_ref[...]))
+    cross += over_rows(rows(other_ref[:, 0]), rows(yother_ref[...]))
     slab = jnp.where(place_ref[1] == 0, other_ref[0], own_ref[nx - 1])
     cross += over_rows(rows(slab), rows(xhalo_ref[...]))
-    gram = gram_ref[...] - 0.5 * cross
+    inside = over_rows(rows(own_ref[0]), rows(other_ref[nx - 1]))
+    gram = gram_ref[...] - 0.5 * (cross + jnp.where(place_ref[0] == 1, inside, 0.0))
     total = (scale * (gram + jnp.transpose(gram))).astype(BF16)
     total = total.reshape(nb // (groups * depth), groups, depth, nb)
     for d in range(groups):
@@ -259,17 +216,18 @@
     place = jnp.stack((core, odd)).astype(jnp.int32)
     pot = jnp.transpose(potential, (1, 0, 2))
 
-    own, last, slab = prepare(place, bands, pot)
     same, next_core, x_pairs = pairs_of(gx, gyz)
     partner = [(g, g ^ 1) for g in range(gx)]
+    last = bands[:, ny - 1]
     yother = lax.ppermute(last, BOTH, next_core)
     yown = lax.ppermute(last, BOTH, same)
+    other = lax.ppermute(bands, "gx", partner)
+    other_pot = lax.ppermute(pot, "gx", partner)
+    gram, slab = half_gram(place, bands, pot)
     xhalo = lax.ppermute(slab, BOTH, x_pairs)
-    other = lax.ppermute(own, "gx", partner)
-
-    gram = local_gram(place, own, other, pot, bands.shape)
+    gram = half_gram(place, other, other_pot, (gram,))
     sent = add_cross(
-        scale, inner, place, gram, own, other, yown, yother, xhalo, eigenvectors
+        scale, inner, place, gram, bands, other, yown, yother, xhalo, eigenvectors
     )
     arrived = exchanged(sent, "gyz", [[o * inner + i for i in range(inner)] for o in range(outer)])
     sent = middle(place, arrived, outer)

time: 84.1 us -> 85.8 us (1.020)
  starting transfers between devices: 30.5 us -> 28.6 us
  local copies, waits for them, and re-layouts: 2.78 us -> 4.51 us
  blocking collectives: 31.6 us -> 33.2 us
  waiting for transfers between devices: 6.19 us -> 7.27 us
  Pallas kernels: 9.46 us -> 8.59 us
    all_to_all x1, starting transfers between devices: 14.1 us -> 9.32 us  [exchanged(): return lax.all_to_all(x, axis, 0, 0, tiled=True, axis_index_groups=groups)]
    ppermute x1 -> x2, starting transfers between devices: 8.75 us -> 10.7 us  [the longest x1 8.75 us: projected(): other = lax.ppermute(bands, 'gx', partner)]
    squeeze x0 -> x1, local copies, waits for them, and re-layouts: none -> 1.73 us  [projected(): last = bands[:, ny - 1]]
    all_to_all x2, blocking collectives: 31.6 us -> 33.2 us  [exchanged(): return lax.all_to_all(x, axis, 0, 0, tiled=True, axis_index_groups=groups)]
    ppermute x1 -> x2, waiting for transfers between devices: 0.01 us -> 1.16 us  [the longest x1 1.16 us: projected(): other_pot = lax.ppermute(pot, 'gx', partner)]
    pallas_call x5, Pallas kernels: 9.46 us -> 8.59 us  [call(): pl.pallas_call(kernel, out_shape=out_shape, in_specs=in_specs, out_specs=...]
    unnamed x8 -> x10, local copies, waits for them, and re-layouts: 2.17 us -> 2.17 us
  transfers between devices with their start and end apart: 6 -> 7, of which waited for: 1 -> 2; matrix products, arithmetic and copies ran while one was open for 1% -> 3% of each run, Pallas kernels for 7% -> 6%
where the time goes in v6:
time: 85.8 us; the launch traced here: 85.3 us
  blocking collectives  33.2 us (39%)
  starting transfers between devices  28.6 us (33%)
  Pallas kernels  8.59 us (10%)
  waiting for transfers between devices  7.27 us (8%)
  local copies, waits for them, and re-layouts  4.51 us (5%)
  matrix products  2.18 us (3%)
    all_to_all x2, blocking collectives, exchanged(): return lax.all_to_all(x, axis, 0, 0, tiled=True, axis_index_groups=groups)  33.2 us
    all_to_all x1, starting transfers between devices, exchanged(): return lax.all_to_all(x, axis, 0, 0, tiled=True, axis_index_groups=groups)  9.32 us
    ppermute x1, starting transfers between devices, projected(): other = lax.ppermute(bands, 'gx', partner)  8.75 us
    pallas_call x5, Pallas kernels, call(): pl.pallas_call(kernel, out_shape=out_shape, in_specs=in_specs, out_specs=...  8.59 us
    all_to_all x1, waiting for transfers between devices, exchanged(): return lax.all_to_all(x, axis, 0, 0, tiled=True, axis_index_groups=groups)  6.11 us
    ppermute x1, starting transfers between devices, projected(): xhalo = lax.ppermute(slab, BOTH, x_pairs)  3.17 us
    dot_general x1, matrix products, projected(): jnp.dot(bands.reshape(cells, nb), jnp.concatenate((left, right), axis=1),...  2.18 us
    unnamed x10, local copies, waits for them, and re-layouts  2.17 us
  transfers between devices with their start and end apart: 7, of which 2 were waited for; matrix products, arithmetic and copies ran while one was open for 3% of the time, Pallas kernels for 6%

profile of v6, /device:TPU:1, one launch (start us, length us, event | category | flops | bytes accessed | tf_op | source)
XLA Modules:
  0.0 85.3 jit_solution(3890360158338467840)
XLA Ops:
  0.6 8.7 %collective-permute-start = (bf16[8,5,40,512]{3,2,1,0:T(8,128)(2,1)}, bf16[8,5,40,512]{3,2,1,0:T(8,128)(2,1)S(1)}, u32[]{:S(2)}, u32[]{:S(2)}) collective-permute-start(bf16[8,5,40,512]{3,2,1,0:T(8,128)(2,1)} %own_ref.1), channel_id=1, source_target_pairs={{0,64},{64,0},{128,192},{192,128},{256,320},{320,256},{384,448},{4... | collective-permute-start | bytes 4915208 | tf_op jit(solution)/shard_map/ppermute | solution.py:224
  9.4 1.7 %slice_bitcast_fusion = bf16[8,40,512]{2,1,0:T(8,128)(2,1)} fusion(bf16[8,5,40,512]{3,2,1,0:T(8,128)(2,1)} %own_ref.1), kind=kLoop, calls=%fused_computation.4 | loop fusion | bytes 655360 | tf_op jit(solution)/shard_map/squeeze | solution.py:221
  11.1 2.1 %collective-permute-start.2 = (bf16[8,40,512]{2,1,0:T(8,128)(2,1)}, bf16[8,40,512]{2,1,0:T(8,128)(2,1)}, u32[]{:S(2)}, u32[]{:S(2)}) collective-permute-start(bf16[8,40,512]{2,1,0:T(8,128)(2,1)} %slice_bitcast_fusion), channel_id=1, source_target_pairs={{64,65},{65,66},{66,67},{67,68},{68,69},{69,70},{70,71},{71,72},{7... | collective-permute-start | bytes 983048 | tf_op jit(solution)/shard_map/ppermute | solution.py:223
  13.3 1.4 %collective-permute-start.3 = (bf16[8,40,512]{2,1,0:T(8,128)(2,1)}, bf16[8,40,512]{2,1,0:T(8,128)(2,1)}, u32[]{:S(2)}, u32[]{:S(2)}) collective-permute-start(bf16[8,40,512]{2,1,0:T(8,128)(2,1)} %slice_bitcast_fusion), channel_id=1, source_target_pairs={{0,65},{1,66},{2,67},{3,68},{4,69},{5,70},{6,71},{7,72},{8,73},{9,... | collective-permute-start | bytes 983048 | tf_op jit(solution)/shard_map/ppermute | solution.py:222
  14.6 0.1 pad_add_fusion.place_ref
  14.7 1.4 %copy-done = bf16[8,5,40,512]{3,2,1,0:T(8,128)(2,1)S(1)} copy-done((bf16[8,5,40,512]{3,2,1,0:T(8,128)(2,1)S(1)}, bf16[8,5,40,512]{3,2,1,0:T(8,128)(2,1)}, u32[]{:S(2)}) %copy-start) | copy-done | bytes 1638424
  16.2 0.7 copy-done.3
  16.9 2.5 %shard_map.58 = (f32[512,512]{1,0:T(8,128)S(1)}, bf16[5,40,512]{2,1,0:T(8,128)(2,1)S(1)}) custom-call(s32[2]{0:T(128)S(1)} %pad_add_fusion.place_ref, bf16[8,5,40,512]{3,2,1,0:T(8,128)(2,1)S(1)} %copy-done, f32[5,8,40]{2,1,0:T(8,128)S(1)} %bitcast.18), custom_call_target="tpu_custom_call" | custom-call | flops 838860800 | bytes 1644808 | tf_op jit(solution)/shard_map/pallas_call | solution.py:26
  19.4 3.2 %collective-permute-start.4 = (bf16[5,40,512]{2,1,0:T(8,128)(2,1)S(1)}, bf16[5,40,512]{2,1,0:T(8,128)(2,1)S(1)}, u32[]{:S(2)}, u32[]{:S(2)}) collective-permute-start(bf16[5,40,512]{2,1,0:T(8,128)(2,1)S(1)} %get-tuple-element.8), channel_id=1, source_target_pairs={{64,192},{129,65},{66,194},{131,67},{68,196},{133,69},{70,198},{13... | collective-permute-start | bytes 614408 | tf_op jit(solution)/shard_map/ppermute | solution.py:227
  22.6 1.9 %collective-permute-start.1 = (f32[5,8,40]{2,1,0:T(8,128)S(1)}, f32[5,8,40]{2,1,0:T(8,128)S(1)}, u32[]{:S(2)}, u32[]{:S(2)}) collective-permute-start(f32[5,8,40]{2,1,0:T(8,128)S(1)} %bitcast.19), channel_id=1, source_target_pairs={{0,64},{64,0},{128,192},{192,128},{256,320},{320,256},{384,448},{4... | collective-permute-start | bytes 19208 | tf_op jit(solution)/shard_map/ppermute | solution.py:225
  24.5 1.2 %collective-permute-done.1.pot_ref = f32[5,8,40]{2,1,0:T(8,128)S(1)} collective-permute-done((f32[5,8,40]{2,1,0:T(8,128)S(1)}, f32[5,8,40]{2,1,0:T(8,128)S(1)}, u32[]{:S(2)}, u32[]{:S(2)}) %collective-permute-start.1) | collective-permute-done | bytes 6432 | tf_op jit(solution)/shard_map/ppermute | solution.py:225
  25.7 2.4 %shard_map.59.gram_ref = f32[512,512]{1,0:T(8,128)S(1)} custom-call(s32[2]{0:T(128)S(1)} %pad_add_fusion.place_ref, bf16[8,5,40,512]{3,2,1,0:T(8,128)(2,1)S(1)} %collective-permute-done.bands_ref.other_ref, f32[5,8,40]{2,1,0:T(8,128)S(1)} %collective-permute-done.1.pot_ref, f32[512,512]{1,0:T(8,128)S(1)} %get-tuple-element.7.refs_0_), custom_call_target="tpu_custom_call" | custom-call | flops 838860800 | bytes 2693384 | tf_op jit(solution)/shard_map/pallas_call | solution.py:26
  28.1 0.0 collective-permute-done.4.xhalo_ref
  28.1 0.0 collective-permute-done.2.yown_ref
  28.2 2.3 %shard_map.60 = bf16[8,72,512]{2,1,0:T(8,128)(2,1)S(1)} custom-call(s32[2]{0:T(128)S(1)} %pad_add_fusion.place_ref, f32[512,512]{1,0:T(8,128)S(1)} %shard_map.59.gram_ref, bf16[8,5,40,512]{3,2,1,0:T(8,128)(2,1)S(1)} %copy-done.1, bf16[8,5,40,512]{3,2,1,0:T(8,128)(2,1)S(1)} %collective-permute-done.bands_ref.other_ref, ...), custom_call_target="tpu_custom_call" | custom-call | flops 440401920 | bytes 5193736 | tf_op jit(solution)/shard_map/pallas_call | solution.py:26
  30.5 15.0 %all_to_all.15.in_ref = bf16[8,72,512]{2,1,0:T(8,128)(2,1)S(1)} all-to-all(bf16[8,72,512]{2,1,0:T(8,128)(2,1)S(1)} %shard_map.60), channel_id=1, replica_groups={{0,1,2,3,4,5,6,7},{8,9,10,11,12,13,14,15},{16,17,18,19,20,21,22,23},{24..., dimensions={0} | all-to-all | bytes 1179648 | tf_op jit(solution)/shard_map/all_to_all | solution.py:203
  45.5 0.6 shard_map.61
  46.1 18.3 %all_to_all.16.in_ref = bf16[8,40,512]{2,1,0:T(8,128)(2,1)S(1)} all-to-all(bf16[8,40,512]{2,1,0:T(8,128)(2,1)S(1)} %shard_map.61), channel_id=1, replica_groups={{0,8,16,24,32,40,48,56},{1,9,17,25,33,41,49,57},{2,10,18,26,34,42,50,58..., dimensions={0} | all-to-all | bytes 655360 | tf_op jit(solution)/shard_map/all_to_all | solution.py:203
  64.4 0.7 shard_map.62
  65.1 9.3 %all-to-all-start.2 = ((f32[8,8,512]{2,1,0:T(8,128)}), f32[8,8,512]{2,1,0:T(8,128)S(1)}, u32[]{:S(2)}, u32[]{:S(2)}) async-start(f32[8,8,512]{2,1,0:T(8,128)} %get-tuple-element.9), calls=%async_computation.2 | async-start | bytes 262144 | tf_op jit(solution)/shard_map/all_to_all | solution.py:203
  74.4 1.9 %collective-permute-start.5 = (bf16[512,256]{1,0:T(8,128)(2,1)S(1)}, bf16[512,256]{1,0:T(8,128)(2,1)S(1)}, u32[]{:S(2)}, u32[]{:S(2)}) collective-permute-start(bf16[512,256]{1,0:T(8,128)(2,1)S(1)} %get-tuple-element.10), channel_id=1, source_target_pairs={{0,64},{64,0},{128,192},{192,128},{256,320},{320,256},{384,448},{4... | collective-permute-start | bytes 786440 | tf_op jit(solution)/shard_map/ppermute | solution.py:236
  76.3 6.1 %all-to-all-done.2 = f32[8,8,512]{2,1,0:T(8,128)S(1)} async-done(((f32[8,8,512]{2,1,0:T(8,128)}), f32[8,8,512]{2,1,0:T(8,128)S(1)}, u32[]{:S(2)}, u32[]{:S(2)}) %all-to-all-start.2) | async-done | bytes 131104 | tf_op jit(solution)/shard_map/all_to_all | solution.py:203
  82.4 0.6 slice_bitcast_fusion.1
  83.1 2.2 %convolution_convert_fusion = bf16[512,1600]{0,1:T(8,128)(2,1)} fusion(bf16[1600,512]{1,0:T(8,128)(2,1)S(1)} %bitcast.17, bf16[512,256]{1,0:T(8,128)(2,1)S(1)} %get-tuple-element.12, bf16[512,256]{1,0:T(8,128)(2,1)S(1)} %get-tuple-element.11), kind=kOutput, calls=%fused_computation | convolution fusion | flops 840728576 | bytes 3801088 | tf_op jit(solution)/shard_map/dot_general | solution.py:242
  (13 shorter events, 0.1 us)
Async XLA Ops:
  0.6 25.1 %collective-permute-start = (bf16[8,5,40,512]{3,2,1,0:T(8,128)(2,1)}, bf16[8,5,40,512]{3,2,1,0:T(8,128)(2,1)S(1)}, u32[]{:S(2)}, u32[]{:S(2)}) collective-permute-start(bf16[8,5,40,512]{3,2,1,0:T(8,128)(2,1)} %own_ref.1), channel_id=1, source_target_pairs={{0,64},{64,0},{128,192},{192,128},{256,320},{320,256},{384,448},{4... | collective-permute-start | bytes 4915208 | tf_op jit(solution)/shard_map/ppermute | solution.py:224
  11.1 11.5 %copy-start.4 = (f32[8,5,40]{2,0,1:T(8,128)S(1)}, f32[8,5,40]{2,0,1:T(8,128)}, u32[]{:S(2)}) copy-start(f32[8,5,40]{2,0,1:T(8,128)} %param.4) | copy-start | bytes 19204
  11.1 17.0 %collective-permute-start.2 = (bf16[8,40,512]{2,1,0:T(8,128)(2,1)}, bf16[8,40,512]{2,1,0:T(8,128)(2,1)}, u32[]{:S(2)}, u32[]{:S(2)}) collective-permute-start(bf16[8,40,512]{2,1,0:T(8,128)(2,1)} %slice_bitcast_fusion), channel_id=1, source_target_pairs={{64,65},{65,66},{66,67},{67,68},{68,69},{69,70},{70,71},{71,72},{7... | collective-permute-start | bytes 983048 | tf_op jit(solution)/shard_map/ppermute | solution.py:223
  13.3 14.9 %collective-permute-start.3 = (bf16[8,40,512]{2,1,0:T(8,128)(2,1)}, bf16[8,40,512]{2,1,0:T(8,128)(2,1)}, u32[]{:S(2)}, u32[]{:S(2)}) collective-permute-start(bf16[8,40,512]{2,1,0:T(8,128)(2,1)} %slice_bitcast_fusion), channel_id=1, source_target_pairs={{0,65},{1,66},{2,67},{3,68},{4,69},{5,70},{6,71},{7,72},{8,73},{9,... | collective-permute-start | bytes 983048 | tf_op jit(solution)/shard_map/ppermute | solution.py:222
  14.7 1.4 %copy-start = (bf16[8,5,40,512]{3,2,1,0:T(8,128)(2,1)S(1)}, bf16[8,5,40,512]{3,2,1,0:T(8,128)(2,1)}, u32[]{:S(2)}) copy-start(bf16[8,5,40,512]{3,2,1,0:T(8,128)(2,1)} %own_ref.1) | copy-start | bytes 4915204
  16.2 0.7 copy-start.3
  19.4 8.7 %collective-permute-start.4 = (bf16[5,40,512]{2,1,0:T(8,128)(2,1)S(1)}, bf16[5,40,512]{2,1,0:T(8,128)(2,1)S(1)}, u32[]{:S(2)}, u32[]{:S(2)}) collective-permute-start(bf16[5,40,512]{2,1,0:T(8,128)(2,1)S(1)} %get-tuple-element.8), channel_id=1, source_target_pairs={{64,192},{129,65},{66,194},{131,67},{68,196},{133,69},{70,198},{13... | collective-permute-start | bytes 614408 | tf_op jit(solution)/shard_map/ppermute | solution.py:227
  22.6 3.1 %collective-permute-start.1 = (f32[5,8,40]{2,1,0:T(8,128)S(1)}, f32[5,8,40]{2,1,0:T(8,128)S(1)}, u32[]{:S(2)}, u32[]{:S(2)}) collective-permute-start(f32[5,8,40]{2,1,0:T(8,128)S(1)} %bitcast.19), channel_id=1, source_target_pairs={{0,64},{64,0},{128,192},{192,128},{256,320},{320,256},{384,448},{4... | collective-permute-start | bytes 19208 | tf_op jit(solution)/shard_map/ppermute | solution.py:225
  25.7 2.5 %copy-start.1 = (bf16[8,5,40,512]{3,2,1,0:T(8,128)(2,1)S(1)}, bf16[8,5,40,512]{3,2,1,0:T(8,128)(2,1)}, u32[]{:S(2)}) copy-start(bf16[8,5,40,512]{3,2,1,0:T(8,128)(2,1)} %own_ref.1) | copy-start | bytes 4915204
  25.7 2.5 %copy-start.2 = (bf16[8,512]{1,0:T(8,128)(2,1)S(1)}, bf16[8,512]{1,0:T(8,128)(2,1)}, u32[]{:S(2)}) copy-start(bf16[8,512]{1,0:T(8,128)(2,1)} %coef_ref.1) | copy-start | bytes 24580
  65.1 17.3 %all-to-all-start.2 = ((f32[8,8,512]{2,1,0:T(8,128)}), f32[8,8,512]{2,1,0:T(8,128)S(1)}, u32[]{:S(2)}, u32[]{:S(2)}) async-start(f32[8,8,512]{2,1,0:T(8,128)} %get-tuple-element.9), calls=%async_computation.2 | async-start | bytes 262144 | tf_op jit(solution)/shard_map/all_to_all | solution.py:203
  74.4 8.7 %collective-permute-start.5 = (bf16[512,256]{1,0:T(8,128)(2,1)S(1)}, bf16[512,256]{1,0:T(8,128)(2,1)S(1)}, u32[]{:S(2)}, u32[]{:S(2)}) collective-permute-start(bf16[512,256]{1,0:T(8,128)(2,1)S(1)} %get-tuple-element.10), channel_id=1, source_target_pairs={{0,64},{64,0},{128,192},{192,128},{256,320},{320,256},{384,448},{4... | collective-permute-start | bytes 786440 | tf_op jit(solution)/shard_map/ppermute | solution.py:236

commit v7 on v6

--- a/solution.py
+++ b/solution.py
@@ -12,7 +12,10 @@
 BF16 = jnp.bfloat16
 BOTH = ("gx", "gyz")
 
+PIECES = 3
+
 VMEM = pl.BlockSpec(memory_space=pltpu.VMEM)
+HBM = pl.BlockSpec(memory_space=pltpu.HBM)
 SMEM = pl.BlockSpec(memory_space=pltpu.SMEM)
 
 
@@ -34,18 +37,51 @@
     )(*args)
 
 
-def half_kernel(place_ref, bands_ref, pot_ref, *refs):
-    nx, ny, nz, nb = bands_ref.shape
-    right_ref = refs[-1]
-    given = refs[0][...] if refs[1].shape == (nb, nb) else None
-    gram_ref = refs[1] if given is not None else refs[0]
-    if given is None:
-        refs[1][...] = bands_ref[jnp.where(place_ref[1] == 0, nx - 1, 0)]
+def prepare_kernel(place_ref, bands_ref, pot_ref, held_ref, last_ref, slab_ref, pot_vmem, sems):
+    nx, ny, nz, _ = bands_ref.shape
+    sent = jnp.where(place_ref[1] == 0, nx - 1, 0)
+    copies = (
+        pltpu.make_async_copy(pot_ref, pot_vmem, sems.at[0]),
+        pltpu.make_async_copy(bands_ref.at[:, ny - 1], last_ref, sems.at[1]),
+        pltpu.make_async_copy(bands_ref.at[sent], slab_ref, sems.at[2]),
+        pltpu.make_async_copy(bands_ref, held_ref.at[pl.ds(0, nx)], sems.at[3]),
+    )
+    for copy in copies:
+        copy.start()
+    copies[0].wait()
+    rest = pot_vmem[...].reshape(nx * ny, nz)
+    for piece in range(PIECES):
+        part = rest.astype(BF16)
+        held_ref[nx, piece, 0 : nx * ny, 0:nz] = part
+        rest = rest - part.astype(F32)
+    for copy in copies[1:]:
+        copy.wait()
+
+
+def prepare(place, bands, pot):
+    nx, ny, nz, nb = bands.shape
+    assert ny >= PIECES and nx * ny <= nz <= nb
+    shapes = ((nx + 1, ny, nz, nb), (nx, nz, nb), (ny, nz, nb))
+    bands, pot = (pltpu.with_memory_space_constraint(x, pltpu.HBM) for x in (bands, pot))
+    return call(
+        prepare_kernel,
+        tuple(jax.ShapeDtypeStruct(s, BF16) for s in shapes),
+        [SMEM, HBM, HBM],
+        (place, bands, pot),
+        scratch=[pltpu.VMEM(pot.shape, F32), pltpu.SemaphoreType.DMA((4,))],
+    )
+
+
+def half_kernel(place_ref, held_ref, *refs):
+    gram_ref, right_ref, pot_ref = refs[-3:]
+    nx, ny, nz, nb = right_ref.shape
     row = lax.broadcasted_iota(jnp.int32, (nz, nb), 0)
     half = jnp.where(place_ref[0] == 1, 0.5, 0.0).astype(F32)
+    pieces = [held_ref[nx, p, 0 : nx * ny, 0:nz].astype(F32) for p in range(PIECES)]
+    pot_ref[...] = ((pieces[2] + pieces[1]) + pieces[0]).reshape(ny, nx, nz)
 
     def tiles_at(x):
-        return [bands_ref[x, y].astype(F32) for y in range(ny)]
+        return [held_ref[x, y].astype(F32) for y in range(ny)]
 
     def slab(x, first):
         pot = jnp.transpose(pot_ref[:, pl.ds(x, 1), :].reshape(ny, nz))
@@ -66,20 +102,20 @@
 
     slab(0, True)
     lax.fori_loop(1, nx, step, 0, unroll=True)
-    gram = over_rows(bands_ref[...].reshape(-1, nb), right_ref[...].reshape(-1, nb))
-    gram_ref[...] = gram if given is None else given + gram
-
-
-def half_gram(place, bands, pot, given=()):
-    nb = bands.shape[-1]
-    gram = jax.ShapeDtypeStruct((nb, nb), F32)
+    gram = over_rows(held_ref[0:nx].reshape(-1, nb), right_ref[...].reshape(-1, nb))
+    gram_ref[...] = refs[0][...] + gram if len(refs) > 3 else gram
+
+
+def half_gram(place, held, given=()):
+    nx, ny, nz, nb = held.shape
+    nx -= 1
     return call(
         half_kernel,
-        gram if given else (gram, jax.ShapeDtypeStruct(bands.shape[1:], BF16)),
-        [SMEM] + [VMEM] * (2 + len(given)),
-        (place, bands, pot, *given),
-        scratch=[pltpu.VMEM(bands.shape, BF16)],
-        flops=2 * bands.size * nb,
+        jax.ShapeDtypeStruct((nb, nb), F32),
+        [SMEM] + [VMEM] * (1 + len(given)),
+        (place, held, *given),
+        scratch=[pltpu.VMEM((nx, ny, nz, nb), BF16), pltpu.VMEM((ny, nx, nz), F32)],
+        flops=2 * nx * ny * nz * nb * nb,
     )
 
 
@@ -93,8 +129,8 @@
     def rows(value):
         return value.reshape(-1, nb)
 
-    cross = over_rows(rows(own_ref[:, 0]), rows(yown_ref[...]))
-    cross += over_rows(rows(other_ref[:, 0]), rows(yother_ref[...]))
+    cross = over_rows(rows(own_ref[0:nx, 0]), rows(yown_ref[...]))
+    cross += over_rows(rows(other_ref[0:nx, 0]), rows(yother_ref[...]))
     slab = jnp.where(place_ref[1] == 0, other_ref[0], own_ref[nx - 1])
     cross += over_rows(rows(slab), rows(xhalo_ref[...]))
     inside = over_rows(rows(own_ref[0]), rows(other_ref[nx - 1]))
@@ -216,18 +252,17 @@
     place = jnp.stack((core, odd)).astype(jnp.int32)
     pot = jnp.transpose(potential, (1, 0, 2))
 
+    own, last, slab = prepare(place, bands, pot)
     same, next_core, x_pairs = pairs_of(gx, gyz)
     partner = [(g, g ^ 1) for g in range(gx)]
-    last = bands[:, ny - 1]
     yother = lax.ppermute(last, BOTH, next_core)
     yown = lax.ppermute(last, BOTH, same)
-    other = lax.ppermute(bands, "gx", partner)
-    other_pot = lax.ppermute(pot, "gx", partner)
-    gram, slab = half_gram(place, bands, pot)
+    other = lax.ppermute(own, "gx", partner)
     xhalo = lax.ppermute(slab, BOTH, x_pairs)
-    gram = half_gram(place, other, other_pot, (gram,))
+    gram = half_gram(place, own)
+    gram = half_gram(place, other, (gram,))
     sent = add_cross(
-        scale, inner, place, gram, bands, other, yown, yother, xhalo, eigenvectors
+        scale, inner, place, gram, own, other, yown, yother, xhalo, eigenvectors
     )
     arrived = exchanged(sent, "gyz", [[o * inner + i for i in range(inner)] for o in range(outer)])
     sent = middle(place, arrived, outer)

time: 85.8 us -> 82.6 us (0.963)
  local copies, waits for them, and re-layouts: 4.51 us -> 0.62 us
  Pallas kernels: 8.59 us -> 10.3 us
  blocking collectives: 33.2 us -> 31.7 us
  starting transfers between devices: 28.6 us -> 29.5 us
    all_to_all x1, starting transfers between devices: 9.32 us -> 13.7 us  [exchanged(): return lax.all_to_all(x, axis, 0, 0, tiled=True, axis_index_groups=groups)]
    unnamed x10 -> x4, local copies, waits for them, and re-layouts: 2.17 us -> 0.01 us
    ppermute x2 -> x1, starting transfers between devices: 10.7 us -> 8.75 us  [projected(): other = lax.ppermute(own, 'gx', partner)]
    squeeze x1 -> x0, local copies, waits for them, and re-layouts: 1.73 us -> none  [projected(): last = bands[:, ny - 1]]
    pallas_call x5 -> x6, Pallas kernels: 8.59 us -> 10.3 us  [call(): pl.pallas_call(kernel, out_shape=out_shape, in_specs=in_specs, out_specs=...]
    all_to_all x2, blocking collectives: 33.2 us -> 31.7 us  [exchanged(): return lax.all_to_all(x, axis, 0, 0, tiled=True, axis_index_groups=groups)]
    ppermute x2 -> x1, waiting for transfers between devices: 1.16 us -> 0.01 us  [projected(): other = lax.ppermute(own, 'gx', partner)]
  transfers between devices with their start and end apart: 7 -> 6, of which waited for: 2 -> 2; matrix products, arithmetic and copies ran while one was open for 3% -> 1% of each run, Pallas kernels for 6% -> 6%
where the time goes in v7:
time: 82.6 us; the launch traced here: 82.2 us
  blocking collectives  31.7 us (38%)
  starting transfers between devices  29.5 us (36%)
  Pallas kernels  10.3 us (12%)
  waiting for transfers between devices  6.99 us (8%)
  matrix products  2.18 us (3%)
    all_to_all x2, blocking collectives, exchanged(): return lax.all_to_all(x, axis, 0, 0, tiled=True, axis_index_groups=groups)  31.7 us
    all_to_all x1, starting transfers between devices, exchanged(): return lax.all_to_all(x, axis, 0, 0, tiled=True, axis_index_groups=groups)  13.7 us
    pallas_call x6, Pallas kernels, call(): pl.pallas_call(kernel, out_shape=out_shape, in_specs=in_specs, out_specs=...  10.3 us
    ppermute x1, starting transfers between devices, projected(): other = lax.ppermute(own, 'gx', partner)  8.75 us
    all_to_all x1, waiting for transfers between devices, exchanged(): return lax.all_to_all(x, axis, 0, 0, tiled=True, axis_index_groups=groups)  6.18 us
    ppermute x1, starting transfers between devices, projected(): xhalo = lax.ppermute(slab, BOTH, x_pairs)  3.18 us
    dot_general x1, matrix products, projected(): jnp.dot(bands.reshape(cells, nb), jnp.concatenate((left, right), axis=1),...  2.18 us
    ppermute x1, starting transfers between devices, projected(): coef_other = lax.ppermute(coef, 'gx', partner)  1.91 us
  transfers between devices with their start and end apart: 6, of which 2 were waited for; matrix products, arithmetic and copies ran while one was open for 1% of the time, Pallas kernels for 6%

profile of v7, /device:TPU:1, one launch (start us, length us, event | category | flops | bytes accessed | tf_op | source)
XLA Modules:
  0.0 82.2 jit_solution(12562622130658938564)
XLA Ops:
  0.6 0.1 pad_add_fusion.place_ref
  0.7 2.2 %shard_map.58 = (bf16[9,5,40,512]{3,2,1,0:T(8,128)(2,1)S(1)}, bf16[8,40,512]{2,1,0:T(8,128)(2,1)S(1)}, bf16[5,40,512]{2,1,0:T(8,128)(2,1)S(1)}) custom-call(s32[2]{0:T(128)S(1)} %pad_add_fusion.place_ref, bf16[8,5,40,512]{3,2,1,0:T(8,128)(2,1)} %bands_ref.1, f32[5,8,40]{2,1,0:T(8,128)} %bitcast.15), custom_call_target="tpu_custom_call" | custom-call | bytes 1644808 | tf_op jit(solution)/shard_map/pallas_call | solution.py:29
  3.0 8.7 %collective-permute-start = (bf16[9,5,40,512]{3,2,1,0:T(8,128)(2,1)S(1)}, bf16[9,5,40,512]{3,2,1,0:T(8,128)(2,1)S(1)}, u32[]{:S(2)}, u32[]{:S(2)}) collective-permute-start(bf16[9,5,40,512]{3,2,1,0:T(8,128)(2,1)S(1)} %get-tuple-element.8.held_ref.own_ref), channel_id=1, source_target_pairs={{0,64},{64,0},{128,192},{192,128},{256,320},{320,256},{384,448},{4... | collective-permute-start | bytes 5529608 | tf_op jit(solution)/shard_map/ppermute | solution.py:260
  11.7 1.3 %collective-permute-start.1 = (bf16[8,40,512]{2,1,0:T(8,128)(2,1)S(1)}, bf16[8,40,512]{2,1,0:T(8,128)(2,1)S(1)}, u32[]{:S(2)}, u32[]{:S(2)}) collective-permute-start(bf16[8,40,512]{2,1,0:T(8,128)(2,1)S(1)} %get-tuple-element.9), channel_id=1, source_target_pairs={{64,65},{65,66},{66,67},{67,68},{68,69},{69,70},{70,71},{71,72},{7... | collective-permute-start | bytes 983048 | tf_op jit(solution)/shard_map/ppermute | solution.py:259
  13.0 0.7 collective-permute-start.2
  13.7 3.2 %collective-permute-start.3 = (bf16[5,40,512]{2,1,0:T(8,128)(2,1)S(1)}, bf16[5,40,512]{2,1,0:T(8,128)(2,1)S(1)}, u32[]{:S(2)}, u32[]{:S(2)}) collective-permute-start(bf16[5,40,512]{2,1,0:T(8,128)(2,1)S(1)} %get-tuple-element.10), channel_id=1, source_target_pairs={{64,192},{129,65},{66,194},{131,67},{68,196},{133,69},{70,198},{13... | collective-permute-start | bytes 614408 | tf_op jit(solution)/shard_map/ppermute | solution.py:261
  16.9 2.5 %shard_map.59.refs_0_ = f32[512,512]{1,0:T(8,128)S(1)} custom-call(s32[2]{0:T(128)S(1)} %pad_add_fusion.place_ref, bf16[9,5,40,512]{3,2,1,0:T(8,128)(2,1)S(1)} %get-tuple-element.8.held_ref.own_ref), custom_call_target="tpu_custom_call" | custom-call | flops 838860800 | bytes 1843208 | tf_op jit(solution)/shard_map/pallas_call | solution.py:29
  19.4 0.0 copy-start
  19.4 0.0 collective-permute-done.held_ref.other_ref
  19.4 2.5 %shard_map.60.gram_ref = f32[512,512]{1,0:T(8,128)S(1)} custom-call(s32[2]{0:T(128)S(1)} %pad_add_fusion.place_ref, bf16[9,5,40,512]{3,2,1,0:T(8,128)(2,1)S(1)} %collective-permute-done.held_ref.other_ref, f32[512,512]{1,0:T(8,128)S(1)} %shard_map.59.refs_0_), custom_call_target="tpu_custom_call" | custom-call | flops 838860800 | bytes 2891784 | tf_op jit(solution)/shard_map/pallas_call | solution.py:29
  21.9 0.8 collective-permute-done.3.xhalo_ref
  22.7 0.0 collective-permute-done.1.yown_ref
  22.7 0.0 collective-permute-done.2.yother_ref
  22.7 1.8 %shard_map.61 = bf16[8,72,512]{2,1,0:T(8,128)(2,1)S(1)} custom-call(s32[2]{0:T(128)S(1)} %pad_add_fusion.place_ref, f32[512,512]{1,0:T(8,128)S(1)} %shard_map.60.gram_ref, bf16[9,5,40,512]{3,2,1,0:T(8,128)(2,1)S(1)} %get-tuple-element.8.held_ref.own_ref, bf16[9,5,40,512]{3,2,1,0:T(8,128)(2,1)S(1)} %collective-permute-done.held_ref.other_ref, ...), custom_call_target="tpu_custom_call" | custom-call | flops 440401920 | bytes 5603336 | tf_op jit(solution)/shard_map/pallas_call | solution.py:29
  24.5 14.3 %all_to_all.15.in_ref = bf16[8,72,512]{2,1,0:T(8,128)(2,1)S(1)} all-to-all(bf16[8,72,512]{2,1,0:T(8,128)(2,1)S(1)} %shard_map.61), channel_id=1, replica_groups={{0,1,2,3,4,5,6,7},{8,9,10,11,12,13,14,15},{16,17,18,19,20,21,22,23},{24..., dimensions={0} | all-to-all | bytes 1179648 | tf_op jit(solution)/shard_map/all_to_all | solution.py:239
  38.8 0.6 shard_map.62
  39.5 17.4 %all_to_all.16.in_ref = bf16[8,40,512]{2,1,0:T(8,128)(2,1)S(1)} all-to-all(bf16[8,40,512]{2,1,0:T(8,128)(2,1)S(1)} %shard_map.62), channel_id=1, replica_groups={{0,8,16,24,32,40,48,56},{1,9,17,25,33,41,49,57},{2,10,18,26,34,42,50,58..., dimensions={0} | all-to-all | bytes 655360 | tf_op jit(solution)/shard_map/all_to_all | solution.py:239
  56.8 0.7 shard_map.63
  57.5 13.7 %all-to-all-start.2 = ((f32[8,8,512]{2,1,0:T(8,128)}), f32[8,8,512]{2,1,0:T(8,128)S(1)}, u32[]{:S(2)}, u32[]{:S(2)}) async-start(f32[8,8,512]{2,1,0:T(8,128)} %get-tuple-element.11), calls=%async_computation.2 | async-start | bytes 262144 | tf_op jit(solution)/shard_map/all_to_all | solution.py:239
  71.2 1.9 %collective-permute-start.4 = (bf16[512,256]{1,0:T(8,128)(2,1)S(1)}, bf16[512,256]{1,0:T(8,128)(2,1)S(1)}, u32[]{:S(2)}, u32[]{:S(2)}) collective-permute-start(bf16[512,256]{1,0:T(8,128)(2,1)S(1)} %get-tuple-element.12), channel_id=1, source_target_pairs={{0,64},{64,0},{128,192},{192,128},{256,320},{320,256},{384,448},{4... | collective-permute-start | bytes 786440 | tf_op jit(solution)/shard_map/ppermute | solution.py:271
  73.2 6.2 %all-to-all-done.2 = f32[8,8,512]{2,1,0:T(8,128)S(1)} async-done(((f32[8,8,512]{2,1,0:T(8,128)}), f32[8,8,512]{2,1,0:T(8,128)S(1)}, u32[]{:S(2)}, u32[]{:S(2)}) %all-to-all-start.2) | async-done | bytes 131104 | tf_op jit(solution)/shard_map/all_to_all | solution.py:239
  79.4 0.6 slice_bitcast_fusion
  80.0 0.0 collective-permute-done.4
  80.0 2.2 %convolution_convert_fusion = bf16[512,1600]{0,1:T(8,128)(2,1)} fusion(bf16[1600,512]{1,0:T(8,128)(2,1)S(1)} %bitcast.13, bf16[512,256]{1,0:T(8,128)(2,1)S(1)} %get-tuple-element.14, bf16[512,256]{1,0:T(8,128)(2,1)S(1)} %get-tuple-element.13), kind=kOutput, calls=%fused_computation | convolution fusion | flops 840728576 | bytes 3801088 | tf_op jit(solution)/shard_map/dot_general | solution.py:277
  (5 shorter events, 0.1 us)
Async XLA Ops:
  3.0 16.5 %collective-permute-start = (bf16[9,5,40,512]{3,2,1,0:T(8,128)(2,1)S(1)}, bf16[9,5,40,512]{3,2,1,0:T(8,128)(2,1)S(1)}, u32[]{:S(2)}, u32[]{:S(2)}) collective-permute-start(bf16[9,5,40,512]{3,2,1,0:T(8,128)(2,1)S(1)} %get-tuple-element.8.held_ref.own_ref), channel_id=1, source_target_pairs={{0,64},{64,0},{128,192},{192,128},{256,320},{320,256},{384,448},{4... | collective-permute-start | bytes 5529608 | tf_op jit(solution)/shard_map/ppermute | solution.py:260
  11.7 11.0 %collective-permute-start.1 = (bf16[8,40,512]{2,1,0:T(8,128)(2,1)S(1)}, bf16[8,40,512]{2,1,0:T(8,128)(2,1)S(1)}, u32[]{:S(2)}, u32[]{:S(2)}) collective-permute-start(bf16[8,40,512]{2,1,0:T(8,128)(2,1)S(1)} %get-tuple-element.9), channel_id=1, source_target_pairs={{64,65},{65,66},{66,67},{67,68},{68,69},{69,70},{70,71},{71,72},{7... | collective-permute-start | bytes 983048 | tf_op jit(solution)/shard_map/ppermute | solution.py:259
  13.0 9.7 %collective-permute-start.2 = (bf16[8,40,512]{2,1,0:T(8,128)(2,1)S(1)}, bf16[8,40,512]{2,1,0:T(8,128)(2,1)S(1)}, u32[]{:S(2)}, u32[]{:S(2)}) collective-permute-start(bf16[8,40,512]{2,1,0:T(8,128)(2,1)S(1)} %get-tuple-element.9), channel_id=1, source_target_pairs={{0,65},{1,66},{2,67},{3,68},{4,69},{5,70},{6,71},{7,72},{8,73},{9,... | collective-permute-start | bytes 983048 | tf_op jit(solution)/shard_map/ppermute | solution.py:258
  13.7 9.0 %collective-permute-start.3 = (bf16[5,40,512]{2,1,0:T(8,128)(2,1)S(1)}, bf16[5,40,512]{2,1,0:T(8,128)(2,1)S(1)}, u32[]{:S(2)}, u32[]{:S(2)}) collective-permute-start(bf16[5,40,512]{2,1,0:T(8,128)(2,1)S(1)} %get-tuple-element.10), channel_id=1, source_target_pairs={{64,192},{129,65},{66,194},{131,67},{68,196},{133,69},{70,198},{13... | collective-permute-start | bytes 614408 | tf_op jit(solution)/shard_map/ppermute | solution.py:261
  19.4 3.3 %copy-start = (bf16[8,512]{1,0:T(8,128)(2,1)S(1)}, bf16[8,512]{1,0:T(8,128)(2,1)}, u32[]{:S(2)}) copy-start(bf16[8,512]{1,0:T(8,128)(2,1)} %coef_ref.1) | copy-start | bytes 24580
  38.8 41.2 %copy-start.1 = (bf16[8,5,40,512]{3,2,1,0:T(8,128)(2,1)S(1)}, bf16[8,5,40,512]{3,2,1,0:T(8,128)(2,1)}, u32[]{:S(2)}) copy-start(bf16[8,5,40,512]{3,2,1,0:T(8,128)(2,1)} %bands_ref.1) | copy-start | bytes 4915204
  57.5 21.8 %all-to-all-start.2 = ((f32[8,8,512]{2,1,0:T(8,128)}), f32[8,8,512]{2,1,0:T(8,128)S(1)}, u32[]{:S(2)}, u32[]{:S(2)}) async-start(f32[8,8,512]{2,1,0:T(8,128)} %get-tuple-element.11), calls=%async_computation.2 | async-start | bytes 262144 | tf_op jit(solution)/shard_map/all_to_all | solution.py:239
  71.2 8.7 %collective-permute-start.4 = (bf16[512,256]{1,0:T(8,128)(2,1)S(1)}, bf16[512,256]{1,0:T(8,128)(2,1)S(1)}, u32[]{:S(2)}, u32[]{:S(2)}) collective-permute-start(bf16[512,256]{1,0:T(8,128)(2,1)S(1)} %get-tuple-element.12), channel_id=1, source_target_pairs={{0,64},{64,0},{128,192},{192,128},{256,320},{320,256},{384,448},{4... | collective-permute-start | bytes 786440 | tf_op jit(solution)/shard_map/ppermute | solution.py:271

commit v8 on v7

--- a/solution.py
+++ b/solution.py
@@ -76,34 +76,39 @@
     gram_ref, right_ref, pot_ref = refs[-3:]
     nx, ny, nz, nb = right_ref.shape
     row = lax.broadcasted_iota(jnp.int32, (nz, nb), 0)
-    half = jnp.where(place_ref[0] == 1, 0.5, 0.0).astype(F32)
-    pieces = [held_ref[nx, p, 0 : nx * ny, 0:nz].astype(F32) for p in range(PIECES)]
-    pot_ref[...] = ((pieces[2] + pieces[1]) + pieces[0]).reshape(ny, nx, nz)
 
     def tiles_at(x):
         return [held_ref[x, y].astype(F32) for y in range(ny)]
 
-    def slab(x, first):
+    def slab(x):
         pot = jnp.transpose(pot_ref[:, pl.ds(x, 1), :].reshape(ny, nz))
-        factor = 0.5 + half * (2.0 + pot)
+        factor = 1.5 + 0.5 * pot
         tiles = tiles_at(x)
-        below = None if first else tiles_at(x - 1)
+        below = None if x == 0 else tiles_at(x - 1)
         for y in range(ny):
             total = jnp.where(row > 0, pltpu.roll(tiles[y], 1, 0), 0.0)
             if y > 0:
                 total += tiles[y - 1]
-            if not first:
+            if x > 0:
                 total += below[y]
-            right_ref[x, y] = (factor[:, y : y + 1] * tiles[y] - half * total).astype(BF16)
-
-    def step(x, carry):
-        slab(x, False)
-        return carry
-
-    slab(0, True)
-    lax.fori_loop(1, nx, step, 0, unroll=True)
-    gram = over_rows(held_ref[0:nx].reshape(-1, nb), right_ref[...].reshape(-1, nb))
-    gram_ref[...] = refs[0][...] + gram if len(refs) > 3 else gram
+            right_ref[x, y] = (factor[:, y : y + 1] * tiles[y] - 0.5 * total).astype(BF16)
+
+    def store(gram):
+        gram_ref[...] = refs[0][...] + gram if len(refs) > 3 else gram
+
+    bands = held_ref[0:nx].reshape(-1, nb)
+
+    @pl.when(place_ref[0] == 1)
+    def _():
+        pieces = [held_ref[nx, p, 0 : nx * ny, 0:nz].astype(F32) for p in range(PIECES)]
+        pot_ref[...] = ((pieces[2] + pieces[1]) + pieces[0]).reshape(ny, nx, nz)
+        for x in range(nx):
+            slab(x)
+        store(over_rows(bands, right_ref[...].reshape(-1, nb)))
+
+    @pl.when(place_ref[0] == 0)
+    def _():
+        store(over_rows(bands, bands))
 
 
 def half_gram(place, held, given=()):
@@ -129,17 +134,25 @@
     def rows(value):
         return value.reshape(-1, nb)
 
-    cross = over_rows(rows(own_ref[0:nx, 0]), rows(yown_ref[...]))
-    cross += over_rows(rows(other_ref[0:nx, 0]), rows(yother_ref[...]))
-    slab = jnp.where(place_ref[1] == 0, other_ref[0], own_ref[nx - 1])
-    cross += over_rows(rows(slab), rows(xhalo_ref[...]))
-    inside = over_rows(rows(own_ref[0]), rows(other_ref[nx - 1]))
-    gram = gram_ref[...] - 0.5 * (cross + jnp.where(place_ref[0] == 1, inside, 0.0))
-    total = (scale * (gram + jnp.transpose(gram))).astype(BF16)
-    total = total.reshape(nb // (groups * depth), groups, depth, nb)
-    for d in range(groups):
-        out_ref[d, 0 : nb // groups] = rows(total[:, d])
-        out_ref[d, nb // groups :] = coef_ref[...]
+    def send(total):
+        total = total.astype(BF16).reshape(nb // (groups * depth), groups, depth, nb)
+        for d in range(groups):
+            out_ref[d, 0 : nb // groups] = rows(total[:, d])
+            out_ref[d, nb // groups :] = coef_ref[...]
+
+    @pl.when(place_ref[0] == 1)
+    def _():
+        cross = over_rows(rows(own_ref[0:nx, 0]), rows(yown_ref[...]))
+        cross += over_rows(rows(other_ref[0:nx, 0]), rows(yother_ref[...]))
+        slab = jnp.where(place_ref[1] == 0, other_ref[0], own_ref[nx - 1])
+        cross += over_rows(rows(slab), rows(xhalo_ref[...]))
+        cross += over_rows(rows(own_ref[0]), rows(other_ref[nx - 1]))
+        gram = gram_ref[...] - 0.5 * cross
+        send(scale * (gram + jnp.transpose(gram)))
+
+    @pl.when(place_ref[0] == 0)
+    def _():
+        send(scale * gram_ref[...])
 
 
 def add_cross(scale, groups, place, gram, own, other, yown, yother, xhalo, coef):

time: 82.6 us -> 81.2 us (0.983)
  starting transfers between devices: 29.5 us -> 28.4 us
    all_to_all x1, starting transfers between devices: 13.7 us -> 12.6 us  [exchanged(): return lax.all_to_all(x, axis, 0, 0, tiled=True, axis_index_groups=groups)]
where the time goes in v8:
time: 81.2 us; the launch traced here: 80.8 us
  blocking collectives  31.4 us (39%)
  starting transfers between devices  28.4 us (35%)
  Pallas kernels  10.4 us (13%)
  waiting for transfers between devices  6.86 us (8%)
  matrix products  2.18 us (3%)
    all_to_all x2, blocking collectives, exchanged(): return lax.all_to_all(x, axis, 0, 0, tiled=True, axis_index_groups=groups)  31.4 us
    all_to_all x1, starting transfers between devices, exchanged(): return lax.all_to_all(x, axis, 0, 0, tiled=True, axis_index_groups=groups)  12.6 us
    pallas_call x6, Pallas kernels, call(): pl.pallas_call(kernel, out_shape=out_shape, in_specs=in_specs, out_specs=...  10.4 us
    ppermute x1, starting transfers between devices, projected(): other = lax.ppermute(own, 'gx', partner)  8.75 us
    all_to_all x1, waiting for transfers between devices, exchanged(): return lax.all_to_all(x, axis, 0, 0, tiled=True, axis_index_groups=groups)  6.18 us
    ppermute x1, starting transfers between devices, projected(): xhalo = lax.ppermute(slab, BOTH, x_pairs)  3.18 us
    dot_general x1, matrix products, projected(): jnp.dot(bands.reshape(cells, nb), jnp.concatenate((left, right), axis=1),...  2.18 us
    ppermute x1, starting transfers between devices, projected(): coef_other = lax.ppermute(coef, 'gx', partner)  1.91 us
  transfers between devices with their start and end apart: 6, of which 2 were waited for; matrix products, arithmetic and copies ran while one was open for 1% of the time, Pallas kernels for 6%

profile of v8, /device:TPU:1, one launch (start us, length us, event | category | flops | bytes accessed | tf_op | source)
XLA Modules:
  0.0 80.8 jit_solution(16915868600726399270)
XLA Ops:
  0.6 0.1 pad_add_fusion.place_ref
  0.7 2.2 %shard_map.58 = (bf16[9,5,40,512]{3,2,1,0:T(8,128)(2,1)S(1)}, bf16[8,40,512]{2,1,0:T(8,128)(2,1)S(1)}, bf16[5,40,512]{2,1,0:T(8,128)(2,1)S(1)}) custom-call(s32[2]{0:T(128)S(1)} %pad_add_fusion.place_ref, bf16[8,5,40,512]{3,2,1,0:T(8,128)(2,1)} %bands_ref.1, f32[5,8,40]{2,1,0:T(8,128)} %bitcast.15), custom_call_target="tpu_custom_call" | custom-call | bytes 1644808 | tf_op jit(solution)/shard_map/pallas_call | solution.py:29
  3.0 8.7 %collective-permute-start = (bf16[9,5,40,512]{3,2,1,0:T(8,128)(2,1)S(1)}, bf16[9,5,40,512]{3,2,1,0:T(8,128)(2,1)S(1)}, u32[]{:S(2)}, u32[]{:S(2)}) collective-permute-start(bf16[9,5,40,512]{3,2,1,0:T(8,128)(2,1)S(1)} %get-tuple-element.8.held_ref.own_ref), channel_id=1, source_target_pairs={{0,64},{64,0},{128,192},{192,128},{256,320},{320,256},{384,448},{4... | collective-permute-start | bytes 5529608 | tf_op jit(solution)/shard_map/ppermute | solution.py:273
  11.7 1.3 %collective-permute-start.1 = (bf16[8,40,512]{2,1,0:T(8,128)(2,1)S(1)}, bf16[8,40,512]{2,1,0:T(8,128)(2,1)S(1)}, u32[]{:S(2)}, u32[]{:S(2)}) collective-permute-start(bf16[8,40,512]{2,1,0:T(8,128)(2,1)S(1)} %get-tuple-element.9), channel_id=1, source_target_pairs={{64,65},{65,66},{66,67},{67,68},{68,69},{69,70},{70,71},{71,72},{7... | collective-permute-start | bytes 983048 | tf_op jit(solution)/shard_map/ppermute | solution.py:272
  13.0 0.7 collective-permute-start.2
  13.7 3.2 %collective-permute-start.3 = (bf16[5,40,512]{2,1,0:T(8,128)(2,1)S(1)}, bf16[5,40,512]{2,1,0:T(8,128)(2,1)S(1)}, u32[]{:S(2)}, u32[]{:S(2)}) collective-permute-start(bf16[5,40,512]{2,1,0:T(8,128)(2,1)S(1)} %get-tuple-element.10), channel_id=1, source_target_pairs={{64,192},{129,65},{66,194},{131,67},{68,196},{133,69},{70,198},{13... | collective-permute-start | bytes 614408 | tf_op jit(solution)/shard_map/ppermute | solution.py:274
  16.9 2.5 %shard_map.59.refs_0_ = f32[512,512]{1,0:T(8,128)S(1)} custom-call(s32[2]{0:T(128)S(1)} %pad_add_fusion.place_ref, bf16[9,5,40,512]{3,2,1,0:T(8,128)(2,1)S(1)} %get-tuple-element.8.held_ref.own_ref), custom_call_target="tpu_custom_call" | custom-call | flops 838860800 | bytes 1843208 | tf_op jit(solution)/shard_map/pallas_call | solution.py:29
  19.4 0.0 copy-start
  19.4 0.0 collective-permute-done.held_ref.other_ref
  19.5 2.6 %shard_map.60.gram_ref = f32[512,512]{1,0:T(8,128)S(1)} custom-call(s32[2]{0:T(128)S(1)} %pad_add_fusion.place_ref, bf16[9,5,40,512]{3,2,1,0:T(8,128)(2,1)S(1)} %collective-permute-done.held_ref.other_ref, f32[512,512]{1,0:T(8,128)S(1)} %shard_map.59.refs_0_), custom_call_target="tpu_custom_call" | custom-call | flops 838860800 | bytes 2891784 | tf_op jit(solution)/shard_map/pallas_call | solution.py:29
  22.0 0.7 collective-permute-done.3.xhalo_ref
  22.7 0.0 collective-permute-done.1.yown_ref
  22.7 0.0 collective-permute-done.2.yother_ref
  22.7 1.8 %shard_map.61 = bf16[8,72,512]{2,1,0:T(8,128)(2,1)S(1)} custom-call(s32[2]{0:T(128)S(1)} %pad_add_fusion.place_ref, f32[512,512]{1,0:T(8,128)S(1)} %shard_map.60.gram_ref, bf16[9,5,40,512]{3,2,1,0:T(8,128)(2,1)S(1)} %get-tuple-element.8.held_ref.own_ref, bf16[9,5,40,512]{3,2,1,0:T(8,128)(2,1)S(1)} %collective-permute-done.held_ref.other_ref, ...), custom_call_target="tpu_custom_call" | custom-call | flops 440401920 | bytes 5603336 | tf_op jit(solution)/shard_map/pallas_call | solution.py:29
  24.5 14.3 %all_to_all.15.in_ref = bf16[8,72,512]{2,1,0:T(8,128)(2,1)S(1)} all-to-all(bf16[8,72,512]{2,1,0:T(8,128)(2,1)S(1)} %shard_map.61), channel_id=1, replica_groups={{0,1,2,3,4,5,6,7},{8,9,10,11,12,13,14,15},{16,17,18,19,20,21,22,23},{24..., dimensions={0} | all-to-all | bytes 1179648 | tf_op jit(solution)/shard_map/all_to_all | solution.py:252
  38.8 0.6 shard_map.62
  39.5 17.1 %all_to_all.16.in_ref = bf16[8,40,512]{2,1,0:T(8,128)(2,1)S(1)} all-to-all(bf16[8,40,512]{2,1,0:T(8,128)(2,1)S(1)} %shard_map.62), channel_id=1, replica_groups={{0,8,16,24,32,40,48,56},{1,9,17,25,33,41,49,57},{2,10,18,26,34,42,50,58..., dimensions={0} | all-to-all | bytes 655360 | tf_op jit(solution)/shard_map/all_to_all | solution.py:252
  56.6 0.7 shard_map.63
  57.3 12.6 %all-to-all-start.2 = ((f32[8,8,512]{2,1,0:T(8,128)}), f32[8,8,512]{2,1,0:T(8,128)S(1)}, u32[]{:S(2)}, u32[]{:S(2)}) async-start(f32[8,8,512]{2,1,0:T(8,128)} %get-tuple-element.11), calls=%async_computation.2 | async-start | bytes 262144 | tf_op jit(solution)/shard_map/all_to_all | solution.py:252
  69.8 1.9 %collective-permute-start.4 = (bf16[512,256]{1,0:T(8,128)(2,1)S(1)}, bf16[512,256]{1,0:T(8,128)(2,1)S(1)}, u32[]{:S(2)}, u32[]{:S(2)}) collective-permute-start(bf16[512,256]{1,0:T(8,128)(2,1)S(1)} %get-tuple-element.12), channel_id=1, source_target_pairs={{0,64},{64,0},{128,192},{192,128},{256,320},{320,256},{384,448},{4... | collective-permute-start | bytes 786440 | tf_op jit(solution)/shard_map/ppermute | solution.py:284
  71.8 6.2 %all-to-all-done.2 = f32[8,8,512]{2,1,0:T(8,128)S(1)} async-done(((f32[8,8,512]{2,1,0:T(8,128)}), f32[8,8,512]{2,1,0:T(8,128)S(1)}, u32[]{:S(2)}, u32[]{:S(2)}) %all-to-all-start.2) | async-done | bytes 131104 | tf_op jit(solution)/shard_map/all_to_all | solution.py:252
  77.9 0.6 slice_bitcast_fusion
  78.6 0.0 collective-permute-done.4
  78.6 2.2 %convolution_convert_fusion = bf16[512,1600]{0,1:T(8,128)(2,1)} fusion(bf16[1600,512]{1,0:T(8,128)(2,1)S(1)} %bitcast.13, bf16[512,256]{1,0:T(8,128)(2,1)S(1)} %get-tuple-element.14, bf16[512,256]{1,0:T(8,128)(2,1)S(1)} %get-tuple-element.13), kind=kOutput, calls=%fused_computation | convolution fusion | flops 840728576 | bytes 3801088 | tf_op jit(solution)/shard_map/dot_general | solution.py:290
  (5 shorter events, 0.1 us)
Async XLA Ops:
  3.0 16.5 %collective-permute-start = (bf16[9,5,40,512]{3,2,1,0:T(8,128)(2,1)S(1)}, bf16[9,5,40,512]{3,2,1,0:T(8,128)(2,1)S(1)}, u32[]{:S(2)}, u32[]{:S(2)}) collective-permute-start(bf16[9,5,40,512]{3,2,1,0:T(8,128)(2,1)S(1)} %get-tuple-element.8.held_ref.own_ref), channel_id=1, source_target_pairs={{0,64},{64,0},{128,192},{192,128},{256,320},{320,256},{384,448},{4... | collective-permute-start | bytes 5529608 | tf_op jit(solution)/shard_map/ppermute | solution.py:273
  11.7 11.0 %collective-permute-start.1 = (bf16[8,40,512]{2,1,0:T(8,128)(2,1)S(1)}, bf16[8,40,512]{2,1,0:T(8,128)(2,1)S(1)}, u32[]{:S(2)}, u32[]{:S(2)}) collective-permute-start(bf16[8,40,512]{2,1,0:T(8,128)(2,1)S(1)} %get-tuple-element.9), channel_id=1, source_target_pairs={{64,65},{65,66},{66,67},{67,68},{68,69},{69,70},{70,71},{71,72},{7... | collective-permute-start | bytes 983048 | tf_op jit(solution)/shard_map/ppermute | solution.py:272
  13.0 9.7 %collective-permute-start.2 = (bf16[8,40,512]{2,1,0:T(8,128)(2,1)S(1)}, bf16[8,40,512]{2,1,0:T(8,128)(2,1)S(1)}, u32[]{:S(2)}, u32[]{:S(2)}) collective-permute-start(bf16[8,40,512]{2,1,0:T(8,128)(2,1)S(1)} %get-tuple-element.9), channel_id=1, source_target_pairs={{0,65},{1,66},{2,67},{3,68},{4,69},{5,70},{6,71},{7,72},{8,73},{9,... | collective-permute-start | bytes 983048 | tf_op jit(solution)/shard_map/ppermute | solution.py:271
  13.7 9.0 %collective-permute-start.3 = (bf16[5,40,512]{2,1,0:T(8,128)(2,1)S(1)}, bf16[5,40,512]{2,1,0:T(8,128)(2,1)S(1)}, u32[]{:S(2)}, u32[]{:S(2)}) collective-permute-start(bf16[5,40,512]{2,1,0:T(8,128)(2,1)S(1)} %get-tuple-element.10), channel_id=1, source_target_pairs={{64,192},{129,65},{66,194},{131,67},{68,196},{133,69},{70,198},{13... | collective-permute-start | bytes 614408 | tf_op jit(solution)/shard_map/ppermute | solution.py:274
  19.4 3.3 %copy-start = (bf16[8,512]{1,0:T(8,128)(2,1)S(1)}, bf16[8,512]{1,0:T(8,128)(2,1)}, u32[]{:S(2)}) copy-start(bf16[8,512]{1,0:T(8,128)(2,1)} %coef_ref.1) | copy-start | bytes 24580
  38.8 39.8 %copy-start.1 = (bf16[8,5,40,512]{3,2,1,0:T(8,128)(2,1)S(1)}, bf16[8,5,40,512]{3,2,1,0:T(8,128)(2,1)}, u32[]{:S(2)}) copy-start(bf16[8,5,40,512]{3,2,1,0:T(8,128)(2,1)} %bands_ref.1) | copy-start | bytes 4915204
  57.3 20.7 %all-to-all-start.2 = ((f32[8,8,512]{2,1,0:T(8,128)}), f32[8,8,512]{2,1,0:T(8,128)S(1)}, u32[]{:S(2)}, u32[]{:S(2)}) async-start(f32[8,8,512]{2,1,0:T(8,128)} %get-tuple-element.11), calls=%async_computation.2 | async-start | bytes 262144 | tf_op jit(solution)/shard_map/all_to_all | solution.py:252
  69.8 8.7 %collective-permute-start.4 = (bf16[512,256]{1,0:T(8,128)(2,1)S(1)}, bf16[512,256]{1,0:T(8,128)(2,1)S(1)}, u32[]{:S(2)}, u32[]{:S(2)}) collective-permute-start(bf16[512,256]{1,0:T(8,128)(2,1)S(1)} %get-tuple-element.12), channel_id=1, source_target_pairs={{0,64},{64,0},{128,192},{192,128},{256,320},{320,256},{384,448},{4... | collective-permute-start | bytes 786440 | tf_op jit(solution)/shard_map/ppermute | solution.py:284

commit v9 on v8

--- a/solution.py
+++ b/solution.py
@@ -129,16 +129,18 @@
 ):
     _, _, nb = xhalo_ref.shape
     nx = yown_ref.shape[0]
-    groups, depth = out_ref.shape[0], coef_ref.shape[0]
+    count, depth, _ = out_ref.shape
 
     def rows(value):
         return value.reshape(-1, nb)
 
     def send(total):
-        total = total.astype(BF16).reshape(nb // (groups * depth), groups, depth, nb)
-        for d in range(groups):
-            out_ref[d, 0 : nb // groups] = rows(total[:, d])
-            out_ref[d, nb // groups :] = coef_ref[...]
+        out_ref[:, :, 0:nb] = total.astype(BF16).reshape(count, depth, nb)
+
+    coef = coef_ref[...]
+    half = jnp.where(place_ref[0] == 0, coef[:, : nb // 2], coef[:, nb // 2 :])
+    for target in range(count):
+        out_ref[target, :, nb:] = half
 
     @pl.when(place_ref[0] == 1)
     def _():
@@ -155,75 +157,38 @@
         send(scale * gram_ref[...])
 
 
-def add_cross(scale, groups, place, gram, own, other, yown, yother, xhalo, coef):
+def add_cross(scale, place, gram, own, other, yown, yother, xhalo, coef):
     nb = gram.shape[0]
     depth = coef.shape[0]
     halo_rows = (yown.size + yother.size + xhalo.size) // nb
     return call(
         functools.partial(cross_kernel, scale),
-        jax.ShapeDtypeStruct((groups, nb // groups + depth, nb), BF16),
+        jax.ShapeDtypeStruct((nb // depth, depth, nb + nb // 2), BF16),
         [SMEM] + [VMEM] * 7,
         (place, gram, own, other, yown, yother, xhalo, coef),
         flops=2 * halo_rows * nb * nb,
     )
 
 
-def middle_kernel(place_ref, in_ref, out_ref):
-    sources, height, nb = in_ref.shape
-    targets, _, _ = out_ref.shape
-    depth = (height * targets - nb * targets // sources) // targets
-    width = nb // 2
-    total = in_ref[0, 0 : height - depth].astype(F32)
+def finish_kernel(in_ref, rows_ref, coef_ref):
+    sources, _, _ = in_ref.shape
+    nb = rows_ref.shape[-1]
+    total = in_ref[0, :, 0:nb].astype(F32)
     for s in range(1, sources):
-        total += in_ref[s, 0 : height - depth].astype(F32)
-    total = total.astype(BF16).reshape(targets, depth, nb)
-    upper = sources // 2
-    for s in range(sources):
-        coef = in_ref[s, height - depth :]
-        coef = jnp.where(place_ref[0] == 0, coef[:, :width], coef[:, width:])
-        first = depth + (s % upper) * depth
-        lane = (s // upper) * width
-        for t in range(targets):
-            out_ref[t, first : first + depth, lane : lane + width] = coef
-    for t in range(targets):
-        out_ref[t, 0:depth] = total[t]
-
-
-def middle(place, arrived, targets):
-    sources, height, nb = arrived.shape
-    depth = height - nb // sources
-    return call(
-        middle_kernel,
-        jax.ShapeDtypeStruct((targets, depth + sources * depth // 2, nb), BF16),
-        [SMEM, VMEM],
-        (place, arrived),
-    )
-
-
-def last_kernel(in_ref, rows_ref, coef_ref):
-    sources, height, nb = in_ref.shape
-    copies, depth, _ = rows_ref.shape
-    total = in_ref[0, 0:depth].astype(F32)
-    for s in range(1, sources):
-        total += in_ref[s, 0:depth].astype(F32)
-    for c in range(copies):
+        total += in_ref[s, :, 0:nb].astype(F32)
+    for c in range(rows_ref.shape[0]):
         rows_ref[c] = total
-    plane = 2 * (height - depth)
-    for s in range(sources):
-        for part in range(2):
-            start = s * plane + part * (plane // 2)
-            coef_ref[start : start + plane // 2] = in_ref[
-                s, depth:, part * (nb // 2) : (part + 1) * (nb // 2)
-            ]
-
-
-def finish(arrived, copies, depth):
-    _, _, nb = arrived.shape
-    return call(
-        last_kernel,
+    coef_ref[...] = in_ref[:, :, nb:].reshape(coef_ref.shape)
+
+
+def finish(arrived, copies):
+    sources, depth, width = arrived.shape
+    nb = sources * depth
+    return call(
+        finish_kernel,
         (
             jax.ShapeDtypeStruct((copies, depth, nb), F32),
-            jax.ShapeDtypeStruct((nb, nb // 2), BF16),
+            jax.ShapeDtypeStruct((nb, width - nb), BF16),
         ),
         [VMEM],
         (arrived,),
@@ -248,16 +213,13 @@
     return same, next_core, x
 
 
-def exchanged(x, axis, groups=None):
-    return lax.all_to_all(x, axis, 0, 0, tiled=True, axis_index_groups=groups)
+def exchanged(x, axis):
+    return lax.all_to_all(x, axis, 0, 0, tiled=True)
 
 
 def projected(bands, potential, eigenvectors):
     nx, ny, nz, nb = bands.shape
     gx, gyz = lax.axis_size("gx"), lax.axis_size("gyz")
-    depth = eigenvectors.shape[0]
-    inner = 8
-    outer = gyz // inner
     core = lax.rem(lax.axis_index("gx"), 2)
     odd = lax.rem(lax.axis_index("gyz"), 2)
     cells = nx * ny * nz
@@ -274,13 +236,9 @@
     xhalo = lax.ppermute(slab, BOTH, x_pairs)
     gram = half_gram(place, own)
     gram = half_gram(place, other, (gram,))
-    sent = add_cross(
-        scale, inner, place, gram, own, other, yown, yother, xhalo, eigenvectors
-    )
-    arrived = exchanged(sent, "gyz", [[o * inner + i for i in range(inner)] for o in range(outer)])
-    sent = middle(place, arrived, outer)
-    arrived = exchanged(sent, "gyz", [[o * inner + i for o in range(outer)] for i in range(inner)])
-    rows, coef = finish(arrived, gx, depth)
+    sent = add_cross(scale, place, gram, own, other, yown, yother, xhalo, eigenvectors)
+    arrived = exchanged(sent, "gyz")
+    rows, coef = finish(arrived, gx)
     coef_other = lax.ppermute(coef, "gx", partner)
     parts = exchanged(rows, "gx")
     sums = parts.reshape(gx // 2, 2, *parts.shape[1:]).sum(axis=0)

time: 81.2 us -> 79 us (0.973)
  blocking collectives: 31.4 us -> 29.9 us
    all_to_all x2 -> x1, blocking collectives: 31.4 us -> 29.9 us  [exchanged(): return lax.all_to_all(x, axis, 0, 0, tiled=True)]
    pallas_call x6 -> x5, Pallas kernels: 10.4 us -> 9.9 us  [call(): pl.pallas_call(kernel, out_shape=out_shape, in_specs=in_specs, out_specs=...]
where the time goes in v9:
time: 79 us; the launch traced here: 78.7 us
  blocking collectives  29.9 us (38%)
  starting transfers between devices  28.5 us (36%)
  Pallas kernels  9.9 us (13%)
  waiting for transfers between devices  6.76 us (9%)
  matrix products  2.18 us (3%)
    all_to_all x1, blocking collectives, exchanged(): return lax.all_to_all(x, axis, 0, 0, tiled=True)  29.9 us
    all_to_all x1, starting transfers between devices, exchanged(): return lax.all_to_all(x, axis, 0, 0, tiled=True)  12.6 us
    pallas_call x5, Pallas kernels, call(): pl.pallas_call(kernel, out_shape=out_shape, in_specs=in_specs, out_specs=...  9.9 us
    ppermute x1, starting transfers between devices, projected(): other = lax.ppermute(own, 'gx', partner)  8.75 us
    all_to_all x1, waiting for transfers between devices, exchanged(): return lax.all_to_all(x, axis, 0, 0, tiled=True)  6.07 us
    ppermute x1, starting transfers between devices, projected(): xhalo = lax.ppermute(slab, BOTH, x_pairs)  3.18 us
    dot_general x1, matrix products, projected(): jnp.dot(bands.reshape(cells, nb), jnp.concatenate((left, right), axis=1),...  2.18 us
    ppermute x1, starting transfers between devices, projected(): coef_other = lax.ppermute(coef, 'gx', partner)  1.91 us
  transfers between devices with their start and end apart: 6, of which 2 were waited for; matrix products, arithmetic and copies ran while one was open for 1% of the time, Pallas kernels for 6%

profile of v9, /device:TPU:1, one launch (start us, length us, event | category | flops | bytes accessed | tf_op | source)
XLA Modules:
  0.0 78.7 jit_solution(11437543072797112112)
XLA Ops:
  0.6 0.1 pad_add_fusion.place_ref
  0.7 2.2 %shard_map.58 = (bf16[9,5,40,512]{3,2,1,0:T(8,128)(2,1)S(1)}, bf16[8,40,512]{2,1,0:T(8,128)(2,1)S(1)}, bf16[5,40,512]{2,1,0:T(8,128)(2,1)S(1)}) custom-call(s32[2]{0:T(128)S(1)} %pad_add_fusion.place_ref, bf16[8,5,40,512]{3,2,1,0:T(8,128)(2,1)} %bands_ref.1, f32[5,8,40]{2,1,0:T(8,128)} %bitcast.15), custom_call_target="tpu_custom_call" | custom-call | bytes 1644808 | tf_op jit(solution)/shard_map/pallas_call | solution.py:29
  3.0 8.7 %collective-permute-start = (bf16[9,5,40,512]{3,2,1,0:T(8,128)(2,1)S(1)}, bf16[9,5,40,512]{3,2,1,0:T(8,128)(2,1)S(1)}, u32[]{:S(2)}, u32[]{:S(2)}) collective-permute-start(bf16[9,5,40,512]{3,2,1,0:T(8,128)(2,1)S(1)} %get-tuple-element.8.held_ref.own_ref), channel_id=1, source_target_pairs={{0,64},{64,0},{128,192},{192,128},{256,320},{320,256},{384,448},{4... | collective-permute-start | bytes 5529608 | tf_op jit(solution)/shard_map/ppermute | solution.py:235
  11.7 1.3 %collective-permute-start.1 = (bf16[8,40,512]{2,1,0:T(8,128)(2,1)S(1)}, bf16[8,40,512]{2,1,0:T(8,128)(2,1)S(1)}, u32[]{:S(2)}, u32[]{:S(2)}) collective-permute-start(bf16[8,40,512]{2,1,0:T(8,128)(2,1)S(1)} %get-tuple-element.9), channel_id=1, source_target_pairs={{64,65},{65,66},{66,67},{67,68},{68,69},{69,70},{70,71},{71,72},{7... | collective-permute-start | bytes 983048 | tf_op jit(solution)/shard_map/ppermute | solution.py:234
  13.0 0.7 collective-permute-start.2
  13.7 3.2 %collective-permute-start.3 = (bf16[5,40,512]{2,1,0:T(8,128)(2,1)S(1)}, bf16[5,40,512]{2,1,0:T(8,128)(2,1)S(1)}, u32[]{:S(2)}, u32[]{:S(2)}) collective-permute-start(bf16[5,40,512]{2,1,0:T(8,128)(2,1)S(1)} %get-tuple-element.10), channel_id=1, source_target_pairs={{64,192},{129,65},{66,194},{131,67},{68,196},{133,69},{70,198},{13... | collective-permute-start | bytes 614408 | tf_op jit(solution)/shard_map/ppermute | solution.py:236
  16.9 2.5 %shard_map.59.refs_0_ = f32[512,512]{1,0:T(8,128)S(1)} custom-call(s32[2]{0:T(128)S(1)} %pad_add_fusion.place_ref, bf16[9,5,40,512]{3,2,1,0:T(8,128)(2,1)S(1)} %get-tuple-element.8.held_ref.own_ref), custom_call_target="tpu_custom_call" | custom-call | flops 838860800 | bytes 1843208 | tf_op jit(solution)/shard_map/pallas_call | solution.py:29
  19.4 0.0 copy-start
  19.4 0.0 collective-permute-done.held_ref.other_ref
  19.5 2.6 %shard_map.60.gram_ref = f32[512,512]{1,0:T(8,128)S(1)} custom-call(s32[2]{0:T(128)S(1)} %pad_add_fusion.place_ref, bf16[9,5,40,512]{3,2,1,0:T(8,128)(2,1)S(1)} %collective-permute-done.held_ref.other_ref, f32[512,512]{1,0:T(8,128)S(1)} %shard_map.59.refs_0_), custom_call_target="tpu_custom_call" | custom-call | flops 838860800 | bytes 2891784 | tf_op jit(solution)/shard_map/pallas_call | solution.py:29
  22.0 0.7 collective-permute-done.3.xhalo_ref
  22.7 0.0 collective-permute-done.1.yown_ref
  22.7 0.0 collective-permute-done.2.yother_ref
  22.7 0.0 copy-done
  22.7 1.8 %shard_map.61 = bf16[64,8,768]{2,1,0:T(8,128)(2,1)S(1)} custom-call(s32[2]{0:T(128)S(1)} %pad_add_fusion.place_ref, f32[512,512]{1,0:T(8,128)S(1)} %shard_map.60.gram_ref, bf16[9,5,40,512]{3,2,1,0:T(8,128)(2,1)S(1)} %get-tuple-element.8.held_ref.own_ref, bf16[9,5,40,512]{3,2,1,0:T(8,128)(2,1)S(1)} %collective-permute-done.held_ref.other_ref, ...), custom_call_target="tpu_custom_call" | custom-call | flops 440401920 | bytes 5603336 | tf_op jit(solution)/shard_map/pallas_call | solution.py:29
  24.5 0.0 copy-start.1
  24.5 29.9 %all_to_all.10.in_ref = bf16[64,8,768]{2,1,0:T(8,128)(2,1)S(1)} all-to-all(bf16[64,8,768]{2,1,0:T(8,128)(2,1)S(1)} %shard_map.61), channel_id=1, replica_groups=mesh['gx'=8,'gyz'=64] {'gyz'}, dimensions={0} | all-to-all | bytes 1572864 | tf_op jit(solution)/shard_map/all_to_all | solution.py:217
  54.4 0.8 shard_map.62
  55.2 12.6 %all-to-all-start.1 = ((f32[8,8,512]{2,1,0:T(8,128)}), f32[8,8,512]{2,1,0:T(8,128)S(1)}, u32[]{:S(2)}, u32[]{:S(2)}) async-start(f32[8,8,512]{2,1,0:T(8,128)} %get-tuple-element.11), calls=%async_computation.1 | async-start | bytes 262144 | tf_op jit(solution)/shard_map/all_to_all | solution.py:217
  67.8 1.9 %collective-permute-start.4 = (bf16[512,256]{1,0:T(8,128)(2,1)S(1)}, bf16[512,256]{1,0:T(8,128)(2,1)S(1)}, u32[]{:S(2)}, u32[]{:S(2)}) collective-permute-start(bf16[512,256]{1,0:T(8,128)(2,1)S(1)} %get-tuple-element.12), channel_id=1, source_target_pairs={{0,64},{64,0},{128,192},{192,128},{256,320},{320,256},{384,448},{4... | collective-permute-start | bytes 786440 | tf_op jit(solution)/shard_map/ppermute | solution.py:242
  69.7 6.1 %all-to-all-done.1 = f32[8,8,512]{2,1,0:T(8,128)S(1)} async-done(((f32[8,8,512]{2,1,0:T(8,128)}), f32[8,8,512]{2,1,0:T(8,128)S(1)}, u32[]{:S(2)}, u32[]{:S(2)}) %all-to-all-start.1) | async-done | bytes 131104 | tf_op jit(solution)/shard_map/all_to_all | solution.py:217
  75.8 0.6 slice_bitcast_fusion
  76.4 0.0 collective-permute-done.4
  76.5 2.2 %convolution_convert_fusion = bf16[512,1600]{0,1:T(8,128)(2,1)} fusion(bf16[1600,512]{1,0:T(8,128)(2,1)S(1)} %bitcast.13, bf16[512,256]{1,0:T(8,128)(2,1)S(1)} %get-tuple-element.14, bf16[512,256]{1,0:T(8,128)(2,1)S(1)} %get-tuple-element.13), kind=kOutput, calls=%fused_computation | convolution fusion | flops 840728576 | bytes 3801088 | tf_op jit(solution)/shard_map/dot_general | solution.py:248
  (3 shorter events, 0.1 us)
Async XLA Ops:
  3.0 16.5 %collective-permute-start = (bf16[9,5,40,512]{3,2,1,0:T(8,128)(2,1)S(1)}, bf16[9,5,40,512]{3,2,1,0:T(8,128)(2,1)S(1)}, u32[]{:S(2)}, u32[]{:S(2)}) collective-permute-start(bf16[9,5,40,512]{3,2,1,0:T(8,128)(2,1)S(1)} %get-tuple-element.8.held_ref.own_ref), channel_id=1, source_target_pairs={{0,64},{64,0},{128,192},{192,128},{256,320},{320,256},{384,448},{4... | collective-permute-start | bytes 5529608 | tf_op jit(solution)/shard_map/ppermute | solution.py:235
  11.7 11.0 %collective-permute-start.1 = (bf16[8,40,512]{2,1,0:T(8,128)(2,1)S(1)}, bf16[8,40,512]{2,1,0:T(8,128)(2,1)S(1)}, u32[]{:S(2)}, u32[]{:S(2)}) collective-permute-start(bf16[8,40,512]{2,1,0:T(8,128)(2,1)S(1)} %get-tuple-element.9), channel_id=1, source_target_pairs={{64,65},{65,66},{66,67},{67,68},{68,69},{69,70},{70,71},{71,72},{7... | collective-permute-start | bytes 983048 | tf_op jit(solution)/shard_map/ppermute | solution.py:234
  13.0 9.7 %collective-permute-start.2 = (bf16[8,40,512]{2,1,0:T(8,128)(2,1)S(1)}, bf16[8,40,512]{2,1,0:T(8,128)(2,1)S(1)}, u32[]{:S(2)}, u32[]{:S(2)}) collective-permute-start(bf16[8,40,512]{2,1,0:T(8,128)(2,1)S(1)} %get-tuple-element.9), channel_id=1, source_target_pairs={{0,65},{1,66},{2,67},{3,68},{4,69},{5,70},{6,71},{7,72},{8,73},{9,... | collective-permute-start | bytes 983048 | tf_op jit(solution)/shard_map/ppermute | solution.py:233
  13.7 9.0 %collective-permute-start.3 = (bf16[5,40,512]{2,1,0:T(8,128)(2,1)S(1)}, bf16[5,40,512]{2,1,0:T(8,128)(2,1)S(1)}, u32[]{:S(2)}, u32[]{:S(2)}) collective-permute-start(bf16[5,40,512]{2,1,0:T(8,128)(2,1)S(1)} %get-tuple-element.10), channel_id=1, source_target_pairs={{64,192},{129,65},{66,194},{131,67},{68,196},{133,69},{70,198},{13... | collective-permute-start | bytes 614408 | tf_op jit(solution)/shard_map/ppermute | solution.py:236
  19.4 3.3 %copy-start = (bf16[8,512]{1,0:T(8,128)(2,1)S(1)}, bf16[8,512]{1,0:T(8,128)(2,1)}, u32[]{:S(2)}) copy-start(bf16[8,512]{1,0:T(8,128)(2,1)} %coef_ref.1) | copy-start | bytes 24580
  24.5 52.0 %copy-start.1 = (bf16[8,5,40,512]{3,2,1,0:T(8,128)(2,1)S(1)}, bf16[8,5,40,512]{3,2,1,0:T(8,128)(2,1)}, u32[]{:S(2)}) copy-start(bf16[8,5,40,512]{3,2,1,0:T(8,128)(2,1)} %bands_ref.1) | copy-start | bytes 4915204
  55.2 20.6 %all-to-all-start.1 = ((f32[8,8,512]{2,1,0:T(8,128)}), f32[8,8,512]{2,1,0:T(8,128)S(1)}, u32[]{:S(2)}, u32[]{:S(2)}) async-start(f32[8,8,512]{2,1,0:T(8,128)} %get-tuple-element.11), calls=%async_computation.1 | async-start | bytes 262144 | tf_op jit(solution)/shard_map/all_to_all | solution.py:217
  67.8 8.6 %collective-permute-start.4 = (bf16[512,256]{1,0:T(8,128)(2,1)S(1)}, bf16[512,256]{1,0:T(8,128)(2,1)S(1)}, u32[]{:S(2)}, u32[]{:S(2)}) collective-permute-start(bf16[512,256]{1,0:T(8,128)(2,1)S(1)} %get-tuple-element.12), channel_id=1, source_target_pairs={{0,64},{64,0},{128,192},{192,128},{256,320},{320,256},{384,448},{4... | collective-permute-start | bytes 786440 | tf_op jit(solution)/shard_map/ppermute | solution.py:242

commit v10 on v9

--- a/solution.py
+++ b/solution.py
@@ -37,14 +37,12 @@
     )(*args)
 
 
-def prepare_kernel(place_ref, bands_ref, pot_ref, held_ref, last_ref, slab_ref, pot_vmem, sems):
+def prepare_kernel(bands_ref, pot_ref, held_ref, last_ref, pot_vmem, sems):
     nx, ny, nz, _ = bands_ref.shape
-    sent = jnp.where(place_ref[1] == 0, nx - 1, 0)
     copies = (
         pltpu.make_async_copy(pot_ref, pot_vmem, sems.at[0]),
         pltpu.make_async_copy(bands_ref.at[:, ny - 1], last_ref, sems.at[1]),
-        pltpu.make_async_copy(bands_ref.at[sent], slab_ref, sems.at[2]),
-        pltpu.make_async_copy(bands_ref, held_ref.at[pl.ds(0, nx)], sems.at[3]),
+        pltpu.make_async_copy(bands_ref, held_ref.at[pl.ds(0, nx)], sems.at[2]),
     )
     for copy in copies:
         copy.start()
@@ -58,17 +56,17 @@
         copy.wait()
 
 
-def prepare(place, bands, pot):
+def prepare(bands, pot):
     nx, ny, nz, nb = bands.shape
     assert ny >= PIECES and nx * ny <= nz <= nb
-    shapes = ((nx + 1, ny, nz, nb), (nx, nz, nb), (ny, nz, nb))
+    shapes = ((nx + 1, ny, nz, nb), (nx, nz, nb))
     bands, pot = (pltpu.with_memory_space_constraint(x, pltpu.HBM) for x in (bands, pot))
     return call(
         prepare_kernel,
         tuple(jax.ShapeDtypeStruct(s, BF16) for s in shapes),
-        [SMEM, HBM, HBM],
-        (place, bands, pot),
-        scratch=[pltpu.VMEM(pot.shape, F32), pltpu.SemaphoreType.DMA((4,))],
+        [HBM, HBM],
+        (bands, pot),
+        scratch=[pltpu.VMEM(pot.shape, F32), pltpu.SemaphoreType.DMA((3,))],
     )
 
 
@@ -209,7 +207,7 @@
             if r % 2 == 0:
                 x.append((at(2 * chip + 1, r), at(2 * chip + 3, r)))
             else:
-                x.append((at(2 * chip + 2, r), at(2 * chip + 1, r)))
+                x.append((at(2 * chip + 3, r), at(2 * chip + 1, r)))
     return same, next_core, x
 
 
@@ -227,14 +225,15 @@
     place = jnp.stack((core, odd)).astype(jnp.int32)
     pot = jnp.transpose(potential, (1, 0, 2))
 
-    own, last, slab = prepare(place, bands, pot)
+    own, last = prepare(bands, pot)
     same, next_core, x_pairs = pairs_of(gx, gyz)
     partner = [(g, g ^ 1) for g in range(gx)]
+    other = lax.ppermute(own, "gx", partner)
     yother = lax.ppermute(last, BOTH, next_core)
     yown = lax.ppermute(last, BOTH, same)
-    other = lax.ppermute(own, "gx", partner)
+    gram = half_gram(place, own)
+    slab = jnp.where(odd == 0, own[nx - 1], other[0])
     xhalo = lax.ppermute(slab, BOTH, x_pairs)
-    gram = half_gram(place, own)
     gram = half_gram(place, other, (gram,))
     sent = add_cross(scale, place, gram, own, other, yown, yother, xhalo, eigenvectors)
     arrived = exchanged(sent, "gyz")

time: 79 us -> 79.7 us (level)
  starting transfers between devices: 28.5 us -> 24.1 us
  Pallas kernels: 9.9 us -> 12.3 us
  other arithmetic: 0.13 us -> 1.08 us
  waiting for transfers between devices: 6.76 us -> 7.68 us
    all_to_all x1, starting transfers between devices: 12.6 us -> 9.89 us  [exchanged(): return lax.all_to_all(x, axis, 0, 0, tiled=True)]
    pallas_call x5, Pallas kernels: 9.9 us -> 12.3 us  [call(): pl.pallas_call(kernel, out_shape=out_shape, in_specs=in_specs, out_specs=...]
    ppermute x1, waiting for transfers between devices: 0.01 us -> 1.6 us  [projected(): other = lax.ppermute(own, 'gx', partner)]
    ppermute x1, starting transfers between devices: 3.18 us -> 1.6 us  [projected(): xhalo = lax.ppermute(slab, BOTH, x_pairs)]
    select_n x0 -> x1, other arithmetic: none -> 0.95 us  [projected(): slab = jnp.where(odd == 0, own[nx - 1], other[0])]
  transfers between devices with their start and end apart: 6 -> 6, of which waited for: 2 -> 2; matrix products, arithmetic and copies ran while one was open for 1% -> 2% of each run, Pallas kernels for 6% -> 7%
where the time goes in v10:
time: 79.7 us; the launch traced here: 79.2 us
  blocking collectives  30.4 us (38%)
  starting transfers between devices  24.1 us (30%)
  Pallas kernels  12.3 us (15%)
  waiting for transfers between devices  7.68 us (10%)
  matrix products  2.18 us (3%)
  other arithmetic  1.08 us (1%)
    all_to_all x1, blocking collectives, exchanged(): return lax.all_to_all(x, axis, 0, 0, tiled=True)  30.4 us
    pallas_call x5, Pallas kernels, call(): pl.pallas_call(kernel, out_shape=out_shape, in_specs=in_specs, out_specs=...  12.3 us
    all_to_all x1, starting transfers between devices, exchanged(): return lax.all_to_all(x, axis, 0, 0, tiled=True)  9.89 us
    ppermute x1, starting transfers between devices, projected(): other = lax.ppermute(own, 'gx', partner)  8.75 us
    all_to_all x1, waiting for transfers between devices, exchanged(): return lax.all_to_all(x, axis, 0, 0, tiled=True)  6.07 us
    dot_general x1, matrix products, projected(): jnp.dot(bands.reshape(cells, nb), jnp.concatenate((left, right), axis=1),...  2.18 us
    ppermute x1, starting transfers between devices, projected(): coef_other = lax.ppermute(coef, 'gx', partner)  1.91 us
    ppermute x1, starting transfers between devices, projected(): xhalo = lax.ppermute(slab, BOTH, x_pairs)  1.6 us
  transfers between devices with their start and end apart: 6, of which 2 were waited for; matrix products, arithmetic and copies ran while one was open for 2% of the time, Pallas kernels for 7%

profile of v10, /device:TPU:1, one launch (start us, length us, event | category | flops | bytes accessed | tf_op | source)
XLA Modules:
  0.0 79.2 jit_solution(17607128735909954948)
XLA Ops:
  0.6 2.8 %shard_map.58 = (bf16[9,5,40,512]{3,2,1,0:T(8,128)(2,1)}, bf16[8,40,512]{2,1,0:T(8,128)(2,1)S(1)}) custom-call(bf16[8,5,40,512]{3,2,1,0:T(8,128)(2,1)} %bands_ref.1, f32[5,8,40]{2,1,0:T(8,128)} %bitcast.17), custom_call_target="tpu_custom_call" | custom-call | bytes 1644800 | tf_op jit(solution)/shard_map/pallas_call | solution.py:29
  3.5 8.7 %collective-permute-start = (bf16[9,5,40,512]{3,2,1,0:T(8,128)(2,1)}, bf16[9,5,40,512]{3,2,1,0:T(8,128)(2,1)S(1)}, u32[]{:S(2)}, u32[]{:S(2)}) collective-permute-start(bf16[9,5,40,512]{3,2,1,0:T(8,128)(2,1)} %get-tuple-element.7.held_ref.own_ref), channel_id=1, source_target_pairs={{0,64},{64,0},{128,192},{192,128},{256,320},{320,256},{384,448},{4... | collective-permute-start | bytes 5529608 | tf_op jit(solution)/shard_map/ppermute | solution.py:231
  12.2 1.3 %collective-permute-start.1 = (bf16[8,40,512]{2,1,0:T(8,128)(2,1)S(1)}, bf16[8,40,512]{2,1,0:T(8,128)(2,1)S(1)}, u32[]{:S(2)}, u32[]{:S(2)}) collective-permute-start(bf16[8,40,512]{2,1,0:T(8,128)(2,1)S(1)} %get-tuple-element.8), channel_id=1, source_target_pairs={{64,65},{65,66},{66,67},{67,68},{68,69},{69,70},{70,71},{71,72},{7... | collective-permute-start | bytes 983048 | tf_op jit(solution)/shard_map/ppermute | solution.py:233
  13.6 0.7 collective-permute-start.2
  14.3 1.6 %collective-permute-done.held_ref.other_ref = bf16[9,5,40,512]{3,2,1,0:T(8,128)(2,1)S(1)} collective-permute-done((bf16[9,5,40,512]{3,2,1,0:T(8,128)(2,1)}, bf16[9,5,40,512]{3,2,1,0:T(8,128)(2,1)S(1)}, u32[]{:S(2)}, u32[]{:S(2)}) %collective-permute-start) | collective-permute-done | bytes 1843232 | tf_op jit(solution)/shard_map/ppermute | solution.py:231
  15.9 1.0 %fusion.3 = bf16[5,40,512]{2,1,0:T(8,128)(2,1)S(1)} fusion(bf16[9,5,40,512]{3,2,1,0:T(8,128)(2,1)S(1)} %collective-permute-done.held_ref.other_ref, bf16[9,5,40,512]{3,2,1,0:T(8,128)(2,1)} %get-tuple-element.7.held_ref.own_ref, pred[]{:T(512)S(6)} %eq.7), kind=kLoop, calls=%fused_computation.7 | loop fusion | flops 102400 | bytes 614401 | tf_op jit(solution)/shard_map/jit(_where)/select_n | solution.py:235
  16.8 1.6 %collective-permute-start.3 = (bf16[5,40,512]{2,1,0:T(8,128)(2,1)S(1)}, bf16[5,40,512]{2,1,0:T(8,128)(2,1)S(1)}, u32[]{:S(2)}, u32[]{:S(2)}) collective-permute-start(bf16[5,40,512]{2,1,0:T(8,128)(2,1)S(1)} %fusion.3), channel_id=1, source_target_pairs={{64,192},{193,65},{66,194},{195,67},{68,196},{197,69},{70,198},{19... | collective-permute-start | bytes 614408 | tf_op jit(solution)/shard_map/ppermute | solution.py:236
  18.4 0.1 pad_add_fusion.place_ref
  18.5 3.4 %shard_map.59.refs_0_ = f32[512,512]{1,0:T(8,128)S(1)} custom-call(s32[2]{0:T(128)S(1)} %pad_add_fusion.place_ref, bf16[9,5,40,512]{3,2,1,0:T(8,128)(2,1)} %get-tuple-element.7.held_ref.own_ref), custom_call_target="tpu_custom_call" | custom-call | flops 838860800 | bytes 1843208 | tf_op jit(solution)/shard_map/pallas_call | solution.py:29
  21.9 0.0 copy-start
  22.0 2.5 %shard_map.60.gram_ref = f32[512,512]{1,0:T(8,128)S(1)} custom-call(s32[2]{0:T(128)S(1)} %pad_add_fusion.place_ref, bf16[9,5,40,512]{3,2,1,0:T(8,128)(2,1)S(1)} %collective-permute-done.held_ref.other_ref, f32[512,512]{1,0:T(8,128)S(1)} %shard_map.59.refs_0_), custom_call_target="tpu_custom_call" | custom-call | flops 838860800 | bytes 2891784 | tf_op jit(solution)/shard_map/pallas_call | solution.py:29
  24.5 0.0 collective-permute-done.1.yown_ref
  24.5 0.0 collective-permute-done.2.yother_ref
  24.5 0.0 collective-permute-done.3.xhalo_ref
  24.5 2.8 %shard_map.61 = bf16[64,8,768]{2,1,0:T(8,128)(2,1)S(1)} custom-call(s32[2]{0:T(128)S(1)} %pad_add_fusion.place_ref, f32[512,512]{1,0:T(8,128)S(1)} %shard_map.60.gram_ref, bf16[9,5,40,512]{3,2,1,0:T(8,128)(2,1)} %get-tuple-element.7.held_ref.own_ref, bf16[9,5,40,512]{3,2,1,0:T(8,128)(2,1)S(1)} %collective-permute-done.held_ref.other_ref, ...), custom_call_target="tpu_custom_call" | custom-call | flops 440401920 | bytes 5603336 | tf_op jit(solution)/shard_map/pallas_call | solution.py:29
  27.3 0.0 copy-start.1
  27.3 30.4 %all_to_all.10.in_ref = bf16[64,8,768]{2,1,0:T(8,128)(2,1)S(1)} all-to-all(bf16[64,8,768]{2,1,0:T(8,128)(2,1)S(1)} %shard_map.61), channel_id=1, replica_groups=mesh['gx'=8,'gyz'=64] {'gyz'}, dimensions={0} | all-to-all | bytes 1572864 | tf_op jit(solution)/shard_map/all_to_all | solution.py:215
  57.7 0.8 shard_map.62
  58.5 9.9 %all-to-all-start.1 = ((f32[8,8,512]{2,1,0:T(8,128)}), f32[8,8,512]{2,1,0:T(8,128)S(1)}, u32[]{:S(2)}, u32[]{:S(2)}) async-start(f32[8,8,512]{2,1,0:T(8,128)} %get-tuple-element.9), calls=%async_computation.1 | async-start | bytes 262144 | tf_op jit(solution)/shard_map/all_to_all | solution.py:215
  68.4 1.9 %collective-permute-start.4 = (bf16[512,256]{1,0:T(8,128)(2,1)S(1)}, bf16[512,256]{1,0:T(8,128)(2,1)S(1)}, u32[]{:S(2)}, u32[]{:S(2)}) collective-permute-start(bf16[512,256]{1,0:T(8,128)(2,1)S(1)} %get-tuple-element.10), channel_id=1, source_target_pairs={{0,64},{64,0},{128,192},{192,128},{256,320},{320,256},{384,448},{4... | collective-permute-start | bytes 786440 | tf_op jit(solution)/shard_map/ppermute | solution.py:241
  70.3 6.1 %all-to-all-done.1 = f32[8,8,512]{2,1,0:T(8,128)S(1)} async-done(((f32[8,8,512]{2,1,0:T(8,128)}), f32[8,8,512]{2,1,0:T(8,128)S(1)}, u32[]{:S(2)}, u32[]{:S(2)}) %all-to-all-start.1) | async-done | bytes 131104 | tf_op jit(solution)/shard_map/all_to_all | solution.py:215
  76.4 0.6 slice_bitcast_fusion
  77.0 0.0 collective-permute-done.4
  77.0 2.2 %convolution_convert_fusion = bf16[512,1600]{0,1:T(8,128)(2,1)} fusion(bf16[1600,512]{1,0:T(8,128)(2,1)S(1)} %bitcast.15, bf16[512,256]{1,0:T(8,128)(2,1)S(1)} %get-tuple-element.12, bf16[512,256]{1,0:T(8,128)(2,1)S(1)} %get-tuple-element.11), kind=kOutput, calls=%fused_computation | convolution fusion | flops 840728576 | bytes 3801088 | tf_op jit(solution)/shard_map/dot_general | solution.py:247
  (4 shorter events, 0.1 us)
Async XLA Ops:
  3.5 12.4 %collective-permute-start = (bf16[9,5,40,512]{3,2,1,0:T(8,128)(2,1)}, bf16[9,5,40,512]{3,2,1,0:T(8,128)(2,1)S(1)}, u32[]{:S(2)}, u32[]{:S(2)}) collective-permute-start(bf16[9,5,40,512]{3,2,1,0:T(8,128)(2,1)} %get-tuple-element.7.held_ref.own_ref), channel_id=1, source_target_pairs={{0,64},{64,0},{128,192},{192,128},{256,320},{320,256},{384,448},{4... | collective-permute-start | bytes 5529608 | tf_op jit(solution)/shard_map/ppermute | solution.py:231
  12.2 12.2 %collective-permute-start.1 = (bf16[8,40,512]{2,1,0:T(8,128)(2,1)S(1)}, bf16[8,40,512]{2,1,0:T(8,128)(2,1)S(1)}, u32[]{:S(2)}, u32[]{:S(2)}) collective-permute-start(bf16[8,40,512]{2,1,0:T(8,128)(2,1)S(1)} %get-tuple-element.8), channel_id=1, source_target_pairs={{64,65},{65,66},{66,67},{67,68},{68,69},{69,70},{70,71},{71,72},{7... | collective-permute-start | bytes 983048 | tf_op jit(solution)/shard_map/ppermute | solution.py:233
  13.6 10.9 %collective-permute-start.2 = (bf16[8,40,512]{2,1,0:T(8,128)(2,1)S(1)}, bf16[8,40,512]{2,1,0:T(8,128)(2,1)S(1)}, u32[]{:S(2)}, u32[]{:S(2)}) collective-permute-start(bf16[8,40,512]{2,1,0:T(8,128)(2,1)S(1)} %get-tuple-element.8), channel_id=1, source_target_pairs={{0,65},{1,66},{2,67},{3,68},{4,69},{5,70},{6,71},{7,72},{8,73},{9,... | collective-permute-start | bytes 983048 | tf_op jit(solution)/shard_map/ppermute | solution.py:232
  16.8 7.7 %collective-permute-start.3 = (bf16[5,40,512]{2,1,0:T(8,128)(2,1)S(1)}, bf16[5,40,512]{2,1,0:T(8,128)(2,1)S(1)}, u32[]{:S(2)}, u32[]{:S(2)}) collective-permute-start(bf16[5,40,512]{2,1,0:T(8,128)(2,1)S(1)} %fusion.3), channel_id=1, source_target_pairs={{64,192},{193,65},{66,194},{195,67},{68,196},{197,69},{70,198},{19... | collective-permute-start | bytes 614408 | tf_op jit(solution)/shard_map/ppermute | solution.py:236
  21.9 2.5 %copy-start = (bf16[8,512]{1,0:T(8,128)(2,1)S(1)}, bf16[8,512]{1,0:T(8,128)(2,1)}, u32[]{:S(2)}) copy-start(bf16[8,512]{1,0:T(8,128)(2,1)} %coef_ref.1) | copy-start | bytes 24580
  27.3 49.8 %copy-start.1 = (bf16[8,5,40,512]{3,2,1,0:T(8,128)(2,1)S(1)}, bf16[8,5,40,512]{3,2,1,0:T(8,128)(2,1)}, u32[]{:S(2)}) copy-start(bf16[8,5,40,512]{3,2,1,0:T(8,128)(2,1)} %bands_ref.1) | copy-start | bytes 4915204
  58.5 17.9 %all-to-all-start.1 = ((f32[8,8,512]{2,1,0:T(8,128)}), f32[8,8,512]{2,1,0:T(8,128)S(1)}, u32[]{:S(2)}, u32[]{:S(2)}) async-start(f32[8,8,512]{2,1,0:T(8,128)} %get-tuple-element.9), calls=%async_computation.1 | async-start | bytes 262144 | tf_op jit(solution)/shard_map/all_to_all | solution.py:215
  68.4 8.6 %collective-permute-start.4 = (bf16[512,256]{1,0:T(8,128)(2,1)S(1)}, bf16[512,256]{1,0:T(8,128)(2,1)S(1)}, u32[]{:S(2)}, u32[]{:S(2)}) collective-permute-start(bf16[512,256]{1,0:T(8,128)(2,1)S(1)} %get-tuple-element.10), channel_id=1, source_target_pairs={{0,64},{64,0},{128,192},{192,128},{256,320},{320,256},{384,448},{4... | collective-permute-start | bytes 786440 | tf_op jit(solution)/shard_map/ppermute | solution.py:241

commit v11 on v9

--- a/solution.py
+++ b/solution.py
@@ -124,71 +124,96 @@
     )
 
 
+def pick_kernel(place_ref, last_ref, other_ref, slab_ref):
+    @pl.when(place_ref[1] == 0)
+    def _():
+        slab_ref[...] = last_ref[...]
+
+    @pl.when(place_ref[1] != 0)
+    def _():
+        slab_ref[...] = other_ref[0]
+
+
+def pick(place, last, other):
+    return call(
+        pick_kernel,
+        jax.ShapeDtypeStruct(last.shape, BF16),
+        [SMEM, VMEM, VMEM],
+        (place, last, other),
+    )
+
+
 def cross_kernel(
-    scale, place_ref, gram_ref, own_ref, other_ref, yown_ref, yother_ref, xhalo_ref, coef_ref, out_ref
+    scale, place_ref, gram_ref, own_ref, other_ref, yown_ref, yother_ref, xhalo_ref, out_ref
 ):
     _, _, nb = xhalo_ref.shape
     nx = yown_ref.shape[0]
-    count, depth, _ = out_ref.shape
 
     def rows(value):
         return value.reshape(-1, nb)
 
-    def send(total):
-        out_ref[:, :, 0:nb] = total.astype(BF16).reshape(count, depth, nb)
-
+    cross = over_rows(rows(own_ref[0:nx, 0]), rows(yown_ref[...]))
+    cross += over_rows(rows(other_ref[0:nx, 0]), rows(yother_ref[...]))
+    slab = jnp.where(place_ref[1] == 0, other_ref[0], own_ref[nx - 1])
+    cross += over_rows(rows(slab), rows(xhalo_ref[...]))
+    cross += over_rows(rows(own_ref[0]), rows(other_ref[nx - 1]))
+    gram = gram_ref[...] - 0.5 * cross
+    out_ref[...] = (scale * (gram + jnp.transpose(gram))).astype(BF16).reshape(out_ref.shape)
+
+
+def with_cross(scale, depth, place, gram, own, other, yown, yother, xhalo):
+    nb = gram.shape[0]
+    halo_rows = (yown.size + yother.size + xhalo.size) // nb
+    return call(
+        functools.partial(cross_kernel, scale),
+        jax.ShapeDtypeStruct((nb // depth, depth, nb), BF16),
+        [SMEM] + [VMEM] * 6,
+        (place, gram, own, other, yown, yother, xhalo),
+        flops=2 * halo_rows * nb * nb,
+    )
+
+
+def beside_kernel(scale, gram_ref, coef_ref, out_ref):
+    count, depth, _ = out_ref.shape
+    nb = gram_ref.shape[1]
+    out_ref[:, :, 0:nb] = (scale * gram_ref[...]).astype(BF16).reshape(count, depth, nb)
     coef = coef_ref[...]
-    half = jnp.where(place_ref[0] == 0, coef[:, : nb // 2], coef[:, nb // 2 :])
     for target in range(count):
-        out_ref[target, :, nb:] = half
-
-    @pl.when(place_ref[0] == 1)
-    def _():
-        cross = over_rows(rows(own_ref[0:nx, 0]), rows(yown_ref[...]))
-        cross += over_rows(rows(other_ref[0:nx, 0]), rows(yother_ref[...]))
-        slab = jnp.where(place_ref[1] == 0, other_ref[0], own_ref[nx - 1])
-        cross += over_rows(rows(slab), rows(xhalo_ref[...]))
-        cross += over_rows(rows(own_ref[0]), rows(other_ref[nx - 1]))
-        gram = gram_ref[...] - 0.5 * cross
-        send(scale * (gram + jnp.transpose(gram)))
-
-    @pl.when(place_ref[0] == 0)
-    def _():
-        send(scale * gram_ref[...])
-
-
-def add_cross(scale, place, gram, own, other, yown, yother, xhalo, coef):
-    nb = gram.shape[0]
-    depth = coef.shape[0]
-    halo_rows = (yown.size + yother.size + xhalo.size) // nb
-    return call(
-        functools.partial(cross_kernel, scale),
-        jax.ShapeDtypeStruct((nb // depth, depth, nb + nb // 2), BF16),
-        [SMEM] + [VMEM] * 7,
-        (place, gram, own, other, yown, yother, xhalo, coef),
-        flops=2 * halo_rows * nb * nb,
+        out_ref[target, :, nb:] = coef
+
+
+def beside_coef(scale, gram, coef):
+    depth, nb = coef.shape
+    return call(
+        functools.partial(beside_kernel, scale),
+        jax.ShapeDtypeStruct((nb // depth, depth, 2 * nb), BF16),
+        [VMEM] * 2,
+        (gram, coef),
     )
 
 
 def finish_kernel(in_ref, rows_ref, coef_ref):
-    sources, _, _ = in_ref.shape
+    sources, _, width = in_ref.shape
     nb = rows_ref.shape[-1]
     total = in_ref[0, :, 0:nb].astype(F32)
     for s in range(1, sources):
         total += in_ref[s, :, 0:nb].astype(F32)
     for c in range(rows_ref.shape[0]):
         rows_ref[c] = total
-    coef_ref[...] = in_ref[:, :, nb:].reshape(coef_ref.shape)
+    if width > nb:
+        coef_ref[...] = in_ref[:, :, nb:].reshape(coef_ref.shape)
+    else:
+        coef_ref[...] = jnp.zeros(coef_ref.shape, BF16)
 
 
 def finish(arrived, copies):
-    sources, depth, width = arrived.shape
+    sources, depth, _ = arrived.shape
     nb = sources * depth
     return call(
         finish_kernel,
         (
             jax.ShapeDtypeStruct((copies, depth, nb), F32),
-            jax.ShapeDtypeStruct((nb, width - nb), BF16),
+            jax.ShapeDtypeStruct((nb, nb), BF16),
         ),
         [VMEM],
         (arrived,),
@@ -209,7 +234,7 @@
             if r % 2 == 0:
                 x.append((at(2 * chip + 1, r), at(2 * chip + 3, r)))
             else:
-                x.append((at(2 * chip + 2, r), at(2 * chip + 1, r)))
+                x.append((at(2 * chip + 3, r), at(2 * chip + 1, r)))
     return same, next_core, x
 
 
@@ -233,23 +258,28 @@
     yother = lax.ppermute(last, BOTH, next_core)
     yown = lax.ppermute(last, BOTH, same)
     other = lax.ppermute(own, "gx", partner)
+    slab = pick(place, slab, other)
     xhalo = lax.ppermute(slab, BOTH, x_pairs)
     gram = half_gram(place, own)
     gram = half_gram(place, other, (gram,))
-    sent = add_cross(scale, place, gram, own, other, yown, yother, xhalo, eigenvectors)
-    arrived = exchanged(sent, "gyz")
-    rows, coef = finish(arrived, gx)
-    coef_other = lax.ppermute(coef, "gx", partner)
+
+    def correlation_rows(*_):
+        sent = beside_coef(scale, gram, eigenvectors)
+        return finish(exchanged(sent, "gyz"), gx)
+
+    def hamiltonian_rows(*halos):
+        sent = with_cross(scale, eigenvectors.shape[0], place, gram, own, other, *halos)
+        return finish(exchanged(sent, "gyz"), gx)
+
+    rows, coef = lax.cond(
+        core == 0, correlation_rows, hamiltonian_rows, yown, yother, xhalo
+    )
+    coef_other = lax.ppermute(coef, "gx", [(g, g + 1) for g in range(0, gx, 2)])
     parts = exchanged(rows, "gx")
     sums = parts.reshape(gx // 2, 2, *parts.shape[1:]).sum(axis=0)
 
-    left = jnp.where(core == 0, coef, coef_other)
-    right = jnp.where(core == 0, coef_other, coef)
-    rotated = jnp.dot(
-        bands.reshape(cells, nb),
-        jnp.concatenate((left, right), axis=1),
-        preferred_element_type=F32,
-    ).astype(BF16)
+    coef = jnp.where(core == 0, coef, coef_other)
+    rotated = jnp.dot(bands.reshape(cells, nb), coef, preferred_element_type=F32).astype(BF16)
     return sums[0], sums[1], rotated.reshape(bands.shape)
 
 

time: 79 us -> 77.6 us (0.982)
  the two profiles are of different devices: /device:TPU:1 before, /device:TPU:2 now
where the time goes in v11:
time: 77.6 us; the launch traced here: 77.3 us
  blocking collectives  50.7 us (65%)
  starting transfers between devices  15.2 us (20%)
  Pallas kernels  7.6 us (10%)
  matrix products  2.19 us (3%)
    all_to_all x2, blocking collectives, exchanged(): return lax.all_to_all(x, axis, 0, 0, tiled=True)  50.7 us
    pallas_call x6, Pallas kernels, call(): pl.pallas_call(kernel, out_shape=out_shape, in_specs=in_specs, out_specs=...  7.6 us
    ppermute x1, starting transfers between devices, projected(): coef_other = lax.ppermute(coef, 'gx', [(g, g + 1) for g in range(0, gx, 2)])  5.41 us
    ppermute x1, starting transfers between devices, projected(): yother = lax.ppermute(last, BOTH, next_core)  5.12 us
    dot_general x1, matrix products, projected(): jnp.dot(bands.reshape(cells, nb), coef, preferred_element_type=F32)  2.19 us
    ppermute x1, starting transfers between devices, projected(): other = lax.ppermute(own, 'gx', partner)  1.92 us
  transfers between devices with their start and end apart: 5, of which 0 were waited for; matrix products, arithmetic and copies ran while one was open for 1% of the time, Pallas kernels for 7%

profile of v11, /device:TPU:2, one launch (start us, length us, event | category | flops | bytes accessed | tf_op | source)
XLA Modules:
  0.0 77.3 jit_solution(1054089710054671860)
XLA Ops:
  0.6 0.1 pad_add_fusion.place_ref
  0.7 2.2 %shard_map.59 = (bf16[9,5,40,512]{3,2,1,0:T(8,128)(2,1)S(1)}, bf16[8,40,512]{2,1,0:T(8,128)(2,1)S(1)}, bf16[5,40,512]{2,1,0:T(8,128)(2,1)S(1)}) custom-call(s32[2]{0:T(128)S(1)} %pad_add_fusion.place_ref, bf16[8,5,40,512]{3,2,1,0:T(8,128)(2,1)} %bands_ref.1, f32[5,8,40]{2,1,0:T(8,128)} %bitcast.15), custom_call_target="tpu_custom_call" | custom-call | bytes 1644808 | tf_op jit(solution)/shard_map/pallas_call | solution.py:29
  3.0 1.9 %collective-permute-start = (bf16[9,5,40,512]{3,2,1,0:T(8,128)(2,1)S(1)}, bf16[9,5,40,512]{3,2,1,0:T(8,128)(2,1)S(1)}, u32[]{:S(2)}, u32[]{:S(2)}) collective-permute-start(bf16[9,5,40,512]{3,2,1,0:T(8,128)(2,1)S(1)} %get-tuple-element.35.held_ref), channel_id=1, source_target_pairs={{0,64},{64,0},{128,192},{192,128},{256,320},{320,256},{384,448},{4... | collective-permute-start | bytes 5529608 | tf_op jit(solution)/shard_map/ppermute | solution.py:260
  4.9 5.1 %collective-permute-start.2 = (bf16[8,40,512]{2,1,0:T(8,128)(2,1)S(1)}, bf16[8,40,512]{2,1,0:T(8,128)(2,1)}, u32[]{:S(2)}, u32[]{:S(2)}) collective-permute-start(bf16[8,40,512]{2,1,0:T(8,128)(2,1)S(1)} %get-tuple-element.36), channel_id=1, source_target_pairs={{0,65},{1,66},{2,67},{3,68},{4,69},{5,70},{6,71},{7,72},{8,73},{9,... | collective-permute-start | bytes 983048 | tf_op jit(solution)/shard_map/ppermute | solution.py:258
  10.0 1.4 %collective-permute-start.1 = (bf16[8,40,512]{2,1,0:T(8,128)(2,1)S(1)}, bf16[8,40,512]{2,1,0:T(8,128)(2,1)}, u32[]{:S(2)}, u32[]{:S(2)}) collective-permute-start(bf16[8,40,512]{2,1,0:T(8,128)(2,1)S(1)} %get-tuple-element.36), channel_id=1, source_target_pairs={{64,65},{65,66},{66,67},{67,68},{68,69},{69,70},{70,71},{71,72},{7... | collective-permute-start | bytes 983048 | tf_op jit(solution)/shard_map/ppermute | solution.py:259
  11.4 0.0 collective-permute-done.held_ref.other_ref
  11.4 0.6 shard_map.62
  12.0 1.4 %collective-permute-start.3 = (bf16[5,40,512]{2,1,0:T(8,128)(2,1)S(1)}, bf16[5,40,512]{2,1,0:T(8,128)(2,1)}, u32[]{:S(2)}, u32[]{:S(2)}) collective-permute-start(bf16[5,40,512]{2,1,0:T(8,128)(2,1)S(1)} %shard_map.62), channel_id=1, source_target_pairs={{64,192},{193,65},{66,194},{195,67},{68,196},{197,69},{70,198},{19... | collective-permute-start | bytes 614408 | tf_op jit(solution)/shard_map/ppermute | solution.py:262
  13.4 2.8 %shard_map.60.refs_0_ = f32[512,512]{1,0:T(8,128)S(1)} custom-call(s32[2]{0:T(128)S(1)} %pad_add_fusion.place_ref, bf16[9,5,40,512]{3,2,1,0:T(8,128)(2,1)} %copy-done), custom_call_target="tpu_custom_call" | custom-call | flops 838860800 | bytes 1843208 | tf_op jit(solution)/shard_map/pallas_call | solution.py:29
  16.1 0.0 copy-start.3
  16.2 1.8 %shard_map.61 = f32[512,512]{1,0:T(8,128)S(1)} custom-call(s32[2]{0:T(128)S(1)} %pad_add_fusion.place_ref, bf16[9,5,40,512]{3,2,1,0:T(8,128)(2,1)S(1)} %collective-permute-done.held_ref.other_ref, f32[512,512]{1,0:T(8,128)S(1)} %shard_map.60.refs_0_), custom_call_target="tpu_custom_call" | custom-call | flops 838860800 | bytes 2891784 | tf_op jit(solution)/shard_map/pallas_call | solution.py:29
  18.0 0.0 collective-permute-done.2
  18.0 0.0 collective-permute-done.1
  18.0 0.0 collective-permute-done.3
  18.0 0.0 copy-start.2
  18.0 31.3 %conditional.1 = ((f32[8,8,512]{2,1,0:T(8,128)S(1)}, bf16[512,512]{1,0:T(8,128)(2,1)S(1)})) conditional(s32[]{:T(128)} %convert_element_type.9, (s32[2]{0:T(128)S(1)}, f32[512,512]{1,0:T(8,128)S(1)}, bf16[9,5,40,512]{3,2,1,0:T(8,128)(2,1)S(1)}, bf16[9,5,40,512]{3,2,1,0:T(8,128)(2,1)S(1)}, bf16[8,40,512]{2,1,0:T(8,128)(2,1)}, ...), branch_computations={%region_0.0_spmd, %region_1.0_spmd} | conditional | flops 440401920 | bytes 7168016 | solution.py:274
  18.0 0.1 branch_1_fun.2
  18.2 31.0 %all_to_all.14.in_ref = bf16[64,8,1024]{2,1,0:T(8,128)(2,1)S(1)} all-to-all(bf16[64,8,1024]{2,1,0:T(8,128)(2,1)S(1)} %branch_1_fun.2), channel_id=1, replica_groups=mesh['gx'=8,'gyz'=64] {'gyz'}, dimensions={0} | all-to-all | bytes 2097152 | tf_op jit(solution)/shard_map/cond/branch_1_fun/all_to_all | solution.py:242
  49.2 0.1 branch_1_fun.3
  49.3 5.4 %collective-permute-start.4 = (bf16[512,512]{1,0:T(8,128)(2,1)S(1)}, bf16[512,512]{1,0:T(8,128)(2,1)S(1)}, u32[]{:S(2)}, u32[]{:S(2)}) collective-permute-start(bf16[512,512]{1,0:T(8,128)(2,1)S(1)} %get-tuple-element.39), channel_id=1, source_target_pairs={{0,64},{128,192},{256,320},{384,448},{1,65},{129,193},{257,321},{3... | collective-permute-start | bytes 1572872 | tf_op jit(solution)/shard_map/ppermute | solution.py:277
  54.8 19.7 %all_to_all.15 = f32[8,8,512]{2,1,0:T(8,128)S(1)} all-to-all(f32[8,8,512]{2,1,0:T(8,128)S(1)} %get-tuple-element.38), channel_id=1, replica_groups=mesh['gx'=8,'gyz'=64] {'gx'}, dimensions={0} | all-to-all | bytes 262144 | tf_op jit(solution)/shard_map/all_to_all | solution.py:242
  74.5 0.6 slice_bitcast_fusion
  75.1 0.0 collective-permute-done.4
  75.1 2.2 %convolution_convert_fusion = bf16[512,1600]{0,1:T(8,128)(2,1)} fusion(bf16[1600,512]{1,0:T(8,128)(2,1)S(1)} %bitcast.13, bf16[512,512]{1,0:T(8,128)(2,1)S(1)} %get-tuple-element.39, bf16[512,512]{1,0:T(8,128)(2,1)S(1)} %collective-permute-done.4, pred[]{:T(512)S(6)} %eq.4), kind=kOutput, calls=%fused_computation | convolution fusion | flops 839942144 | bytes 4325377 | tf_op jit(solution)/shard_map/dot_general | solution.py:282
  (7 shorter events, 0.0 us)
Async XLA Ops:
  3.0 9.1 %copy-start = (bf16[9,5,40,512]{3,2,1,0:T(8,128)(2,1)}, bf16[9,5,40,512]{3,2,1,0:T(8,128)(2,1)S(1)}, u32[]{:S(2)}) copy-start(bf16[9,5,40,512]{3,2,1,0:T(8,128)(2,1)S(1)} %get-tuple-element.35.held_ref) | copy-start | bytes 5529604
  3.0 8.5 %collective-permute-start = (bf16[9,5,40,512]{3,2,1,0:T(8,128)(2,1)S(1)}, bf16[9,5,40,512]{3,2,1,0:T(8,128)(2,1)S(1)}, u32[]{:S(2)}, u32[]{:S(2)}) collective-permute-start(bf16[9,5,40,512]{3,2,1,0:T(8,128)(2,1)S(1)} %get-tuple-element.35.held_ref), channel_id=1, source_target_pairs={{0,64},{64,0},{128,192},{192,128},{256,320},{320,256},{384,448},{4... | collective-permute-start | bytes 5529608 | tf_op jit(solution)/shard_map/ppermute | solution.py:260
  4.9 13.1 %collective-permute-start.2 = (bf16[8,40,512]{2,1,0:T(8,128)(2,1)S(1)}, bf16[8,40,512]{2,1,0:T(8,128)(2,1)}, u32[]{:S(2)}, u32[]{:S(2)}) collective-permute-start(bf16[8,40,512]{2,1,0:T(8,128)(2,1)S(1)} %get-tuple-element.36), channel_id=1, source_target_pairs={{0,65},{1,66},{2,67},{3,68},{4,69},{5,70},{6,71},{7,72},{8,73},{9,... | collective-permute-start | bytes 983048 | tf_op jit(solution)/shard_map/ppermute | solution.py:258
  10.0 8.0 %collective-permute-start.1 = (bf16[8,40,512]{2,1,0:T(8,128)(2,1)S(1)}, bf16[8,40,512]{2,1,0:T(8,128)(2,1)}, u32[]{:S(2)}, u32[]{:S(2)}) collective-permute-start(bf16[8,40,512]{2,1,0:T(8,128)(2,1)S(1)} %get-tuple-element.36), channel_id=1, source_target_pairs={{64,65},{65,66},{66,67},{67,68},{68,69},{69,70},{70,71},{71,72},{7... | collective-permute-start | bytes 983048 | tf_op jit(solution)/shard_map/ppermute | solution.py:259
  12.0 6.0 %collective-permute-start.3 = (bf16[5,40,512]{2,1,0:T(8,128)(2,1)S(1)}, bf16[5,40,512]{2,1,0:T(8,128)(2,1)}, u32[]{:S(2)}, u32[]{:S(2)}) collective-permute-start(bf16[5,40,512]{2,1,0:T(8,128)(2,1)S(1)} %shard_map.62), channel_id=1, source_target_pairs={{64,192},{193,65},{66,194},{195,67},{68,196},{197,69},{70,198},{19... | collective-permute-start | bytes 614408 | tf_op jit(solution)/shard_map/ppermute | solution.py:262
  16.1 1.9 %copy-start.1 = (bf16[9,5,40,512]{3,2,1,0:T(8,128)(2,1)S(1)}, bf16[9,5,40,512]{3,2,1,0:T(8,128)(2,1)}, u32[]{:S(2)}) copy-start(bf16[9,5,40,512]{3,2,1,0:T(8,128)(2,1)} %copy-done) | copy-start | bytes 5529604
  16.1 1.9 %copy-start.3 = (bf16[8,512]{1,0:T(8,128)(2,1)S(1)}, bf16[8,512]{1,0:T(8,128)(2,1)}, u32[]{:S(2)}) copy-start(bf16[8,512]{1,0:T(8,128)(2,1)} %param.7) | copy-start | bytes 24580
  18.0 57.1 %copy-start.2 = (bf16[8,5,40,512]{3,2,1,0:T(8,128)(2,1)S(1)}, bf16[8,5,40,512]{3,2,1,0:T(8,128)(2,1)}, u32[]{:S(2)}) copy-start(bf16[8,5,40,512]{3,2,1,0:T(8,128)(2,1)} %bands_ref.1) | copy-start | bytes 4915204
  49.3 25.7 %collective-permute-start.4 = (bf16[512,512]{1,0:T(8,128)(2,1)S(1)}, bf16[512,512]{1,0:T(8,128)(2,1)S(1)}, u32[]{:S(2)}, u32[]{:S(2)}) collective-permute-start(bf16[512,512]{1,0:T(8,128)(2,1)S(1)} %get-tuple-element.39), channel_id=1, source_target_pairs={{0,64},{128,192},{256,320},{384,448},{1,65},{129,193},{257,321},{3... | collective-permute-start | bytes 1572872 | tf_op jit(solution)/shard_map/ppermute | solution.py:277

commit v12 on v9

--- a/solution.py
+++ b/solution.py
@@ -124,11 +124,59 @@
     )
 
 
+def pick_kernel(place_ref, last_ref, other_ref, slab_ref):
+    @pl.when(place_ref[1] == 0)
+    def _():
+        slab_ref[...] = last_ref[...]
+
+    @pl.when(place_ref[1] != 0)
+    def _():
+        slab_ref[...] = other_ref[0]
+
+
+def pick(place, last, other):
+    return call(
+        pick_kernel,
+        jax.ShapeDtypeStruct(last.shape, BF16),
+        [SMEM, VMEM, VMEM],
+        (place, last, other),
+    )
+
+
+def sides_kernel(place_ref, gram_ref, own_ref, other_ref, yown_ref, yother_ref, out_ref):
+    nx, _, nb = yown_ref.shape
+
+    def rows(value):
+        return value.reshape(-1, nb)
+
+    @pl.when(place_ref[0] == 1)
+    def _():
+        cross = over_rows(rows(own_ref[0:nx, 0]), rows(yown_ref[...]))
+        cross += over_rows(rows(other_ref[0:nx, 0]), rows(yother_ref[...]))
+        cross += over_rows(rows(own_ref[0]), rows(other_ref[nx - 1]))
+        out_ref[...] = gram_ref[...] - 0.5 * cross
+
+    @pl.when(place_ref[0] == 0)
+    def _():
+        out_ref[...] = gram_ref[...]
+
+
+def add_sides(place, gram, own, other, yown, yother):
+    nb = gram.shape[0]
+    return call(
+        sides_kernel,
+        jax.ShapeDtypeStruct(gram.shape, F32),
+        [SMEM] + [VMEM] * 5,
+        (place, gram, own, other, yown, yother),
+        flops=2 * (yown.size + yother.size) * nb,
+    )
+
+
 def cross_kernel(
-    scale, place_ref, gram_ref, own_ref, other_ref, yown_ref, yother_ref, xhalo_ref, coef_ref, out_ref
+    scale, place_ref, gram_ref, own_ref, other_ref, xhalo_ref, coef_ref, out_ref
 ):
     _, _, nb = xhalo_ref.shape
-    nx = yown_ref.shape[0]
+    nx = own_ref.shape[0] - 1
     count, depth, _ = out_ref.shape
 
     def rows(value):
@@ -144,12 +192,8 @@
 
     @pl.when(place_ref[0] == 1)
     def _():
-        cross = over_rows(rows(own_ref[0:nx, 0]), rows(yown_ref[...]))
-        cross += over_rows(rows(other_ref[0:nx, 0]), rows(yother_ref[...]))
         slab = jnp.where(place_ref[1] == 0, other_ref[0], own_ref[nx - 1])
-        cross += over_rows(rows(slab), rows(xhalo_ref[...]))
-        cross += over_rows(rows(own_ref[0]), rows(other_ref[nx - 1]))
-        gram = gram_ref[...] - 0.5 * cross
+        gram = gram_ref[...] - 0.5 * over_rows(rows(slab), rows(xhalo_ref[...]))
         send(scale * (gram + jnp.transpose(gram)))
 
     @pl.when(place_ref[0] == 0)
@@ -157,15 +201,15 @@
         send(scale * gram_ref[...])
 
 
-def add_cross(scale, place, gram, own, other, yown, yother, xhalo, coef):
+def add_cross(scale, place, gram, own, other, xhalo, coef):
     nb = gram.shape[0]
     depth = coef.shape[0]
-    halo_rows = (yown.size + yother.size + xhalo.size) // nb
+    halo_rows = xhalo.size // nb
     return call(
         functools.partial(cross_kernel, scale),
         jax.ShapeDtypeStruct((nb // depth, depth, nb + nb // 2), BF16),
-        [SMEM] + [VMEM] * 7,
-        (place, gram, own, other, yown, yother, xhalo, coef),
+        [SMEM] + [VMEM] * 5,
+        (place, gram, own, other, xhalo, coef),
         flops=2 * halo_rows * nb * nb,
     )
 
@@ -209,7 +253,7 @@
             if r % 2 == 0:
                 x.append((at(2 * chip + 1, r), at(2 * chip + 3, r)))
             else:
-                x.append((at(2 * chip + 2, r), at(2 * chip + 1, r)))
+                x.append((at(2 * chip + 3, r), at(2 * chip + 1, r)))
     return same, next_core, x
 
 
@@ -233,10 +277,12 @@
     yother = lax.ppermute(last, BOTH, next_core)
     yown = lax.ppermute(last, BOTH, same)
     other = lax.ppermute(own, "gx", partner)
+    slab = pick(place, slab, other)
     xhalo = lax.ppermute(slab, BOTH, x_pairs)
     gram = half_gram(place, own)
     gram = half_gram(place, other, (gram,))
-    sent = add_cross(scale, place, gram, own, other, yown, yother, xhalo, eigenvectors)
+    gram = add_sides(place, gram, own, other, yown, yother)
+    sent = add_cross(scale, place, gram, own, other, xhalo, eigenvectors)
     arrived = exchanged(sent, "gyz")
     rows, coef = finish(arrived, gx)
     coef_other = lax.ppermute(coef, "gx", partner)

time: 79 us -> 76.2 us (0.965)
  starting transfers between devices: 28.5 us -> 25.2 us
  blocking collectives: 29.9 us -> 28.2 us
  Pallas kernels: 9.9 us -> 11.2 us
    all_to_all x1, starting transfers between devices: 12.6 us -> 10.1 us  [exchanged(): return lax.all_to_all(x, axis, 0, 0, tiled=True)]
    all_to_all x1, blocking collectives: 29.9 us -> 28.2 us  [exchanged(): return lax.all_to_all(x, axis, 0, 0, tiled=True)]
    ppermute x1, waiting for transfers between devices: 0.01 us -> 1.39 us  [projected(): other = lax.ppermute(own, 'gx', partner)]
    pallas_call x5 -> x7, Pallas kernels: 9.9 us -> 11.2 us  [call(): pl.pallas_call(kernel, out_shape=out_shape, in_specs=in_specs, out_specs=...]
  transfers between devices with their start and end apart: 6 -> 6, of which waited for: 2 -> 2; matrix products, arithmetic and copies ran while one was open for 1% -> 1% of each run, Pallas kernels for 6% -> 9%
where the time goes in v12:
time: 76.2 us; the launch traced here: 75.9 us
  blocking collectives  28.2 us (37%)
  starting transfers between devices  25.2 us (33%)
  Pallas kernels  11.2 us (15%)
  waiting for transfers between devices  7.48 us (10%)
  matrix products  2.18 us (3%)
  between operations  0.79 us (1%)
    all_to_all x1, blocking collectives, exchanged(): return lax.all_to_all(x, axis, 0, 0, tiled=True)  28.2 us
    pallas_call x7, Pallas kernels, call(): pl.pallas_call(kernel, out_shape=out_shape, in_specs=in_specs, out_specs=...  11.2 us
    all_to_all x1, starting transfers between devices, exchanged(): return lax.all_to_all(x, axis, 0, 0, tiled=True)  10.1 us
    ppermute x1, starting transfers between devices, projected(): other = lax.ppermute(own, 'gx', partner)  8.75 us
    all_to_all x1, waiting for transfers between devices, exchanged(): return lax.all_to_all(x, axis, 0, 0, tiled=True)  6.07 us
    ppermute x1, starting transfers between devices, projected(): xhalo = lax.ppermute(slab, BOTH, x_pairs)  2.41 us
    dot_general x1, matrix products, projected(): jnp.dot(bands.reshape(cells, nb), jnp.concatenate((left, right), axis=1),...  2.18 us
    ppermute x1, starting transfers between devices, projected(): coef_other = lax.ppermute(coef, 'gx', partner)  1.91 us
  transfers between devices with their start and end apart: 6, of which 2 were waited for; matrix products, arithmetic and copies ran while one was open for 1% of the time, Pallas kernels for 9%

profile of v12, /device:TPU:1, one launch (start us, length us, event | category | flops | bytes accessed | tf_op | source)
XLA Modules:
  0.0 75.9 jit_solution(15827862820914971109)
XLA Ops:
  0.6 0.1 pad_add_fusion.place_ref
  0.7 2.2 %shard_map.58 = (bf16[9,5,40,512]{3,2,1,0:T(8,128)(2,1)S(1)}, bf16[8,40,512]{2,1,0:T(8,128)(2,1)S(1)}, bf16[5,40,512]{2,1,0:T(8,128)(2,1)S(1)}) custom-call(s32[2]{0:T(128)S(1)} %pad_add_fusion.place_ref, bf16[8,5,40,512]{3,2,1,0:T(8,128)(2,1)} %bands_ref.1, f32[5,8,40]{2,1,0:T(8,128)} %bitcast.15), custom_call_target="tpu_custom_call" | custom-call | bytes 1644808 | tf_op jit(solution)/shard_map/pallas_call | solution.py:29
  3.0 8.7 %collective-permute-start = (bf16[9,5,40,512]{3,2,1,0:T(8,128)(2,1)S(1)}, bf16[9,5,40,512]{3,2,1,0:T(8,128)(2,1)S(1)}, u32[]{:S(2)}, u32[]{:S(2)}) collective-permute-start(bf16[9,5,40,512]{3,2,1,0:T(8,128)(2,1)S(1)} %get-tuple-element.8.held_ref.own_ref), channel_id=1, source_target_pairs={{0,64},{64,0},{128,192},{192,128},{256,320},{320,256},{384,448},{4... | collective-permute-start | bytes 5529608 | tf_op jit(solution)/shard_map/ppermute | solution.py:279
  11.7 0.7 collective-permute-start.2
  12.4 1.3 %collective-permute-start.1 = (bf16[8,40,512]{2,1,0:T(8,128)(2,1)S(1)}, bf16[8,40,512]{2,1,0:T(8,128)(2,1)S(1)}, u32[]{:S(2)}, u32[]{:S(2)}) collective-permute-start(bf16[8,40,512]{2,1,0:T(8,128)(2,1)S(1)} %get-tuple-element.9), channel_id=1, source_target_pairs={{64,65},{65,66},{66,67},{67,68},{68,69},{69,70},{70,71},{71,72},{7... | collective-permute-start | bytes 983048 | tf_op jit(solution)/shard_map/ppermute | solution.py:278
  13.7 1.4 %collective-permute-done.held_ref.other_ref = bf16[9,5,40,512]{3,2,1,0:T(8,128)(2,1)S(1)} collective-permute-done((bf16[9,5,40,512]{3,2,1,0:T(8,128)(2,1)S(1)}, bf16[9,5,40,512]{3,2,1,0:T(8,128)(2,1)S(1)}, u32[]{:S(2)}, u32[]{:S(2)}) %collective-permute-start) | collective-permute-done | bytes 1843232 | tf_op jit(solution)/shard_map/ppermute | solution.py:279
  15.1 0.6 shard_map.62
  15.7 2.4 %collective-permute-start.3 = (bf16[5,40,512]{2,1,0:T(8,128)(2,1)S(1)}, bf16[5,40,512]{2,1,0:T(8,128)(2,1)S(1)}, u32[]{:S(2)}, u32[]{:S(2)}) collective-permute-start(bf16[5,40,512]{2,1,0:T(8,128)(2,1)S(1)} %shard_map.62), channel_id=1, source_target_pairs={{64,192},{193,65},{66,194},{195,67},{68,196},{197,69},{70,198},{19... | collective-permute-start | bytes 614408 | tf_op jit(solution)/shard_map/ppermute | solution.py:281
  18.1 2.5 %shard_map.59.refs_0_ = f32[512,512]{1,0:T(8,128)S(1)} custom-call(s32[2]{0:T(128)S(1)} %pad_add_fusion.place_ref, bf16[9,5,40,512]{3,2,1,0:T(8,128)(2,1)S(1)} %get-tuple-element.8.held_ref.own_ref), custom_call_target="tpu_custom_call" | custom-call | flops 838860800 | bytes 1843208 | tf_op jit(solution)/shard_map/pallas_call | solution.py:29
  20.6 2.6 %shard_map.60.gram_ref = f32[512,512]{1,0:T(8,128)S(1)} custom-call(s32[2]{0:T(128)S(1)} %pad_add_fusion.place_ref, bf16[9,5,40,512]{3,2,1,0:T(8,128)(2,1)S(1)} %collective-permute-done.held_ref.other_ref, f32[512,512]{1,0:T(8,128)S(1)} %shard_map.59.refs_0_), custom_call_target="tpu_custom_call" | custom-call | flops 838860800 | bytes 2891784 | tf_op jit(solution)/shard_map/pallas_call | solution.py:29
  23.2 0.0 copy-start
  23.2 0.0 collective-permute-done.2.yother_ref
  23.2 0.0 collective-permute-done.1.yown_ref
  23.2 1.4 %shard_map.61.gram_ref = f32[512,512]{1,0:T(8,128)S(1)} custom-call(s32[2]{0:T(128)S(1)} %pad_add_fusion.place_ref, f32[512,512]{1,0:T(8,128)S(1)} %shard_map.60.gram_ref, bf16[9,5,40,512]{3,2,1,0:T(8,128)(2,1)S(1)} %get-tuple-element.8.held_ref.own_ref, bf16[9,5,40,512]{3,2,1,0:T(8,128)(2,1)S(1)} %collective-permute-done.held_ref.other_ref, ...), custom_call_target="tpu_custom_call" | custom-call | flops 335544320 | bytes 5390344 | tf_op jit(solution)/shard_map/pallas_call | solution.py:29
  24.7 0.0 collective-permute-done.3.xhalo_ref
  24.7 1.2 %shard_map.63 = bf16[64,8,768]{2,1,0:T(8,128)(2,1)S(1)} custom-call(s32[2]{0:T(128)S(1)} %pad_add_fusion.place_ref, f32[512,512]{1,0:T(8,128)S(1)} %shard_map.61.gram_ref, bf16[9,5,40,512]{3,2,1,0:T(8,128)(2,1)S(1)} %get-tuple-element.8.held_ref.own_ref, bf16[9,5,40,512]{3,2,1,0:T(8,128)(2,1)S(1)} %collective-permute-done.held_ref.other_ref, ...), custom_call_target="tpu_custom_call" | custom-call | flops 104857600 | bytes 4947976 | tf_op jit(solution)/shard_map/pallas_call | solution.py:29
  25.9 0.0 copy-start.1
  25.9 28.2 %all_to_all.10.in_ref = bf16[64,8,768]{2,1,0:T(8,128)(2,1)S(1)} all-to-all(bf16[64,8,768]{2,1,0:T(8,128)(2,1)S(1)} %shard_map.63), channel_id=1, replica_groups=mesh['gx'=8,'gyz'=64] {'gyz'}, dimensions={0} | all-to-all | bytes 1572864 | tf_op jit(solution)/shard_map/all_to_all | solution.py:261
  54.1 0.8 %shard_map.64 = (f32[8,8,512]{2,1,0:T(8,128)}, bf16[512,256]{1,0:T(8,128)(2,1)S(1)}) custom-call(bf16[64,8,768]{2,1,0:T(8,128)(2,1)S(1)} %all_to_all.10.in_ref), custom_call_target="tpu_custom_call" | custom-call | bytes 786432 | tf_op jit(solution)/shard_map/pallas_call | solution.py:29
  54.9 10.1 %all-to-all-start.1 = ((f32[8,8,512]{2,1,0:T(8,128)}), f32[8,8,512]{2,1,0:T(8,128)S(1)}, u32[]{:S(2)}, u32[]{:S(2)}) async-start(f32[8,8,512]{2,1,0:T(8,128)} %get-tuple-element.11), calls=%async_computation.1 | async-start | bytes 262144 | tf_op jit(solution)/shard_map/all_to_all | solution.py:261
  65.0 1.9 %collective-permute-start.4 = (bf16[512,256]{1,0:T(8,128)(2,1)S(1)}, bf16[512,256]{1,0:T(8,128)(2,1)S(1)}, u32[]{:S(2)}, u32[]{:S(2)}) collective-permute-start(bf16[512,256]{1,0:T(8,128)(2,1)S(1)} %get-tuple-element.12), channel_id=1, source_target_pairs={{0,64},{64,0},{128,192},{192,128},{256,320},{320,256},{384,448},{4... | collective-permute-start | bytes 786440 | tf_op jit(solution)/shard_map/ppermute | solution.py:288
  66.9 6.1 %all-to-all-done.1 = f32[8,8,512]{2,1,0:T(8,128)S(1)} async-done(((f32[8,8,512]{2,1,0:T(8,128)}), f32[8,8,512]{2,1,0:T(8,128)S(1)}, u32[]{:S(2)}, u32[]{:S(2)}) %all-to-all-start.1) | async-done | bytes 131104 | tf_op jit(solution)/shard_map/all_to_all | solution.py:261
  73.0 0.6 slice_bitcast_fusion
  73.7 2.2 %convolution_convert_fusion = bf16[512,1600]{0,1:T(8,128)(2,1)} fusion(bf16[1600,512]{1,0:T(8,128)(2,1)S(1)} %bitcast.13, bf16[512,256]{1,0:T(8,128)(2,1)S(1)} %get-tuple-element.14, bf16[512,256]{1,0:T(8,128)(2,1)S(1)} %get-tuple-element.13), kind=kOutput, calls=%fused_computation | convolution fusion | flops 840728576 | bytes 3801088 | tf_op jit(solution)/shard_map/dot_general | solution.py:294
  (5 shorter events, 0.1 us)
Async XLA Ops:
  3.0 12.2 %collective-permute-start = (bf16[9,5,40,512]{3,2,1,0:T(8,128)(2,1)S(1)}, bf16[9,5,40,512]{3,2,1,0:T(8,128)(2,1)S(1)}, u32[]{:S(2)}, u32[]{:S(2)}) collective-permute-start(bf16[9,5,40,512]{3,2,1,0:T(8,128)(2,1)S(1)} %get-tuple-element.8.held_ref.own_ref), channel_id=1, source_target_pairs={{0,64},{64,0},{128,192},{192,128},{256,320},{320,256},{384,448},{4... | collective-permute-start | bytes 5529608 | tf_op jit(solution)/shard_map/ppermute | solution.py:279
  11.7 11.5 %collective-permute-start.2 = (bf16[8,40,512]{2,1,0:T(8,128)(2,1)S(1)}, bf16[8,40,512]{2,1,0:T(8,128)(2,1)S(1)}, u32[]{:S(2)}, u32[]{:S(2)}) collective-permute-start(bf16[8,40,512]{2,1,0:T(8,128)(2,1)S(1)} %get-tuple-element.9), channel_id=1, source_target_pairs={{0,65},{1,66},{2,67},{3,68},{4,69},{5,70},{6,71},{7,72},{8,73},{9,... | collective-permute-start | bytes 983048 | tf_op jit(solution)/shard_map/ppermute | solution.py:277
  12.4 10.8 %collective-permute-start.1 = (bf16[8,40,512]{2,1,0:T(8,128)(2,1)S(1)}, bf16[8,40,512]{2,1,0:T(8,128)(2,1)S(1)}, u32[]{:S(2)}, u32[]{:S(2)}) collective-permute-start(bf16[8,40,512]{2,1,0:T(8,128)(2,1)S(1)} %get-tuple-element.9), channel_id=1, source_target_pairs={{64,65},{65,66},{66,67},{67,68},{68,69},{69,70},{70,71},{71,72},{7... | collective-permute-start | bytes 983048 | tf_op jit(solution)/shard_map/ppermute | solution.py:278
  15.7 9.0 %collective-permute-start.3 = (bf16[5,40,512]{2,1,0:T(8,128)(2,1)S(1)}, bf16[5,40,512]{2,1,0:T(8,128)(2,1)S(1)}, u32[]{:S(2)}, u32[]{:S(2)}) collective-permute-start(bf16[5,40,512]{2,1,0:T(8,128)(2,1)S(1)} %shard_map.62), channel_id=1, source_target_pairs={{64,192},{193,65},{66,194},{195,67},{68,196},{197,69},{70,198},{19... | collective-permute-start | bytes 614408 | tf_op jit(solution)/shard_map/ppermute | solution.py:281
  23.2 1.5 %copy-start = (bf16[8,512]{1,0:T(8,128)(2,1)S(1)}, bf16[8,512]{1,0:T(8,128)(2,1)}, u32[]{:S(2)}) copy-start(bf16[8,512]{1,0:T(8,128)(2,1)} %coef_ref.1) | copy-start | bytes 24580
  25.9 47.8 %copy-start.1 = (bf16[8,5,40,512]{3,2,1,0:T(8,128)(2,1)S(1)}, bf16[8,5,40,512]{3,2,1,0:T(8,128)(2,1)}, u32[]{:S(2)}) copy-start(bf16[8,5,40,512]{3,2,1,0:T(8,128)(2,1)} %bands_ref.1) | copy-start | bytes 4915204
  54.9 18.1 %all-to-all-start.1 = ((f32[8,8,512]{2,1,0:T(8,128)}), f32[8,8,512]{2,1,0:T(8,128)S(1)}, u32[]{:S(2)}, u32[]{:S(2)}) async-start(f32[8,8,512]{2,1,0:T(8,128)} %get-tuple-element.11), calls=%async_computation.1 | async-start | bytes 262144 | tf_op jit(solution)/shard_map/all_to_all | solution.py:261
  65.0 8.6 %collective-permute-start.4 = (bf16[512,256]{1,0:T(8,128)(2,1)S(1)}, bf16[512,256]{1,0:T(8,128)(2,1)S(1)}, u32[]{:S(2)}, u32[]{:S(2)}) collective-permute-start(bf16[512,256]{1,0:T(8,128)(2,1)S(1)} %get-tuple-element.12), channel_id=1, source_target_pairs={{0,64},{64,0},{128,192},{192,128},{256,320},{320,256},{384,448},{4... | collective-permute-start | bytes 786440 | tf_op jit(solution)/shard_map/ppermute | solution.py:288

commit v13 on v9

--- a/solution.py
+++ b/solution.py
@@ -124,6 +124,25 @@
     )
 
 
+def pick_kernel(place_ref, last_ref, other_ref, slab_ref):
+    @pl.when(place_ref[1] == 0)
+    def _():
+        slab_ref[...] = last_ref[...]
+
+    @pl.when(place_ref[1] != 0)
+    def _():
+        slab_ref[...] = other_ref[0]
+
+
+def pick(place, last, other):
+    return call(
+        pick_kernel,
+        jax.ShapeDtypeStruct(last.shape, BF16),
+        [SMEM, VMEM, VMEM],
+        (place, last, other),
+    )
+
+
 def cross_kernel(
     scale, place_ref, gram_ref, own_ref, other_ref, yown_ref, yother_ref, xhalo_ref, coef_ref, out_ref
 ):
@@ -209,7 +228,7 @@
             if r % 2 == 0:
                 x.append((at(2 * chip + 1, r), at(2 * chip + 3, r)))
             else:
-                x.append((at(2 * chip + 2, r), at(2 * chip + 1, r)))
+                x.append((at(2 * chip + 3, r), at(2 * chip + 1, r)))
     return same, next_core, x
 
 
@@ -233,6 +252,7 @@
     yother = lax.ppermute(last, BOTH, next_core)
     yown = lax.ppermute(last, BOTH, same)
     other = lax.ppermute(own, "gx", partner)
+    slab = pick(place, slab, other)
     xhalo = lax.ppermute(slab, BOTH, x_pairs)
     gram = half_gram(place, own)
     gram = half_gram(place, other, (gram,))

time: 79 us -> 78.1 us (0.989)
  starting transfers between devices: 28.5 us -> 25.8 us
  waiting for transfers between devices: 6.76 us -> 7.55 us
    ppermute x1, waiting for transfers between devices: 0.01 us -> 1.39 us  [projected(): other = lax.ppermute(own, 'gx', partner)]
    ppermute x1, starting transfers between devices: 3.18 us -> 1.8 us  [projected(): xhalo = lax.ppermute(slab, BOTH, x_pairs)]
    all_to_all x1, starting transfers between devices: 12.6 us -> 11.3 us  [exchanged(): return lax.all_to_all(x, axis, 0, 0, tiled=True)]
    pallas_call x5 -> x6, Pallas kernels: 9.9 us -> 10.5 us  [call(): pl.pallas_call(kernel, out_shape=out_shape, in_specs=in_specs, out_specs=...]
  transfers between devices with their start and end apart: 6 -> 6, of which waited for: 2 -> 3; matrix products, arithmetic and copies ran while one was open for 1% -> 1% of each run, Pallas kernels for 6% -> 7%
where the time goes in v13:
time: 78.1 us; the launch traced here: 77.7 us
  blocking collectives  30.2 us (39%)
  starting transfers between devices  25.8 us (33%)
  Pallas kernels  10.5 us (13%)
  waiting for transfers between devices  7.55 us (10%)
  matrix products  2.18 us (3%)
    all_to_all x1, blocking collectives, exchanged(): return lax.all_to_all(x, axis, 0, 0, tiled=True)  30.2 us
    all_to_all x1, starting transfers between devices, exchanged(): return lax.all_to_all(x, axis, 0, 0, tiled=True)  11.3 us
    pallas_call x6, Pallas kernels, call(): pl.pallas_call(kernel, out_shape=out_shape, in_specs=in_specs, out_specs=...  10.5 us
    ppermute x1, starting transfers between devices, projected(): other = lax.ppermute(own, 'gx', partner)  8.75 us
    all_to_all x1, waiting for transfers between devices, exchanged(): return lax.all_to_all(x, axis, 0, 0, tiled=True)  6.07 us
    dot_general x1, matrix products, projected(): jnp.dot(bands.reshape(cells, nb), jnp.concatenate((left, right), axis=1),...  2.18 us
    ppermute x1, starting transfers between devices, projected(): coef_other = lax.ppermute(coef, 'gx', partner)  1.91 us
    ppermute x1, starting transfers between devices, projected(): xhalo = lax.ppermute(slab, BOTH, x_pairs)  1.8 us
  transfers between devices with their start and end apart: 6, of which 3 were waited for; matrix products, arithmetic and copies ran while one was open for 1% of the time, Pallas kernels for 7%

profile of v13, /device:TPU:1, one launch (start us, length us, event | category | flops | bytes accessed | tf_op | source)
XLA Modules:
  0.0 77.7 jit_solution(6139319449525113181)
XLA Ops:
  0.6 0.1 pad_add_fusion.place_ref
  0.7 2.2 %shard_map.58 = (bf16[9,5,40,512]{3,2,1,0:T(8,128)(2,1)S(1)}, bf16[8,40,512]{2,1,0:T(8,128)(2,1)S(1)}, bf16[5,40,512]{2,1,0:T(8,128)(2,1)S(1)}) custom-call(s32[2]{0:T(128)S(1)} %pad_add_fusion.place_ref, bf16[8,5,40,512]{3,2,1,0:T(8,128)(2,1)} %bands_ref.1, f32[5,8,40]{2,1,0:T(8,128)} %bitcast.15), custom_call_target="tpu_custom_call" | custom-call | bytes 1644808 | tf_op jit(solution)/shard_map/pallas_call | solution.py:29
  3.0 8.7 %collective-permute-start = (bf16[9,5,40,512]{3,2,1,0:T(8,128)(2,1)S(1)}, bf16[9,5,40,512]{3,2,1,0:T(8,128)(2,1)S(1)}, u32[]{:S(2)}, u32[]{:S(2)}) collective-permute-start(bf16[9,5,40,512]{3,2,1,0:T(8,128)(2,1)S(1)} %get-tuple-element.8.held_ref.own_ref), channel_id=1, source_target_pairs={{0,64},{64,0},{128,192},{192,128},{256,320},{320,256},{384,448},{4... | collective-permute-start | bytes 5529608 | tf_op jit(solution)/shard_map/ppermute | solution.py:254
  11.7 1.3 %collective-permute-start.1 = (bf16[8,40,512]{2,1,0:T(8,128)(2,1)S(1)}, bf16[8,40,512]{2,1,0:T(8,128)(2,1)S(1)}, u32[]{:S(2)}, u32[]{:S(2)}) collective-permute-start(bf16[8,40,512]{2,1,0:T(8,128)(2,1)S(1)} %get-tuple-element.9), channel_id=1, source_target_pairs={{64,65},{65,66},{66,67},{67,68},{68,69},{69,70},{70,71},{71,72},{7... | collective-permute-start | bytes 983048 | tf_op jit(solution)/shard_map/ppermute | solution.py:253
  13.0 0.7 collective-permute-start.2
  13.7 1.4 %collective-permute-done.held_ref.other_ref = bf16[9,5,40,512]{3,2,1,0:T(8,128)(2,1)S(1)} collective-permute-done((bf16[9,5,40,512]{3,2,1,0:T(8,128)(2,1)S(1)}, bf16[9,5,40,512]{3,2,1,0:T(8,128)(2,1)S(1)}, u32[]{:S(2)}, u32[]{:S(2)}) %collective-permute-start) | collective-permute-done | bytes 1843232 | tf_op jit(solution)/shard_map/ppermute | solution.py:254
  15.1 0.6 shard_map.61
  15.7 1.8 %collective-permute-start.3 = (bf16[5,40,512]{2,1,0:T(8,128)(2,1)S(1)}, bf16[5,40,512]{2,1,0:T(8,128)(2,1)S(1)}, u32[]{:S(2)}, u32[]{:S(2)}) collective-permute-start(bf16[5,40,512]{2,1,0:T(8,128)(2,1)S(1)} %shard_map.61), channel_id=1, source_target_pairs={{64,192},{193,65},{66,194},{195,67},{68,196},{197,69},{70,198},{19... | collective-permute-start | bytes 614408 | tf_op jit(solution)/shard_map/ppermute | solution.py:256
  17.5 2.5 %shard_map.59.refs_0_ = f32[512,512]{1,0:T(8,128)S(1)} custom-call(s32[2]{0:T(128)S(1)} %pad_add_fusion.place_ref, bf16[9,5,40,512]{3,2,1,0:T(8,128)(2,1)S(1)} %get-tuple-element.8.held_ref.own_ref), custom_call_target="tpu_custom_call" | custom-call | flops 838860800 | bytes 1843208 | tf_op jit(solution)/shard_map/pallas_call | solution.py:29
  20.0 0.0 copy-start
  20.0 2.6 %shard_map.60.gram_ref = f32[512,512]{1,0:T(8,128)S(1)} custom-call(s32[2]{0:T(128)S(1)} %pad_add_fusion.place_ref, bf16[9,5,40,512]{3,2,1,0:T(8,128)(2,1)S(1)} %collective-permute-done.held_ref.other_ref, f32[512,512]{1,0:T(8,128)S(1)} %shard_map.59.refs_0_), custom_call_target="tpu_custom_call" | custom-call | flops 838860800 | bytes 2891784 | tf_op jit(solution)/shard_map/pallas_call | solution.py:29
  22.6 0.0 collective-permute-done.1.yown_ref
  22.6 0.0 collective-permute-done.2.yother_ref
  22.6 0.1 collective-permute-done.3.xhalo_ref
  22.7 1.8 %shard_map.62 = bf16[64,8,768]{2,1,0:T(8,128)(2,1)S(1)} custom-call(s32[2]{0:T(128)S(1)} %pad_add_fusion.place_ref, f32[512,512]{1,0:T(8,128)S(1)} %shard_map.60.gram_ref, bf16[9,5,40,512]{3,2,1,0:T(8,128)(2,1)S(1)} %get-tuple-element.8.held_ref.own_ref, bf16[9,5,40,512]{3,2,1,0:T(8,128)(2,1)S(1)} %collective-permute-done.held_ref.other_ref, ...), custom_call_target="tpu_custom_call" | custom-call | flops 440401920 | bytes 5603336 | tf_op jit(solution)/shard_map/pallas_call | solution.py:29
  24.5 0.0 copy-start.1
  24.5 30.2 %all_to_all.10.in_ref = bf16[64,8,768]{2,1,0:T(8,128)(2,1)S(1)} all-to-all(bf16[64,8,768]{2,1,0:T(8,128)(2,1)S(1)} %shard_map.62), channel_id=1, replica_groups=mesh['gx'=8,'gyz'=64] {'gyz'}, dimensions={0} | all-to-all | bytes 1572864 | tf_op jit(solution)/shard_map/all_to_all | solution.py:236
  54.8 0.8 shard_map.63
  55.5 11.3 %all-to-all-start.1 = ((f32[8,8,512]{2,1,0:T(8,128)}), f32[8,8,512]{2,1,0:T(8,128)S(1)}, u32[]{:S(2)}, u32[]{:S(2)}) async-start(f32[8,8,512]{2,1,0:T(8,128)} %get-tuple-element.11), calls=%async_computation.1 | async-start | bytes 262144 | tf_op jit(solution)/shard_map/all_to_all | solution.py:236
  66.9 1.9 %collective-permute-start.4 = (bf16[512,256]{1,0:T(8,128)(2,1)S(1)}, bf16[512,256]{1,0:T(8,128)(2,1)S(1)}, u32[]{:S(2)}, u32[]{:S(2)}) collective-permute-start(bf16[512,256]{1,0:T(8,128)(2,1)S(1)} %get-tuple-element.12), channel_id=1, source_target_pairs={{0,64},{64,0},{128,192},{192,128},{256,320},{320,256},{384,448},{4... | collective-permute-start | bytes 786440 | tf_op jit(solution)/shard_map/ppermute | solution.py:262
  68.8 6.1 %all-to-all-done.1 = f32[8,8,512]{2,1,0:T(8,128)S(1)} async-done(((f32[8,8,512]{2,1,0:T(8,128)}), f32[8,8,512]{2,1,0:T(8,128)S(1)}, u32[]{:S(2)}, u32[]{:S(2)}) %all-to-all-start.1) | async-done | bytes 131104 | tf_op jit(solution)/shard_map/all_to_all | solution.py:236
  74.9 0.6 slice_bitcast_fusion
  75.5 0.0 collective-permute-done.4
  75.5 2.2 %convolution_convert_fusion = bf16[512,1600]{0,1:T(8,128)(2,1)} fusion(bf16[1600,512]{1,0:T(8,128)(2,1)S(1)} %bitcast.13, bf16[512,256]{1,0:T(8,128)(2,1)S(1)} %get-tuple-element.14, bf16[512,256]{1,0:T(8,128)(2,1)S(1)} %get-tuple-element.13), kind=kOutput, calls=%fused_computation | convolution fusion | flops 840728576 | bytes 3801088 | tf_op jit(solution)/shard_map/dot_general | solution.py:268
  (4 shorter events, 0.1 us)
Async XLA Ops:
  3.0 12.2 %collective-permute-start = (bf16[9,5,40,512]{3,2,1,0:T(8,128)(2,1)S(1)}, bf16[9,5,40,512]{3,2,1,0:T(8,128)(2,1)S(1)}, u32[]{:S(2)}, u32[]{:S(2)}) collective-permute-start(bf16[9,5,40,512]{3,2,1,0:T(8,128)(2,1)S(1)} %get-tuple-element.8.held_ref.own_ref), channel_id=1, source_target_pairs={{0,64},{64,0},{128,192},{192,128},{256,320},{320,256},{384,448},{4... | collective-permute-start | bytes 5529608 | tf_op jit(solution)/shard_map/ppermute | solution.py:254
  11.7 10.9 %collective-permute-start.1 = (bf16[8,40,512]{2,1,0:T(8,128)(2,1)S(1)}, bf16[8,40,512]{2,1,0:T(8,128)(2,1)S(1)}, u32[]{:S(2)}, u32[]{:S(2)}) collective-permute-start(bf16[8,40,512]{2,1,0:T(8,128)(2,1)S(1)} %get-tuple-element.9), channel_id=1, source_target_pairs={{64,65},{65,66},{66,67},{67,68},{68,69},{69,70},{70,71},{71,72},{7... | collective-permute-start | bytes 983048 | tf_op jit(solution)/shard_map/ppermute | solution.py:253
  13.0 9.6 %collective-permute-start.2 = (bf16[8,40,512]{2,1,0:T(8,128)(2,1)S(1)}, bf16[8,40,512]{2,1,0:T(8,128)(2,1)S(1)}, u32[]{:S(2)}, u32[]{:S(2)}) collective-permute-start(bf16[8,40,512]{2,1,0:T(8,128)(2,1)S(1)} %get-tuple-element.9), channel_id=1, source_target_pairs={{0,65},{1,66},{2,67},{3,68},{4,69},{5,70},{6,71},{7,72},{8,73},{9,... | collective-permute-start | bytes 983048 | tf_op jit(solution)/shard_map/ppermute | solution.py:252
  15.7 7.0 %collective-permute-start.3 = (bf16[5,40,512]{2,1,0:T(8,128)(2,1)S(1)}, bf16[5,40,512]{2,1,0:T(8,128)(2,1)S(1)}, u32[]{:S(2)}, u32[]{:S(2)}) collective-permute-start(bf16[5,40,512]{2,1,0:T(8,128)(2,1)S(1)} %shard_map.61), channel_id=1, source_target_pairs={{64,192},{193,65},{66,194},{195,67},{68,196},{197,69},{70,198},{19... | collective-permute-start | bytes 614408 | tf_op jit(solution)/shard_map/ppermute | solution.py:256
  20.0 2.7 %copy-start = (bf16[8,512]{1,0:T(8,128)(2,1)S(1)}, bf16[8,512]{1,0:T(8,128)(2,1)}, u32[]{:S(2)}) copy-start(bf16[8,512]{1,0:T(8,128)(2,1)} %coef_ref.1) | copy-start | bytes 24580
  24.5 51.0 %copy-start.1 = (bf16[8,5,40,512]{3,2,1,0:T(8,128)(2,1)S(1)}, bf16[8,5,40,512]{3,2,1,0:T(8,128)(2,1)}, u32[]{:S(2)}) copy-start(bf16[8,5,40,512]{3,2,1,0:T(8,128)(2,1)} %bands_ref.1) | copy-start | bytes 4915204
  55.5 19.3 %all-to-all-start.1 = ((f32[8,8,512]{2,1,0:T(8,128)}), f32[8,8,512]{2,1,0:T(8,128)S(1)}, u32[]{:S(2)}, u32[]{:S(2)}) async-start(f32[8,8,512]{2,1,0:T(8,128)} %get-tuple-element.11), calls=%async_computation.1 | async-start | bytes 262144 | tf_op jit(solution)/shard_map/all_to_all | solution.py:236
  66.9 8.6 %collective-permute-start.4 = (bf16[512,256]{1,0:T(8,128)(2,1)S(1)}, bf16[512,256]{1,0:T(8,128)(2,1)S(1)}, u32[]{:S(2)}, u32[]{:S(2)}) collective-permute-start(bf16[512,256]{1,0:T(8,128)(2,1)S(1)} %get-tuple-element.12), channel_id=1, source_target_pairs={{0,64},{64,0},{128,192},{192,128},{256,320},{320,256},{384,448},{4... | collective-permute-start | bytes 786440 | tf_op jit(solution)/shard_map/ppermute | solution.py:262
